TPU v7x, 256 devices: a whole 4x4x8 slice. The times are simulated.
256 devices in a mesh: gx: 8 (over z_lo, core), gy: 32 (over z_hi, y, x).
Axes of the slice: x: 4, y: 4, z: 8 (z_hi: 2, z_lo: 4; z = z_hi * 4 + z_lo), core: 2. Of those that a mesh axis runs over, the one named last changes fastest.
Arguments:
- density: float32 [128, 512, 256], P('gx', 'gy'), may hold values from 0.5 to 2
- momentum: float32 [3, 128, 512, 256], P(None, 'gx', 'gy'), may hold values from -3 to 3
- energy: float32 [128, 512, 256], P('gx', 'gy'), may hold values from 1 to 3
- parcel_mass: float32 [2097152], P(('gx', 'gy')), may hold values from 0.2 to 2
- droplet_velocity: float32 [3, 2097152], P(None, ('gx', 'gy')), may hold values from -4 to 4
- parcel_temp: float32 [2097152], P(('gx', 'gy')), may hold values from 0.1 to 4
- parcel_cell: int32 [3, 2097152], P(None, ('gx', 'gy')), may hold values from 0 to 511, as said below
- parcel_count: int32 [256], P(('gx', 'gy')), may hold values from 2048 to 8192, as said below
Outputs:
- updated_fluid_density: float32 [128, 512, 256], P('gx', 'gy')
- updated_fluid_impulse: float32 [3, 128, 512, 256], P(None, 'gx', 'gy')
- energy_out: float32 [128, 512, 256], P('gx', 'gy')
- moved_state: float32 [5, 2621440], P(None, ('gx', 'gy'))
- moved_cell: int32 [3, 2621440], P(None, ('gx', 'gy'))
- time_step: float32 [], replicated
Inputs may be any that keep to these rules, and one draw needn't show every extreme that they name: `parcel_cell`: each row of device d lies in d's block of 16 x 16 x 256 cells or in the layer of cells just beyond one of its four side faces inside the grid, never beyond an edge. Among the live rows of one device at most 512 lie beyond any one face; on every device some face along each of the two axes has exactly 512. `parcel_count`: some devices are full.
All inputs are finite; a program needn't handle non-finite values.
Results may differ from a plain program's by a relative error of at most 0.0003.
Values sent between devices are 32-bit elements; how exact they have to be, the bound alone decides.
No kernel may reach another device: no remote copies, remote signals or barrier semaphores. Data moves between devices by JAX's collectives and lax.ppermute only.
A program may use at most 192 MiB of HBM per device.

v0:
```python
import jax
import jax.numpy as jnp
from jax import lax
from jax.sharding import Mesh
from jax.sharding import PartitionSpec as P

GX = ("gx_0", "gx_1")
GY = ("gy_0", "gy_1", "gy_2")
GX_GY = ("gx_0", "gx_1", "gy_0", "gy_1", "gy_2")


ADIABATIC_INDEX = 1.4
KICK = 0.25
COURANT = 0.4
SHRINK = 0.5


def with_halo(cells, sides, width):
    for axis, dim in sides:
        count = lax.axis_size(axis)
        ends = count - 1
        head = lax.slice_in_dim(cells, 0, width, axis=dim)
        tail = lax.slice_in_dim(cells, cells.shape[dim] - width, cells.shape[dim], axis=dim)
        cells = jnp.concatenate(
            [
                lax.ppermute(tail, axis, [(i, (i + 1) % count) for i in range(ends)]),
                cells,
                lax.ppermute(head, axis, [((i + 1) % count, i) for i in range(ends)]),
            ],
            axis=dim,
        )
    return cells


def padded_2(shard, sides, width):
    edges = {}
    for axis, dim in sides:
        size, length = (lax.axis_size(axis), shard.shape[dim])
        up = [(i, (i + 1) % size) for i in range(size - 1)]
        last = lax.slice_in_dim(shard, length - width, length, axis=dim)
        leading = lax.slice_in_dim(shard, 0, width, axis=dim)
        edges[dim] = (
            lax.ppermute(last, axis, up),
            lax.ppermute(leading, axis, [(b, a) for a, b in up]),
        )
    done = []
    for _, dim in sides:
        low, high = edges[dim]
        around = [(width, width) if d in done else (0, 0) for d in range(shard.ndim)]
        shard = jnp.concatenate([jnp.pad(low, around), shard, jnp.pad(high, around)], axis=dim)
        done.append(dim)
    return shard


def over_axes(shard, axes):
    for axis in axes:
        shard = lax.pmax(shard, axis)
    return shard


def gather_coupling_feedback(boiled_off_amount, ambient_stream_speed, ambient_thermal_reading):
    specific_movement_budget = 0.5 * jnp.sum(ambient_stream_speed * ambient_stream_speed, axis=0)
    return jnp.concatenate(
        [
            boiled_off_amount[None],
            boiled_off_amount[None] * ambient_stream_speed,
            (boiled_off_amount * (ambient_thermal_reading + specific_movement_budget))[None],
        ],
        axis=0,
    )


def on_device(
    density, momentum, energy, parcel_mass, droplet_velocity, parcel_temp, parcel_cell, parcel_count
):
    cells_x, cells_y, depth_cells = density.shape
    row_total = parcel_mass.shape[0]
    capacity = row_total // 16
    anchor_x = lax.axis_index(GX) * cells_x
    anchor_y = lax.axis_index(GY) * cells_y
    live = jnp.arange(row_total, dtype=jnp.int32) < parcel_count[0]
    boiled_off_amount = jnp.where(
        live, parcel_mass * jax.nn.sigmoid(2.0 * (parcel_temp - 2.0)), 0.0
    )
    sources = gather_coupling_feedback(boiled_off_amount, droplet_velocity, parcel_temp)
    local_x = parcel_cell[0] - anchor_x
    local_y = parcel_cell[1] - anchor_y
    heading = jnp.where(
        local_x < 0,
        0,
        jnp.where(
            local_x >= cells_x, 1, jnp.where(local_y < 0, 2, jnp.where(local_y >= cells_y, 3, 4))
        ),
    )
    heading = jnp.where(live, heading, 5).astype(jnp.int32)
    onehot = (heading[:, None] == jnp.arange(4, dtype=jnp.int32)[None]).astype(jnp.int32)
    earlier = jnp.cumsum(onehot, axis=0) - onehot
    rank = jnp.sum(earlier * onehot, axis=1)
    carried_records = jnp.concatenate(
        [
            (parcel_mass - SHRINK * boiled_off_amount)[None],
            droplet_velocity,
            parcel_temp[None],
            parcel_cell.astype(jnp.float32),
            boiled_off_amount[None],
        ],
        axis=0,
    )
    target = jnp.where(heading < 4, heading * capacity + rank, 4 * capacity)
    buckets = (
        jnp.zeros((9, 4 * capacity), jnp.float32)
        .at[:, target]
        .set(carried_records, mode="drop")
        .reshape(9, 4, capacity)
    )
    staying = jnp.where((heading == 4)[None], carried_records[:8], 0.0)
    block_cells = cells_x * cells_y * depth_cells
    face_x = (cells_y + 2) * depth_cells
    face_y = cells_x * depth_cells
    total_cells = block_cells + 2 * face_x + 2 * face_y
    depth_of = parcel_cell[2]
    within_x = (local_x >= 0) & (local_x < cells_x)
    within_y = (local_y >= 0) & (local_y < cells_y)
    cell_slot = jnp.where(
        within_x & within_y,
        (local_x * cells_y + local_y) * depth_cells + depth_of,
        jnp.where(
            local_x < 0,
            block_cells + (local_y + 1) * depth_cells + depth_of,
            jnp.where(
                local_x >= cells_x,
                block_cells + face_x + (local_y + 1) * depth_cells + depth_of,
                jnp.where(
                    local_y < 0,
                    block_cells + 2 * face_x + local_x * depth_cells + depth_of,
                    block_cells + 2 * face_x + face_y + local_x * depth_cells + depth_of,
                ),
            ),
        ),
    )
    cell_slot = jnp.clip(cell_slot, 0, total_cells - 1)

    def deposit_one(values):
        return jax.ops.segment_sum(values, cell_slot, num_segments=total_cells)

    flat_sums = jax.vmap(deposit_one)(sources)
    core = flat_sums[:, :block_cells].reshape(5, cells_x, cells_y, depth_cells)
    lower_x = flat_sums[:, block_cells : block_cells + face_x]
    upper_x = flat_sums[:, block_cells + face_x : block_cells + 2 * face_x]
    lower_y = flat_sums[:, block_cells + 2 * face_x : block_cells + 2 * face_x + face_y].reshape(
        5, cells_x, depth_cells
    )
    upper_y = flat_sums[:, block_cells + 2 * face_x + face_y :].reshape(5, cells_x, depth_cells)
    eight = buckets[:8]
    size_x = 5 * face_x
    faces_x = jnp.stack([lower_x.reshape(-1), upper_x.reshape(-1)])
    faces_x = jnp.concatenate(
        [faces_x, jnp.stack([eight[:, 0].reshape(-1), eight[:, 1].reshape(-1)])], axis=1
    )
    got_x = with_halo(faces_x, ((GX, 0),), 1)
    from_lower = got_x[0, :size_x].reshape(5, cells_y + 2, depth_cells)
    from_upper = got_x[3, :size_x].reshape(5, cells_y + 2, depth_cells)
    core = core.at[:, 0].add(from_lower[:, 1 : cells_y + 1])
    core = core.at[:, cells_x - 1].add(from_upper[:, 1 : cells_y + 1])
    lower_y = lower_y.at[:, 0].add(from_lower[:, 0]).at[:, cells_x - 1].add(from_upper[:, 0])
    upper_y = (
        upper_y.at[:, 0]
        .add(from_lower[:, cells_y + 1])
        .at[:, cells_x - 1]
        .add(from_upper[:, cells_y + 1])
    )
    size_y = 5 * face_y
    faces_y = jnp.stack([lower_y.reshape(-1), upper_y.reshape(-1)])
    faces_y = jnp.concatenate(
        [faces_y, jnp.stack([eight[:, 2].reshape(-1), eight[:, 3].reshape(-1)])], axis=1
    )
    got_y = with_halo(faces_y, ((GY, 0),), 1)
    core = core.at[:, :, 0].add(got_y[0, :size_y].reshape(5, cells_x, depth_cells))
    core = core.at[:, :, cells_y - 1].add(got_y[3, :size_y].reshape(5, cells_x, depth_cells))
    arrived = jnp.concatenate(
        [
            got_x[0, size_x:].reshape(8, capacity),
            got_x[3, size_x:].reshape(8, capacity),
            got_y[0, size_y:].reshape(8, capacity),
            got_y[3, size_y:].reshape(8, capacity),
        ],
        axis=1,
    )
    updated_fluid_density = density + core[0]
    energy_out = energy + core[4]
    lifted = momentum + core[1:4]
    normal_stress_field = (ADIABATIC_INDEX - 1.0) * energy_out
    padded = padded_2(normal_stress_field, ((GX, 0), (GY, 1)), 1)
    grad_x = 0.5 * (padded[2:, 1:-1] - padded[:-2, 1:-1])
    grad_y = 0.5 * (padded[1:-1, 2:] - padded[1:-1, :-2])
    deep = jnp.pad(normal_stress_field, ((0, 0), (0, 0), (1, 1)))
    grad_z = 0.5 * (deep[:, :, 2:] - deep[:, :, :-2])
    updated_fluid_impulse = lifted - KICK * jnp.stack([grad_x, grad_y, grad_z])
    ambient_stream_speed = updated_fluid_impulse / updated_fluid_density[None]
    acoustic_signal = jnp.max(jnp.abs(ambient_stream_speed), axis=0) + jnp.sqrt(
        ADIABATIC_INDEX * normal_stress_field / updated_fluid_density
    )
    fastest = over_axes(jnp.max(acoustic_signal), GX_GY)
    time_step = COURANT / fastest
    table = jnp.concatenate([staying, arrived], axis=1)
    moved_state = table[:5]
    moved_cell = table[5:].astype(jnp.int32)
    return (
        updated_fluid_density,
        updated_fluid_impulse,
        energy_out,
        moved_state,
        moved_cell,
        time_step,
    )


def solution(mesh):
    split = Mesh(mesh.devices.reshape(4, 2, 2, 4, 4), ("gx_0", "gx_1", "gy_0", "gy_1", "gy_2"))
    return jax.shard_map(
        on_device,
        mesh=split,
        in_specs=(
            P(GX, GY, None),
            P(None, GX, GY, None),
            P(GX, GY, None),
            P(GX_GY),
            P(None, GX_GY),
            P(GX_GY),
            P(None, GX_GY),
            P(GX_GY),
        ),
        out_specs=(
            P(GX, GY, None),
            P(None, GX, GY, None),
            P(GX, GY, None),
            P(None, GX_GY),
            P(None, GX_GY),
            P(),
        ),
        check_vma=False,
    )
```

profile of v0, /device:TPU:1, one launch (start us, length us, event | category | flops | bytes accessed | tf_op | source)
XLA Modules:
  0.0 276.1 jit_solution(5672505770449375735)
XLA Ops:
  9.6 2.6 copy.27
  12.5 21.1 %scatter_custom_fusion.1 = f32[9,2048]{0,1:T(8,128)S(1)} fusion(s32[8192]{0:T(1024)S(1)} %bitcast.131, f32[8192,9]{1,0:T(8,128)} %copy.27, f32[]{:T(128)} %constant.250.clone.1), kind=kCustom, calls=%fused_computation.8 | custom fusion | bytes 74240 | tf_op jit(solution)/shard_map/scatter | solution.py:113
  34.9 2.7 copy.23
  37.5 61.0 %scatter_custom_fusion = f32[5,82944]{0,1:T(8,128)} fusion(s32[8192]{0:T(1024)S(1)} %bitcast.132, f32[8192,5]{1,0:T(8,128)} %copy.23, f32[]{:T(128)} %constant.250.clone.1), kind=kCustom, calls=%fused_computation.2 | custom fusion | flops 40960 | bytes 1659392 | tf_op jit(solution)/shard_map/vmap()/scatter-add | solution.py:144
  98.5 4.1 %fusion.34 = (f32[5,4608]{0,1:T(8,128)}, f32[5,4608]{0,1:T(8,128)S(1)}) fusion(f32[5,82944]{0,1:T(8,128)} %scatter_custom_fusion), kind=kLoop, calls=%fused_computation.103 | loop fusion | bytes 368640 | tf_op jit(solution)/shard_map/slice | solution.py:148
  102.6 2.4 copy.25
  107.0 4.9 %collective-permute-start = (f32[1,27136]{1,0:T(1,128)}, f32[1,27136]{1,0:T(1,128)}, u32[]{:S(2)}, u32[]{:S(2)}) collective-permute-start(f32[1,27136]{1,0:T(1,128)} %get-tuple-element.127), channel_id=1, source_target_pairs={{0,32},{32,64},{64,96},{96,128},{128,160},{160,192},{192,224},{1,3... | collective-permute-start | bytes 325640 | tf_op jit(solution)/shard_map/ppermute | solution.py:26
  114.9 4.4 %fusion.33 = (f32[5,4096]{0,1:T(8,128)}, f32[5,4096]{0,1:T(8,128)}) fusion(f32[5,82944]{0,1:T(8,128)} %scatter_custom_fusion), kind=kLoop, calls=%fused_computation.102 | loop fusion | bytes 327680 | tf_op jit(solution)/shard_map/slice | solution.py:150
  119.3 11.9 %slice.406 = f32[5,65536]{0,1:T(8,128)S(1)} slice(f32[5,82944]{0,1:T(8,128)} %scatter_custom_fusion), slice={[0:5], [0:65536]} | slice | bytes 2621440 | tf_op jit(solution)/shard_map/slice | solution.py:147
  131.2 11.1 %copy-done = f32[5,65536]{0,1:T(8,128)} copy-done((f32[5,65536]{0,1:T(8,128)}, f32[5,65536]{0,1:T(8,128)S(1)}, u32[]{:S(2)}) %copy-start) | copy-done | bytes 1310744
  142.4 19.5 %copy.30 = f32[5,16,16,256]{3,2,1,0:T(8,128)S(1)} copy(f32[5,16,16,256]{0,3,2,1:T(8,128)} %bitcast.101) | data formatting | bytes 2621440 | tf_op jit(solution)/shard_map/reshape | solution.py:147
  162.0 2.8 %copy.33 = f32[5,16,256]{2,1,0:T(8,128)} copy(f32[5,16,256]{0,2,1:T(8,128)} %bitcast.103) | data formatting | bytes 163840 | tf_op jit(solution)/shard_map/reshape | solution.py:150
  164.8 2.2 copy.35
  178.8 2.9 %collective-permute-start.2 = (f32[1,24576]{1,0:T(1,128)S(1)}, f32[1,24576]{1,0:T(1,128)S(1)}, u32[]{:S(2)}, u32[]{:S(2)}) collective-permute-start(f32[1,24576]{1,0:T(1,128)S(1)} %get-tuple-element.129), channel_id=1, source_target_pairs={{0,1},{1,2},{2,3},{3,4},{4,5},{5,6},{6,7},{7,8},{8,9},{9,10},{10,1... | collective-permute-start | bytes 294920 | tf_op jit(solution)/shard_map/ppermute | solution.py:26
  185.0 3.2 %scatter-add.54 = f32[5,16,16,256]{3,2,1,0:T(8,128)S(1)} dynamic-update-slice(f32[5,16,16,256]{3,2,1,0:T(8,128)S(1)} %fusion.24, f32[5,16,1,256]{3,2,1,0:T(1,128)S(1)} %slice_add_fusion.2, s32[]{:T(128)} %constant.251.clone.1, s32[]{:T(128)} %constant.251.clone.1, s32[]{:T(128)} %constant.251.clone.1, s32[]{:T(128)} %constant.251.clone.1) | dynamic-update-slice | bytes 163844 | tf_op jit(solution)/shard_map/scatter-add | solution.py:178
  188.3 3.2 %scatter-add.55 = f32[5,16,16,256]{3,2,1,0:T(8,128)S(1)} dynamic-update-slice(f32[5,16,16,256]{3,2,1,0:T(8,128)S(1)} %scatter-add.54, f32[5,16,1,256]{3,2,1,0:T(1,128)S(1)} %slice_add_fusion.1, s32[]{:T(128)} %constant.251.clone.1, s32[]{:T(128)} %constant.251.clone.1, s32[]{:T(128)} %constant.277.clone.1, s32[]{:T(128)} %constant.251.clone.1) | dynamic-update-slice | bytes 163844 | tf_op jit(solution)/shard_map/scatter-add | solution.py:179
  193.7 5.1 %collective-permute-start.5 = (f32[1,16,256]{2,1,0:T(8,128)S(1)}, f32[1,16,256]{2,1,0:T(8,128)S(1)}, u32[]{:S(2)}, u32[]{:S(2)}) collective-permute-start(f32[1,16,256]{2,1,0:T(8,128)S(1)} %get-tuple-element.124), channel_id=1, source_target_pairs={{0,32},{32,64},{64,96},{96,128},{128,160},{160,192},{192,224},{1,3... | collective-permute-start | bytes 49160 | tf_op jit(solution)/shard_map/ppermute | solution.py:43
  200.1 4.0 %collective-permute-start.7 = (f32[16,1,256]{2,1,0:T(1,128)S(1)}, f32[16,1,256]{2,1,0:T(1,128)S(1)}, u32[]{:S(2)}, u32[]{:S(2)}) collective-permute-start(f32[16,1,256]{2,1,0:T(1,128)S(1)} %get-tuple-element.123), channel_id=1, source_target_pairs={{0,1},{1,2},{2,3},{3,4},{4,5},{5,6},{6,7},{7,8},{8,9},{9,10},{10,1... | collective-permute-start | bytes 49160 | tf_op jit(solution)/shard_map/ppermute | solution.py:43
  206.4 2.4 abs_reduce_fusion
  209.5 9.3 %pmax.35 = f32[]{:T(128)} all-reduce(f32[]{:T(128)} %add_reduce_fusion), channel_id=1, replica_groups=mesh['gx_0'=4,'gx_1'=2,'gy_0'=2,'gy_1'=4,'gy_2'=4] {'gx_0'}, use_global_device_ids=true, to_apply=%region_8.9 | all-reduce | flops 1 | bytes 8 | tf_op jit(solution)/shard_map/pmax | solution.py:57
  219.4 6.5 %pmax.36 = f32[]{:T(128)} all-reduce(f32[]{:T(128)} %pmax.35), channel_id=1, replica_groups=mesh['gx_0'=4,'gx_1'=2,'gy_0'=2,'gy_1'=4,'gy_2'=4] {'gx_1'}, use_global_device_ids=true, to_apply=%region_9.10 | all-reduce | flops 1 | bytes 8 | tf_op jit(solution)/shard_map/pmax | solution.py:57
  225.9 32.2 %pmax.37 = f32[]{:T(128)} all-reduce(f32[]{:T(128)} %pmax.36), channel_id=1, replica_groups=mesh['gx_0'=4,'gx_1'=2,'gy_0'=2,'gy_1'=4,'gy_2'=4] {'gy_0'}, use_global_device_ids=true, to_apply=%region_10.11 | all-reduce | flops 1 | bytes 8 | tf_op jit(solution)/shard_map/pmax | solution.py:57
  258.7 6.6 %pmax.38 = f32[]{:T(128)} all-reduce(f32[]{:T(128)} %pmax.37), channel_id=1, replica_groups=mesh['gx_0'=4,'gx_1'=2,'gy_0'=2,'gy_1'=4,'gy_2'=4] {'gy_1'}, use_global_device_ids=true, to_apply=%region_11.12 | all-reduce | flops 1 | bytes 8 | tf_op jit(solution)/shard_map/pmax | solution.py:57
  267.0 7.3 %pmax.39 = f32[]{:T(128)} all-reduce(f32[]{:T(128)} %pmax.38), channel_id=1, replica_groups=mesh['gx_0'=4,'gx_1'=2,'gy_0'=2,'gy_1'=4,'gy_2'=4] {'gy_2'}, use_global_device_ids=true, to_apply=%region_12.13 | all-reduce | flops 1 | bytes 8 | tf_op jit(solution)/shard_map/pmax | solution.py:57
  (96 shorter events, 39.1 us)
Async XLA Ops:
  12.3 22.5 %copy-start.4 = (f32[8192]{0:T(1024)S(1)}, f32[8192]{0:T(1024)}, u32[]{:S(2)}) copy-start(f32[8192]{0:T(1024)} %param.29) | copy-start | bytes 98308
  105.0 9.0 %copy-start.2 = (f32[3,8192]{1,0:T(4,128)S(1)}, f32[3,8192]{1,0:T(4,128)}, u32[]{:S(2)}) copy-start(f32[3,8192]{1,0:T(4,128)} %param.28) | copy-start | bytes 294916
  107.0 63.5 %collective-permute-start = (f32[1,27136]{1,0:T(1,128)}, f32[1,27136]{1,0:T(1,128)}, u32[]{:S(2)}, u32[]{:S(2)}) collective-permute-start(f32[1,27136]{1,0:T(1,128)} %get-tuple-element.127), channel_id=1, source_target_pairs={{0,32},{32,64},{64,96},{96,128},{128,160},{160,192},{192,224},{1,3... | collective-permute-start | bytes 325640 | tf_op jit(solution)/shard_map/ppermute | solution.py:26
  111.9 62.1 %collective-permute-start.1 = (f32[1,27136]{1,0:T(1,128)}, f32[1,27136]{1,0:T(1,128)}, u32[]{:S(2)}, u32[]{:S(2)}) collective-permute-start(f32[1,27136]{1,0:T(1,128)} %get-tuple-element.126), channel_id=1, source_target_pairs={{32,0},{64,32},{96,64},{128,96},{160,128},{192,160},{224,192},{33,... | collective-permute-start | bytes 325640 | tf_op jit(solution)/shard_map/ppermute | solution.py:28
  131.2 11.1 %copy-start = (f32[5,65536]{0,1:T(8,128)}, f32[5,65536]{0,1:T(8,128)S(1)}, u32[]{:S(2)}) copy-start(f32[5,65536]{0,1:T(8,128)S(1)} %slice.406) | copy-start | bytes 3932164
  170.5 21.1 %copy-start.5 = (f32[16,16,256]{2,1,0:T(8,128)S(1)}, f32[16,16,256]{2,1,0:T(8,128)}, u32[]{:S(2)}) copy-start(f32[16,16,256]{2,1,0:T(8,128)} %param.26) | copy-start | bytes 786436
  170.5 21.1 %copy-start.6 = (f32[16,16,256]{2,1,0:T(8,128)S(1)}, f32[16,16,256]{2,1,0:T(8,128)}, u32[]{:S(2)}) copy-start(f32[16,16,256]{2,1,0:T(8,128)} %param.24) | copy-start | bytes 786436
  178.8 6.0 %collective-permute-start.2 = (f32[1,24576]{1,0:T(1,128)S(1)}, f32[1,24576]{1,0:T(1,128)S(1)}, u32[]{:S(2)}, u32[]{:S(2)}) collective-permute-start(f32[1,24576]{1,0:T(1,128)S(1)} %get-tuple-element.129), channel_id=1, source_target_pairs={{0,1},{1,2},{2,3},{3,4},{4,5},{5,6},{6,7},{7,8},{8,9},{9,10},{10,1... | collective-permute-start | bytes 294920 | tf_op jit(solution)/shard_map/ppermute | solution.py:26
  182.7 5.5 %collective-permute-start.3 = (f32[1,24576]{1,0:T(1,128)S(1)}, f32[1,24576]{1,0:T(1,128)S(1)}, u32[]{:S(2)}, u32[]{:S(2)}) collective-permute-start(f32[1,24576]{1,0:T(1,128)S(1)} %get-tuple-element.128), channel_id=1, source_target_pairs={{1,0},{2,1},{3,2},{4,3},{5,4},{6,5},{7,6},{8,7},{9,8},{10,9},{11,1... | collective-permute-start | bytes 294920 | tf_op jit(solution)/shard_map/ppermute | solution.py:28
  191.7 17.1 %copy-start.1 = (f32[16,16,256]{2,1,0:T(8,128)}, f32[16,16,256]{2,1,0:T(8,128)S(1)}, u32[]{:S(2)}) copy-start(f32[16,16,256]{2,1,0:T(8,128)S(1)} %get-tuple-element.114) | copy-start | bytes 786436
  191.7 17.1 %copy-start.3 = (f32[16,16,256]{2,1,0:T(8,128)}, f32[16,16,256]{2,1,0:T(8,128)S(1)}, u32[]{:S(2)}) copy-start(f32[16,16,256]{2,1,0:T(8,128)S(1)} %get-tuple-element.107) | copy-start | bytes 786436
  191.8 14.4 %collective-permute-start.4 = (f32[1,16,256]{2,1,0:T(8,128)S(1)}, f32[1,16,256]{2,1,0:T(8,128)S(1)}, u32[]{:S(2)}, u32[]{:S(2)}) collective-permute-start(f32[1,16,256]{2,1,0:T(8,128)S(1)} %get-tuple-element.125), channel_id=1, source_target_pairs={{32,0},{64,32},{96,64},{128,96},{160,128},{192,160},{224,192},{33,... | collective-permute-start | bytes 49160 | tf_op jit(solution)/shard_map/ppermute | solution.py:44
  193.7 12.5 %collective-permute-start.5 = (f32[1,16,256]{2,1,0:T(8,128)S(1)}, f32[1,16,256]{2,1,0:T(8,128)S(1)}, u32[]{:S(2)}, u32[]{:S(2)}) collective-permute-start(f32[1,16,256]{2,1,0:T(8,128)S(1)} %get-tuple-element.124), channel_id=1, source_target_pairs={{0,32},{32,64},{64,96},{96,128},{128,160},{160,192},{192,224},{1,3... | collective-permute-start | bytes 49160 | tf_op jit(solution)/shard_map/ppermute | solution.py:43
  198.8 7.4 %collective-permute-start.6 = (f32[16,1,256]{2,1,0:T(1,128)S(1)}, f32[16,1,256]{2,1,0:T(1,128)S(1)}, u32[]{:S(2)}, u32[]{:S(2)}) collective-permute-start(f32[16,1,256]{2,1,0:T(1,128)S(1)} %get-tuple-element.122), channel_id=1, source_target_pairs={{1,0},{2,1},{3,2},{4,3},{5,4},{6,5},{7,6},{8,7},{9,8},{10,9},{11,1... | collective-permute-start | bytes 49160 | tf_op jit(solution)/shard_map/ppermute | solution.py:44
  200.1 6.1 %collective-permute-start.7 = (f32[16,1,256]{2,1,0:T(1,128)S(1)}, f32[16,1,256]{2,1,0:T(1,128)S(1)}, u32[]{:S(2)}, u32[]{:S(2)}) collective-permute-start(f32[16,1,256]{2,1,0:T(1,128)S(1)} %get-tuple-element.123), channel_id=1, source_target_pairs={{0,1},{1,2},{2,3},{3,4},{4,5},{5,6},{6,7},{7,8},{8,9},{9,10},{10,1... | collective-permute-start | bytes 49160 | tf_op jit(solution)/shard_map/ppermute | solution.py:43
where the time goes:
time: 281 us; the launch traced here: 276 us
  local copies, waits for them, and re-layouts  110 us (39%)
  other arithmetic  77.4 us (28%)
  blocking collectives  61.9 us (22%)
  starting transfers between devices  23.5 us (8%)
  between operations  3.61 us (1%)
    pmax x5, blocking collectives, over_axes(): shard = lax.pmax(shard, axis)  61.9 us
    scatter-add x1, other arithmetic, deposit_one(): return jax.ops.segment_sum(values, cell_slot, num_segments=total_cells)  61 us
    scatter x1, local copies, waits for them, and re-layouts, on_device(): buckets = jnp.zeros((9, 4 * capacity), jnp.float32).at[:, target].set(car...  21.1 us
    reshape x1, local copies, waits for them, and re-layouts, on_device(): core = flat_sums[:, :block_cells].reshape(5, cells_x, cells_y, depth_cells)  19.5 us
    unnamed x28, local copies, waits for them, and re-layouts  16.8 us
    slice x1, local copies, waits for them, and re-layouts, on_device(): core = flat_sums[:, :block_cells].reshape(5, cells_x, cells_y, depth_cells)  11.9 us
    ppermute x2, starting transfers between devices, padded_2(): lax.ppermute(last, axis, up)  9.06 us
    ppermute x2, starting transfers between devices, with_halo(): lax.ppermute(tail, axis, [(i, (i + 1) % count) for i in range(ends)])  7.86 us
  transfers between devices with their start and end apart: 8, of which 0 were waited for; matrix products, arithmetic and copies ran while one was open for 20% of the time, Pallas kernels for 0%

commit v1 on v0

v1 whole, which is shorter than its diff:
```python
import functools

import jax
import jax.numpy as jnp
from jax import lax
from jax.experimental import pallas as pl
from jax.experimental.pallas import tpu as pltpu
from jax.sharding import PartitionSpec as P

ADIABATIC_INDEX = 1.4
KICK = 0.25
COURANT = 0.4
SHRINK = 0.5

F32 = jnp.float32
BF16 = jnp.bfloat16
I32 = jnp.int32
LANES = 128
VMEM = pltpu.VMEM
TRANSPOSED = (((1,), (1,)), ((), ()))


def iota(shape, dim, dtype=I32):
    return lax.broadcasted_iota(dtype, shape, dim)


def sigmoid_of(temp):
    return 1.0 / (1.0 + jnp.exp(-2.0 * (temp - 2.0)))


def prep_kernel(
    cells_x, cells_y, count, mass, temp, vel, cell,
    out0, out1, out2, out3, stay,
    pay, cx, cy, pos, compact, table_v, table_s, tiles, sem,
):
    chunks = mass.shape[0]
    anchor_x = lax.axis_index("gx") * cells_x
    anchor_y = lax.axis_index("gy") * cells_y
    for b in range(chunks):
        lanes = slice(b * LANES, (b + 1) * LANES)
        cx[b : b + 1, :] = cell[0:1, lanes]
        cy[b : b + 1, :] = cell[1:2, lanes]
    shape = (chunks, LANES)
    live = iota(shape, 0) * LANES + iota(shape, 1) < count[0]
    kept = mass[...] * (1.0 - SHRINK * jnp.where(live, sigmoid_of(temp[...]), 0.0))
    local_x = cx[...] - anchor_x
    local_y = cy[...] - anchor_y
    heading = jnp.where(
        local_x < 0,
        0,
        jnp.where(
            local_x >= cells_x, 1, jnp.where(local_y < 0, 2, jnp.where(local_y >= cells_y, 3, 4))
        ),
    )
    heading = jnp.where(live, heading, 5)
    masks = [jnp.where(heading == h, 1.0, 0.0) for h in range(4)]
    lane_r = iota((LANES, 2 * LANES), 0)
    lane_c = iota((LANES, 2 * LANES), 1)
    scan = jnp.where((lane_r < lane_c) | (lane_c >= LANES), 1.0, 0.0).astype(BF16)
    both = jnp.dot(
        jnp.concatenate(masks, axis=0).astype(BF16), scan, preferred_element_type=F32
    )
    inner = [both[h * chunks : (h + 1) * chunks, :LANES] for h in range(4)]
    total = [both[h * chunks : (h + 1) * chunks, LANES:] for h in range(4)]
    below = jnp.where(iota((chunks, chunks), 1) < iota((chunks, chunks), 0), 1.0, 0.0).astype(BF16)
    base = jnp.dot(
        below, jnp.concatenate(total, axis=1).astype(BF16), preferred_element_type=F32
    )
    lane = iota(shape, 1)
    offset = jnp.zeros(shape, F32)
    place = jnp.full(shape, -1.0, F32)
    words = jnp.zeros(shape, I32)
    for h in range(4):
        place = jnp.where(heading == h, inner[h] + offset, place)
        base_h = base[:, h * LANES : (h + 1) * LANES]
        word = base_h.astype(I32) + offset.astype(I32) * 1024 + total[h].astype(I32) * (1024 * 256)
        words = jnp.where(lane == h, word, words)
        offset = offset + total[h]
    table_v[...] = words
    load = pltpu.make_async_copy(table_v, table_s, sem)
    load.start()
    pos[...] = place
    pay[1:4, :] = vel[...]
    pay[5:8, :] = cell[...].astype(F32)
    stays = jnp.where(heading == 4, 1.0, 0.0)
    for b in range(chunks):
        lanes = slice(b * LANES, (b + 1) * LANES)
        pay[0:1, lanes] = kept[b : b + 1, :]
        pay[4:5, lanes] = temp[b : b + 1, :]
    for b in range(chunks):
        lanes = slice(b * LANES, (b + 1) * LANES)
        stay[:, lanes] = jnp.where(stays[b : b + 1, :] > 0.0, pay[:, lanes], 0.0)
    group = 16

    def pack(g, carry):
        for u in range(group):
            b = g * group + u
            slots = pos[pl.ds(b, 1), :]
            onehot = jnp.where(slots == iota((LANES, LANES), 0).astype(F32), 1.0, 0.0).astype(BF16)
            rows = pay[:, pl.ds(pl.multiple_of(b * LANES, LANES), LANES)]
            high = rows.astype(BF16).astype(F32)
            rest = rows - high
            middle = rest.astype(BF16).astype(F32)
            low = rest - middle
            parts = jnp.concatenate([high, middle, low, jnp.zeros_like(low)], axis=0).astype(BF16)
            got = lax.dot_general(parts, onehot, TRANSPOSED, preferred_element_type=F32)
            compact[b] = got[0:8] + got[8:16] + got[16:24]
        return carry

    lax.fori_loop(0, chunks // group, pack, 0)
    tiles[...] = jnp.zeros(tiles.shape, F32)
    load.wait()
    lane8 = iota((8, LANES), 1)
    unroll = 8

    def place_all(g, carry):
        carry = list(carry)
        for u in range(unroll):
            b = g * unroll + u
            rows = compact[b]
            for h in range(4):
                word = table_s[b, h]
                start = word & 1023
                first = (word >> 10) & 255
                number = word >> 18
                within = start & (LANES - 1)
                end = within + number
                turned = pltpu.roll(rows, (start - first) & (LANES - 1), 1)
                merged = jnp.where((lane8 >= within) & (lane8 < end), turned, carry[h])
                tiles[h, start >> 7] = merged
                over = jnp.where(lane8 < end - LANES, turned, 0.0)
                carry[h] = jnp.where(end >= LANES, over, merged)
        return tuple(carry)

    carry = lax.fori_loop(
        0, chunks // unroll, place_all, tuple(jnp.zeros((8, LANES), F32) for _ in range(4))
    )
    for h in range(4):
        word = table_s[chunks - 1, h]
        tiles[h, ((word & 1023) + (word >> 18)) >> 7] = carry[h]
    for h, out in enumerate((out0, out1, out2, out3)):
        for t in range(out.shape[1] // LANES):
            out[:, t * LANES : (t + 1) * LANES] = tiles[h, t]


def source_rows(rows):
    kept, temp = rows[0:1], rows[4:5]
    v0, v1, v2 = rows[1:2], rows[2:3], rows[3:4]
    share = sigmoid_of(temp)
    gone = kept * share / (1.0 - SHRINK * share)
    heat = temp + 0.5 * (v0 * v0 + v1 * v1 + v2 * v2)
    fields = [gone, gone * v0, gone * v1, gone * v2, gone * heat]
    high = [f.astype(BF16).astype(F32) for f in fields]
    low = [f - g for f, g in zip(fields, high)]
    return high + low


def spread(columns, sources, number):
    n = columns.shape[1]
    hot = jnp.where(columns == iota((number, n), 0).astype(F32), 1.0, 0.0).astype(BF16)
    hot = hot.reshape(number // 16, 16, n)
    parts = []
    for source in sources:
        value = jnp.broadcast_to(source, (16, n)).astype(BF16)
        parts.append((hot * value[None]).reshape(number, n))
    return jnp.concatenate(parts, axis=0)


def depth_onehot(rows, depth):
    n = rows.shape[1]
    return jnp.where(rows[7:8] == iota((depth, n), 0).astype(F32), 1.0, 0.0).astype(BF16)


def deposit_kernel(cells_x, cells_y, step, stay, state, where_to, dep, acc):
    total = stay.shape[1]
    columns = cells_x * cells_y
    depth = dep.shape[2]
    anchor_x = (lax.axis_index("gx") * cells_x).astype(F32)
    anchor_y = (lax.axis_index("gy") * cells_y).astype(F32)
    acc[...] = jnp.zeros(acc.shape, F32)

    def one(k, carry):
        rows = stay[:, pl.ds(pl.multiple_of(k * step, step), step)]
        column = (rows[5:6] - anchor_x) * cells_y + (rows[6:7] - anchor_y)
        left = spread(column, source_rows(rows), columns)
        acc[...] += lax.dot_general(
            left, depth_onehot(rows, depth), TRANSPOSED, preferred_element_type=F32
        )
        return carry

    lax.fori_loop(0, total // step, one, 0)
    for f in range(5):
        dep[f] = (
            acc[f * columns : (f + 1) * columns, :] + acc[(5 + f) * columns : (6 + f) * columns, :]
        )
    state[:, :total] = stay[0:5, :]
    where_to[:, :total] = stay[5:8, :].astype(I32)


def arrive_kernel(
    cells_x, cells_y, in0, in1, in2, in3, energy, dep4, state_in, where_in,
    planes, face_x0, face_x1, face_y0, face_y1, state, where_to,
):
    depth = planes.shape[3]
    anchor_x = (lax.axis_index("gx") * cells_x).astype(F32)
    anchor_y = (lax.axis_index("gy") * cells_y).astype(F32)
    capacity = in0.shape[1]
    for q, table in enumerate((in0, in1, in2, in3)):
        rows = table[...]
        along = (rows[6:7] - anchor_y) if q < 2 else (rows[5:6] - anchor_x)
        number = cells_y if q < 2 else cells_x
        left = spread(along, source_rows(rows), number)
        got = lax.dot_general(left, depth_onehot(rows, depth), TRANSPOSED, preferred_element_type=F32)
        for f in range(5):
            planes[q, f] = (
                got[f * number : (f + 1) * number] + got[(5 + f) * number : (6 + f) * number]
            )
        lanes = slice(q * capacity, (q + 1) * capacity)
        state[:, lanes] = rows[0:5]
        where_to[:, lanes] = rows[5:8].astype(I32)
    scale = ADIABATIC_INDEX - 1.0
    row = iota((cells_y, depth), 0)
    for q, face, x in ((0, face_x0, 0), (1, face_x1, cells_x - 1)):
        plane = energy[x] + dep4[x] + planes[q, 4]
        plane = plane + jnp.where(row == 0, planes[2, 4, x : x + 1, :], 0.0)
        plane = plane + jnp.where(row == cells_y - 1, planes[3, 4, x : x + 1, :], 0.0)
        face[...] = scale * plane
    row = iota((cells_x, depth), 0)
    for q, face, y in ((2, face_y0, 0), (3, face_y1, cells_y - 1)):
        plane = energy[:, y, :] + dep4[:, y, :] + planes[q, 4]
        plane = plane + jnp.where(row == 0, planes[0, 4, y : y + 1, :], 0.0)
        plane = plane + jnp.where(row == cells_x - 1, planes[1, 4, y : y + 1, :], 0.0)
        face[...] = scale * plane


def update_kernel(
    cells_x, cells_y, density, momentum, energy, dep, planes, halo_x0, halo_x1, halo_y0, halo_y1,
    rho_out, impulse, energy_out, fastest, pressure,
):
    depth = energy.shape[2]
    scale = ADIABATIC_INDEX - 1.0
    shape = (cells_y, depth)
    row = iota(shape, 0)
    lane = iota(shape, 1)

    def with_planes(f, x, value):
        if x == 0:
            value = value + planes[0, f]
        if x == cells_x - 1:
            value = value + planes[1, f]
        value = value + jnp.where(row == 0, planes[2, f, x : x + 1, :], 0.0)
        return value + jnp.where(row == cells_y - 1, planes[3, f, x : x + 1, :], 0.0)

    pressure[0] = halo_x0[...]
    pressure[cells_x + 1] = halo_x1[...]
    for x in range(cells_x):
        value = with_planes(4, x, energy[x] + dep[4, x])
        energy_out[x] = value
        pressure[x + 1] = scale * value
    top = jnp.zeros(shape, F32)
    for x in range(cells_x):
        here = pressure[x + 1]
        grad_x = 0.5 * (pressure[x + 2] - pressure[x])
        after = jnp.where(row == cells_y - 1, halo_y1[x : x + 1, :], pltpu.roll(here, cells_y - 1, 0))
        before = jnp.where(row == 0, halo_y0[x : x + 1, :], pltpu.roll(here, 1, 0))
        grad_y = 0.5 * (after - before)
        after = jnp.where(lane == depth - 1, 0.0, pltpu.roll(here, depth - 1, 1))
        before = jnp.where(lane == 0, 0.0, pltpu.roll(here, 1, 1))
        grad_z = 0.5 * (after - before)
        rho = with_planes(0, x, density[x] + dep[0, x])
        rho_out[x] = rho
        largest = jnp.zeros(shape, F32)
        for k, grad in enumerate((grad_x, grad_y, grad_z)):
            value = with_planes(1 + k, x, momentum[k, x] + dep[1 + k, x]) - KICK * grad
            impulse[k, x] = value
            largest = jnp.maximum(largest, jnp.abs(value))
        wave = largest / rho + jnp.sqrt(ADIABATIC_INDEX * here / rho)
        top = jnp.maximum(top, wave)
    fastest[...] = jnp.max(top, axis=(0, 1), keepdims=True)


def call(kernel, outs, scratch=(), out_specs=None, in_specs=None, aliases=None, name=None, **extra):
    if in_specs is not None:
        extra["in_specs"] = in_specs
    if out_specs is not None:
        extra["out_specs"] = out_specs
    return pl.pallas_call(
        kernel,
        out_shape=outs,
        scratch_shapes=list(scratch),
        input_output_aliases=aliases or {},
        compiler_params=pltpu.CompilerParams(vmem_limit_bytes=48 * 1024 * 1024),
        name=name,
        **extra,
    )


def on_device(
    density, momentum, energy, parcel_mass, droplet_velocity, parcel_temp, parcel_cell, parcel_count
):
    cells_x, cells_y, depth = density.shape
    rows = parcel_mass.shape[0]
    capacity = rows // 16
    chunks = rows // LANES
    sds = jax.ShapeDtypeStruct
    whole = pl.BlockSpec(memory_space=VMEM)
    bucket = sds((8, capacity), F32)
    *buckets, stay = call(
        functools.partial(prep_kernel, cells_x, cells_y),
        (bucket, bucket, bucket, bucket, sds((8, rows), F32)),
        scratch=(
            VMEM((8, rows), F32),
            VMEM((chunks, LANES), I32),
            VMEM((chunks, LANES), I32),
            VMEM((chunks, LANES), F32),
            VMEM((chunks, 8, LANES), F32),
            VMEM((chunks, LANES), I32),
            pltpu.SMEM((chunks, LANES), I32),
            VMEM((4, capacity // LANES + 1, 8, LANES), F32),
            pltpu.SemaphoreType.DMA,
        ),
        in_specs=[pl.BlockSpec(memory_space=pltpu.SMEM)] + [whole] * 4,
        name="prep",
    )(
        parcel_count,
        parcel_mass.reshape(chunks, LANES),
        parcel_temp.reshape(chunks, LANES),
        droplet_velocity,
        parcel_cell,
    )

    def exchange(to_low_x, to_high_x, to_low_y, to_high_y):
        got = []
        for axis, down, up in (("gx", to_low_x, to_high_x), ("gy", to_low_y, to_high_y)):
            ends = lax.axis_size(axis) - 1
            got.append(lax.ppermute(up, axis, [(i, i + 1) for i in range(ends)]))
            got.append(lax.ppermute(down, axis, [(i + 1, i) for i in range(ends)]))
        return got

    arrived = exchange(*buckets)
    slots = rows + 4 * capacity
    state, where_to, dep = call(
        functools.partial(deposit_kernel, cells_x, cells_y, min(1024, rows)),
        (sds((5, slots), F32), sds((3, slots), I32), sds((5, cells_x * cells_y, depth), F32)),
        scratch=(VMEM((10 * cells_x * cells_y, depth), F32),),
        name="deposit",
    )(stay)
    dep = dep.reshape(5, cells_x, cells_y, depth)
    face = lambda n: sds((n, depth), F32)
    planes, *faces, state, where_to = call(
        functools.partial(arrive_kernel, cells_x, cells_y),
        (
            sds((4, 5, cells_x, depth), F32),
            face(cells_y), face(cells_y), face(cells_x), face(cells_x),
            sds(state.shape, F32),
            sds(where_to.shape, I32),
        ),
        in_specs=[whole] * 5
        + [pl.BlockSpec((None, cells_x, cells_y, depth), lambda i: (4, 0, 0, 0))]
        + [pl.BlockSpec(memory_space=pl.ANY)] * 2,
        out_specs=(whole,) * 5
        + (
            pl.BlockSpec((5, 4 * capacity), lambda i: (0, rows // (4 * capacity))),
            pl.BlockSpec((3, 4 * capacity), lambda i: (0, rows // (4 * capacity))),
        ),
        aliases={6: 5, 7: 6},
        name="arrive",
        grid=(1,),
    )(*arrived, energy, dep, state, where_to)
    halos = exchange(*faces)
    rho, impulse, energy_out, top = call(
        functools.partial(update_kernel, cells_x, cells_y),
        (
            sds(density.shape, F32),
            sds(momentum.shape, F32),
            sds(energy.shape, F32),
            sds((1, 1), F32),
        ),
        scratch=(VMEM((cells_x + 2, cells_y, depth), F32),),
        name="update",
    )(density, momentum, energy, dep, planes, *halos)
    fastest = lax.pmax(top[0, 0], ("gx", "gy"))
    return rho, impulse, energy_out, state, where_to, COURANT / fastest


def solution(mesh):
    both = ("gx", "gy")
    return jax.shard_map(
        on_device,
        mesh=mesh,
        in_specs=(
            P("gx", "gy", None),
            P(None, "gx", "gy", None),
            P("gx", "gy", None),
            P(both),
            P(None, both),
            P(both),
            P(None, both),
            P(both),
        ),
        out_specs=(
            P("gx", "gy", None),
            P(None, "gx", "gy", None),
            P("gx", "gy", None),
            P(None, both),
            P(None, both),
            P(),
        ),
        check_vma=False,
    )
```

time: 281 us -> 150 us (0.53); the launches traced: 276 us -> 150 us
  local copies, waits for them, and re-layouts: 110 us -> 4.27 us
  other arithmetic: 77.4 us -> 0 us
  blocking collectives: 61.9 us -> 96.8 us
  Pallas kernels: 0 us -> 19.7 us
  waiting for transfers between devices: 0.03 us -> 3.17 us
    scatter-add x3 -> x0, other arithmetic: 61.9 us -> none  [the longest x1 61 us: deposit_one(): return jax.ops.segment_sum(values, cell_slot, num_segments=total_cells)]
    pmax x5 -> x1, blocking collectives: 61.9 us -> 96.8 us  [on_device(): fastest = lax.pmax(top[0, 0], ('gx', 'gy'))]
    slice x17 -> x0, local copies, waits for them, and re-layouts: 29.3 us -> none  [the longest x1 11.9 us: on_device(): core = flat_sums[:, :block_cells].reshape(5, cells_x, cells_y, depth_cells)]
    reshape x3 -> x0, local copies, waits for them, and re-layouts: 24.6 us -> none  [the longest x1 19.5 us: on_device(): core = flat_sums[:, :block_cells].reshape(5, cells_x, cells_y, depth_cells)]
    scatter x1 -> x0, local copies, waits for them, and re-layouts: 21.1 us -> none  [on_device(): buckets = jnp.zeros((9, 4 * capacity), jnp.float32).at[:, target].set(car...]
    pallas_call x0 -> x4, Pallas kernels: none -> 19.7 us  [the longest x1 13.6 us: on_device(): call(functools.partial(deposit_kernel, cells_x, cells_y, min(1024, rows))...]
    unnamed x28 -> x16, local copies, waits for them, and re-layouts: 16.8 us -> 4.27 us
    scatter-add x6 -> x0, local copies, waits for them, and re-layouts: 9.38 us -> none  [the longest x1 3.23 us: on_device(): core.at[:, :, 0].add(got_y[0, :size_y].reshape(5, cells_x, depth_cells))]
  transfers between devices with their start and end apart: 8 -> 8, of which waited for: 0 -> 1; matrix products, arithmetic and copies ran while one was open for 20% -> 0% of each run, Pallas kernels for 0% -> 9%
where the time goes in v1:
time: 150 us
  blocking collectives  96.8 us (65%)
  starting transfers between devices  22.6 us (15%)
  Pallas kernels  19.7 us (13%)
  local copies, waits for them, and re-layouts  4.27 us (3%)
  between operations  3.23 us (2%)
  waiting for transfers between devices  3.17 us (2%)
    pmax x1, blocking collectives, on_device(): fastest = lax.pmax(top[0, 0], ('gx', 'gy'))  96.8 us
    ppermute x4, starting transfers between devices, exchange(): got.append(lax.ppermute(up, axis, [(i, i + 1) for i in range(ends)]))  16.2 us
    pallas_call x1, Pallas kernels, on_device(): call(functools.partial(deposit_kernel, cells_x, cells_y, min(1024, rows))...  13.6 us
    ppermute x4, starting transfers between devices, exchange(): got.append(lax.ppermute(down, axis, [(i + 1, i) for i in range(ends)]))  6.43 us
    unnamed x16, local copies, waits for them, and re-layouts  4.27 us
    pallas_call x1, Pallas kernels, on_device(): call(functools.partial(prep_kernel, cells_x, cells_y), (bucket, bucket, b...  3.51 us
    ppermute x4, waiting for transfers between devices, exchange(): got.append(lax.ppermute(down, axis, [(i + 1, i) for i in range(ends)]))  3.16 us
  transfers between devices with their start and end apart: 8, of which 1 were waited for; matrix products, arithmetic and copies ran while one was open for 0% of the time, Pallas kernels for 9%

profile of v1, /device:TPU:1, one launch (start us, length us, event | category | flops | bytes accessed | tf_op | source)
XLA Modules:
  0.0 149.8 jit_solution(10935235401479632771)
XLA Ops:
  1.3 0.9 copy-done.4
  2.2 0.9 copy-done.5
  3.1 0.8 copy-done.6
  3.9 0.8 copy-done.7
  4.6 3.5 %prep.1 = (f32[8,512]{1,0:T(8,128)S(1)}, f32[8,512]{1,0:T(8,128)S(1)}, f32[8,512]{1,0:T(8,128)S(1)}, f32[8,512]{1,0:T(8,128)S(1)}, f32[8,8192]{1,0:T(8,128)S(1)}) custom-call(s32[1]{0:T(128)S(6)} %copy.18.count, f32[64,128]{1,0:T(8,128)S(1)} %bitcast.6, f32[64,128]{1,0:T(8,128)S(1)} %bitcast.7, f32[3,8192]{1,0:T(4,128)S(1)} %copy-done.4, s32[3,8192]{1,0:T(4,128)S(1)} %copy-done.5), custom_call_target="tpu_custom_call" | custom-call | tf_op jit(solution)/shard_map/prep/pallas_call | solution.py:308
  8.1 4.9 %collective-permute-start = (f32[8,512]{1,0:T(8,128)S(1)}, f32[8,512]{1,0:T(8,128)S(1)}, u32[]{:S(2)}, u32[]{:S(2)}) collective-permute-start(f32[8,512]{1,0:T(8,128)S(1)} %get-tuple-element.27), channel_id=1, source_target_pairs={{0,32},{32,64},{64,96},{96,128},{128,160},{160,192},{192,224},{1,3... | collective-permute-start | bytes 49160 | tf_op jit(solution)/shard_map/ppermute | solution.py:336
  13.1 1.9 %collective-permute-start.1 = (f32[8,512]{1,0:T(8,128)S(1)}, f32[8,512]{1,0:T(8,128)S(1)}, u32[]{:S(2)}, u32[]{:S(2)}) collective-permute-start(f32[8,512]{1,0:T(8,128)S(1)} %get-tuple-element.28), channel_id=1, source_target_pairs={{32,0},{64,32},{96,64},{128,96},{160,128},{192,160},{224,192},{33,... | collective-permute-start | bytes 49160 | tf_op jit(solution)/shard_map/ppermute | solution.py:337
  15.0 3.1 %collective-permute-start.2 = (f32[8,512]{1,0:T(8,128)S(1)}, f32[8,512]{1,0:T(8,128)S(1)}, u32[]{:S(2)}, u32[]{:S(2)}) collective-permute-start(f32[8,512]{1,0:T(8,128)S(1)} %get-tuple-element.29), channel_id=1, source_target_pairs={{0,1},{1,2},{2,3},{3,4},{4,5},{5,6},{6,7},{7,8},{8,9},{9,10},{10,1... | collective-permute-start | bytes 49160 | tf_op jit(solution)/shard_map/ppermute | solution.py:336
  18.1 1.3 collective-permute-start.3
  19.4 13.6 %deposit.1 = (f32[5,10240]{1,0:T(8,128)}, s32[3,10240]{1,0:T(4,128)}, f32[5,256,256]{2,1,0:T(8,128)S(1)}) custom-call(f32[8,8192]{1,0:T(8,128)S(1)} %get-tuple-element.25.stay), custom_call_target="tpu_custom_call" | custom-call | tf_op jit(solution)/shard_map/deposit/pallas_call | solution.py:342
  33.0 0.0 collective-permute-done.1.in1
  33.0 0.0 collective-permute-done.2.in2
  33.0 0.0 copy-start
  33.0 0.9 copy-done
  34.0 1.0 arrive.1
  35.0 3.9 %collective-permute-start.4 = (f32[16,256]{1,0:T(8,128)S(1)}, f32[16,256]{1,0:T(8,128)S(1)}, u32[]{:S(2)}, u32[]{:S(2)}) collective-permute-start(f32[16,256]{1,0:T(8,128)S(1)} %get-tuple-element.34), channel_id=1, source_target_pairs={{0,32},{32,64},{64,96},{96,128},{128,160},{160,192},{192,224},{1,3... | collective-permute-start | bytes 49160 | tf_op jit(solution)/shard_map/ppermute | solution.py:336
  38.9 1.9 %collective-permute-start.5 = (f32[16,256]{1,0:T(8,128)S(1)}, f32[16,256]{1,0:T(8,128)S(1)}, u32[]{:S(2)}, u32[]{:S(2)}) collective-permute-start(f32[16,256]{1,0:T(8,128)S(1)} %get-tuple-element.35), channel_id=1, source_target_pairs={{32,0},{64,32},{96,64},{128,96},{160,128},{192,160},{224,192},{33,... | collective-permute-start | bytes 49160 | tf_op jit(solution)/shard_map/ppermute | solution.py:337
  40.8 4.3 %collective-permute-start.6 = (f32[16,256]{1,0:T(8,128)S(1)}, f32[16,256]{1,0:T(8,128)S(1)}, u32[]{:S(2)}, u32[]{:S(2)}) collective-permute-start(f32[16,256]{1,0:T(8,128)S(1)} %get-tuple-element.36), channel_id=1, source_target_pairs={{0,1},{1,2},{2,3},{3,4},{4,5},{5,6},{6,7},{7,8},{8,9},{9,10},{10,1... | collective-permute-start | bytes 49160 | tf_op jit(solution)/shard_map/ppermute | solution.py:336
  45.1 1.3 collective-permute-start.7
  46.4 0.0 collective-permute-done.4.halo_x0
  46.4 0.0 collective-permute-done.6.halo_y0
  46.4 3.2 %collective-permute-done.7.halo_y1 = f32[16,256]{1,0:T(8,128)S(1)} collective-permute-done((f32[16,256]{1,0:T(8,128)S(1)}, f32[16,256]{1,0:T(8,128)S(1)}, u32[]{:S(2)}, u32[]{:S(2)}) %collective-permute-start.7) | collective-permute-done | bytes 16416 | tf_op jit(solution)/shard_map/ppermute | solution.py:337
  49.6 1.6 %update.1 = (f32[16,16,256]{2,1,0:T(8,128)}, f32[3,16,16,256]{3,2,1,0:T(8,128)}, f32[16,16,256]{2,1,0:T(8,128)}, f32[1,1]{1,0:T(1,128)}) custom-call(f32[16,16,256]{2,1,0:T(8,128)S(1)} %copy-done.3, f32[3,16,16,256]{3,2,1,0:T(8,128)S(1)} %copy-done.2, f32[16,16,256]{2,1,0:T(8,128)S(1)} %copy-done.1, f32[5,16,16,256]{3,2,1,0:T(8,128)S(1)} %bitcast.5, ...), custom_call_target="tpu_custom_call" | custom-call | tf_op jit(solution)/shard_map/update/pallas_call | solution.py:371
  51.2 96.8 %pmax.7 = f32[]{:T(128)} all-reduce(f32[]{:T(128)} %bitcast.3), channel_id=1, replica_groups=mesh['gx'=8,'gy'=32] {'gx','gy'}, use_global_device_ids=true, to_apply=%region_0.0 | all-reduce | flops 1 | bytes 8 | tf_op jit(solution)/shard_map/pmax | solution.py:382
  (13 shorter events, 0.0 us)
Async XLA Ops:
  1.3 0.9 copy-start.4
  2.2 0.9 copy-start.5
  3.1 0.8 copy-start.6
  3.8 0.8 copy-start.7
  4.6 45.0 %copy-start.1 = (f32[16,16,256]{2,1,0:T(8,128)S(1)}, f32[16,16,256]{2,1,0:T(8,128)}, u32[]{:S(2)}) copy-start(f32[16,16,256]{2,1,0:T(8,128)} %energy.3) | copy-start | bytes 786436
  4.6 45.0 %copy-start.3 = (f32[16,16,256]{2,1,0:T(8,128)S(1)}, f32[16,16,256]{2,1,0:T(8,128)}, u32[]{:S(2)}) copy-start(f32[16,16,256]{2,1,0:T(8,128)} %density.1) | copy-start | bytes 786436
  8.1 24.9 %collective-permute-start = (f32[8,512]{1,0:T(8,128)S(1)}, f32[8,512]{1,0:T(8,128)S(1)}, u32[]{:S(2)}, u32[]{:S(2)}) collective-permute-start(f32[8,512]{1,0:T(8,128)S(1)} %get-tuple-element.27), channel_id=1, source_target_pairs={{0,32},{32,64},{64,96},{96,128},{128,160},{160,192},{192,224},{1,3... | collective-permute-start | bytes 49160 | tf_op jit(solution)/shard_map/ppermute | solution.py:336
  13.1 19.9 %collective-permute-start.1 = (f32[8,512]{1,0:T(8,128)S(1)}, f32[8,512]{1,0:T(8,128)S(1)}, u32[]{:S(2)}, u32[]{:S(2)}) collective-permute-start(f32[8,512]{1,0:T(8,128)S(1)} %get-tuple-element.28), channel_id=1, source_target_pairs={{32,0},{64,32},{96,64},{128,96},{160,128},{192,160},{224,192},{33,... | collective-permute-start | bytes 49160 | tf_op jit(solution)/shard_map/ppermute | solution.py:337
  15.0 18.0 %collective-permute-start.2 = (f32[8,512]{1,0:T(8,128)S(1)}, f32[8,512]{1,0:T(8,128)S(1)}, u32[]{:S(2)}, u32[]{:S(2)}) collective-permute-start(f32[8,512]{1,0:T(8,128)S(1)} %get-tuple-element.29), channel_id=1, source_target_pairs={{0,1},{1,2},{2,3},{3,4},{4,5},{5,6},{6,7},{7,8},{8,9},{9,10},{10,1... | collective-permute-start | bytes 49160 | tf_op jit(solution)/shard_map/ppermute | solution.py:336
  18.1 14.9 %collective-permute-start.3 = (f32[8,512]{1,0:T(8,128)S(1)}, f32[8,512]{1,0:T(8,128)S(1)}, u32[]{:S(2)}, u32[]{:S(2)}) collective-permute-start(f32[8,512]{1,0:T(8,128)S(1)} %get-tuple-element.30), channel_id=1, source_target_pairs={{1,0},{2,1},{3,2},{4,3},{5,4},{6,5},{7,6},{8,7},{9,8},{10,9},{11,1... | collective-permute-start | bytes 49160 | tf_op jit(solution)/shard_map/ppermute | solution.py:337
  33.0 1.0 copy-start
  34.0 15.6 %copy-start.2 = (f32[3,16,16,256]{3,2,1,0:T(8,128)S(1)}, f32[3,16,16,256]{3,2,1,0:T(8,128)}, u32[]{:S(2)}) copy-start(f32[3,16,16,256]{3,2,1,0:T(8,128)} %momentum.1) | copy-start | bytes 2359300
  35.0 11.4 %collective-permute-start.4 = (f32[16,256]{1,0:T(8,128)S(1)}, f32[16,256]{1,0:T(8,128)S(1)}, u32[]{:S(2)}, u32[]{:S(2)}) collective-permute-start(f32[16,256]{1,0:T(8,128)S(1)} %get-tuple-element.34), channel_id=1, source_target_pairs={{0,32},{32,64},{64,96},{96,128},{128,160},{160,192},{192,224},{1,3... | collective-permute-start | bytes 49160 | tf_op jit(solution)/shard_map/ppermute | solution.py:336
  38.9 7.5 %collective-permute-start.5 = (f32[16,256]{1,0:T(8,128)S(1)}, f32[16,256]{1,0:T(8,128)S(1)}, u32[]{:S(2)}, u32[]{:S(2)}) collective-permute-start(f32[16,256]{1,0:T(8,128)S(1)} %get-tuple-element.35), channel_id=1, source_target_pairs={{32,0},{64,32},{96,64},{128,96},{160,128},{192,160},{224,192},{33,... | collective-permute-start | bytes 49160 | tf_op jit(solution)/shard_map/ppermute | solution.py:337
  40.8 5.6 %collective-permute-start.6 = (f32[16,256]{1,0:T(8,128)S(1)}, f32[16,256]{1,0:T(8,128)S(1)}, u32[]{:S(2)}, u32[]{:S(2)}) collective-permute-start(f32[16,256]{1,0:T(8,128)S(1)} %get-tuple-element.36), channel_id=1, source_target_pairs={{0,1},{1,2},{2,3},{3,4},{4,5},{5,6},{6,7},{7,8},{8,9},{9,10},{10,1... | collective-permute-start | bytes 49160 | tf_op jit(solution)/shard_map/ppermute | solution.py:336
  45.1 4.5 %collective-permute-start.7 = (f32[16,256]{1,0:T(8,128)S(1)}, f32[16,256]{1,0:T(8,128)S(1)}, u32[]{:S(2)}, u32[]{:S(2)}) collective-permute-start(f32[16,256]{1,0:T(8,128)S(1)} %get-tuple-element.37), channel_id=1, source_target_pairs={{1,0},{2,1},{3,2},{4,3},{5,4},{6,5},{7,6},{8,7},{9,8},{10,9},{11,1... | collective-permute-start | bytes 49160 | tf_op jit(solution)/shard_map/ppermute | solution.py:337

commit v2 on v1

--- a/solution.py
+++ b/solution.py
@@ -31,8 +31,18 @@
 def prep_kernel(
     cells_x, cells_y, count, mass, temp, vel, cell,
     out0, out1, out2, out3, stay,
-    pay, cx, cy, pos, compact, table_v, table_s, tiles, sem,
+    mass_v, temp_v, vel_v, cell_v, pay, cx, cy, pos, compact, table_v, table_s, tiles, sems,
 ):
+    fetches = [
+        pltpu.make_async_copy(there, here, sems.at[i])
+        for i, (there, here) in enumerate(
+            ((cell, cell_v), (temp, temp_v), (mass, mass_v), (vel, vel_v))
+        )
+    ]
+    for fetch in fetches:
+        fetch.start()
+    mass, temp, vel, cell = mass_v, temp_v, vel_v, cell_v
+    fetches[0].wait()
     chunks = mass.shape[0]
     anchor_x = lax.axis_index("gx") * cells_x
     anchor_y = lax.axis_index("gy") * cells_y
@@ -42,6 +52,8 @@
         cy[b : b + 1, :] = cell[1:2, lanes]
     shape = (chunks, LANES)
     live = iota(shape, 0) * LANES + iota(shape, 1) < count[0]
+    fetches[1].wait()
+    fetches[2].wait()
     kept = mass[...] * (1.0 - SHRINK * jnp.where(live, sigmoid_of(temp[...]), 0.0))
     local_x = cx[...] - anchor_x
     local_y = cy[...] - anchor_y
@@ -77,9 +89,10 @@
         words = jnp.where(lane == h, word, words)
         offset = offset + total[h]
     table_v[...] = words
-    load = pltpu.make_async_copy(table_v, table_s, sem)
+    load = pltpu.make_async_copy(table_v, table_s, sems.at[4])
     load.start()
     pos[...] = place
+    fetches[3].wait()
     pay[1:4, :] = vel[...]
     pay[5:8, :] = cell[...].astype(F32)
     stays = jnp.where(heading == 4, 1.0, 0.0)
@@ -276,7 +289,7 @@
             largest = jnp.maximum(largest, jnp.abs(value))
         wave = largest / rho + jnp.sqrt(ADIABATIC_INDEX * here / rho)
         top = jnp.maximum(top, wave)
-    fastest[...] = jnp.max(top, axis=(0, 1), keepdims=True)
+    fastest[...] = jnp.broadcast_to(jnp.max(top, axis=(0, 1), keepdims=True), fastest.shape)
 
 
 def call(kernel, outs, scratch=(), out_specs=None, in_specs=None, aliases=None, name=None, **extra):
@@ -309,6 +322,10 @@
         functools.partial(prep_kernel, cells_x, cells_y),
         (bucket, bucket, bucket, bucket, sds((8, rows), F32)),
         scratch=(
+            VMEM((chunks, LANES), F32),
+            VMEM((chunks, LANES), F32),
+            VMEM((3, rows), F32),
+            VMEM((3, rows), I32),
             VMEM((8, rows), F32),
             VMEM((chunks, LANES), I32),
             VMEM((chunks, LANES), I32),
@@ -317,9 +334,9 @@
             VMEM((chunks, LANES), I32),
             pltpu.SMEM((chunks, LANES), I32),
             VMEM((4, capacity // LANES + 1, 8, LANES), F32),
-            pltpu.SemaphoreType.DMA,
-        ),
-        in_specs=[pl.BlockSpec(memory_space=pltpu.SMEM)] + [whole] * 4,
+            pltpu.SemaphoreType.DMA((5,)),
+        ),
+        in_specs=[pl.BlockSpec(memory_space=pltpu.SMEM)] + [pl.BlockSpec(memory_space=pltpu.HBM)] * 4,
         name="prep",
     )(
         parcel_count,
@@ -374,12 +391,12 @@
             sds(density.shape, F32),
             sds(momentum.shape, F32),
             sds(energy.shape, F32),
-            sds((1, 1), F32),
+            sds((lax.axis_size(("gx", "gy")), LANES), F32),
         ),
         scratch=(VMEM((cells_x + 2, cells_y, depth), F32),),
         name="update",
     )(density, momentum, energy, dep, planes, *halos)
-    fastest = lax.pmax(top[0, 0], ("gx", "gy"))
+    fastest = jnp.max(lax.all_to_all(top, ("gx", "gy"), 0, 0, tiled=True))
     return rho, impulse, energy_out, state, where_to, COURANT / fastest
 
 

time: 150 us -> 99.2 us (0.66)
  blocking collectives: 96.8 us -> 44.3 us
    pmax x1 -> x0, blocking collectives: 96.8 us -> none  [on_device(): fastest = lax.pmax(top[0, 0], ('gx', 'gy'))]
    all_to_all x0 -> x1, blocking collectives: none -> 44.3 us  [on_device(): fastest = jnp.max(lax.all_to_all(top, ('gx', 'gy'), 0, 0, tiled=True))]
  transfers between devices with their start and end apart: 8 -> 8, of which waited for: 1 -> 1; matrix products, arithmetic and copies ran while one was open for 0% -> 0% of each run, Pallas kernels for 9% -> 14%
where the time goes in v2:
time: 99.2 us; the launch traced here: 98.7 us
  blocking collectives  44.3 us (45%)
  starting transfers between devices  22.6 us (23%)
  Pallas kernels  20.1 us (20%)
  local copies, waits for them, and re-layouts  4.27 us (4%)
  between operations  3.23 us (3%)
  waiting for transfers between devices  3.17 us (3%)
    all_to_all x1, blocking collectives, on_device(): fastest = jnp.max(lax.all_to_all(top, ('gx', 'gy'), 0, 0, tiled=True))  44.3 us
    ppermute x4, starting transfers between devices, exchange(): got.append(lax.ppermute(up, axis, [(i, i + 1) for i in range(ends)]))  16.2 us
    pallas_call x1, Pallas kernels, on_device(): call(functools.partial(deposit_kernel, cells_x, cells_y, min(1024, rows))...  13.6 us
    ppermute x4, starting transfers between devices, exchange(): got.append(lax.ppermute(down, axis, [(i + 1, i) for i in range(ends)]))  6.43 us
    unnamed x16, local copies, waits for them, and re-layouts  4.27 us
    pallas_call x1, Pallas kernels, on_device(): call(functools.partial(prep_kernel, cells_x, cells_y), (bucket, bucket, b...  3.99 us
    ppermute x4, waiting for transfers between devices, exchange(): got.append(lax.ppermute(down, axis, [(i + 1, i) for i in range(ends)]))  3.16 us
  transfers between devices with their start and end apart: 8, of which 1 were waited for; matrix products, arithmetic and copies ran while one was open for 0% of the time, Pallas kernels for 14%

profile of v2, /device:TPU:1, one launch (start us, length us, event | category | flops | bytes accessed | tf_op | source)
XLA Modules:
  0.0 98.7 jit_solution(12309893529632726957)
XLA Ops:
  1.3 0.9 copy-done.4
  2.2 0.9 copy-done.5
  3.1 0.8 copy-done.6
  3.9 0.8 copy-done.7
  4.6 4.0 %prep.1 = (f32[8,512]{1,0:T(8,128)S(1)}, f32[8,512]{1,0:T(8,128)S(1)}, f32[8,512]{1,0:T(8,128)S(1)}, f32[8,512]{1,0:T(8,128)S(1)}, f32[8,8192]{1,0:T(8,128)S(1)}) custom-call(s32[1]{0:T(128)S(6)} %copy.19.count, f32[64,128]{1,0:T(8,128)S(1)} %bitcast.9, f32[64,128]{1,0:T(8,128)S(1)} %bitcast.10, f32[3,8192]{1,0:T(4,128)S(1)} %copy-done.4, ...), custom_call_target="tpu_custom_call" | custom-call | tf_op jit(solution)/shard_map/prep/pallas_call | solution.py:321
  8.6 4.9 %collective-permute-start = (f32[8,512]{1,0:T(8,128)S(1)}, f32[8,512]{1,0:T(8,128)S(1)}, u32[]{:S(2)}, u32[]{:S(2)}) collective-permute-start(f32[8,512]{1,0:T(8,128)S(1)} %get-tuple-element.27), channel_id=1, source_target_pairs={{0,32},{32,64},{64,96},{96,128},{128,160},{160,192},{192,224},{1,3... | collective-permute-start | bytes 49160 | tf_op jit(solution)/shard_map/ppermute | solution.py:353
  13.5 1.9 %collective-permute-start.1 = (f32[8,512]{1,0:T(8,128)S(1)}, f32[8,512]{1,0:T(8,128)S(1)}, u32[]{:S(2)}, u32[]{:S(2)}) collective-permute-start(f32[8,512]{1,0:T(8,128)S(1)} %get-tuple-element.28), channel_id=1, source_target_pairs={{32,0},{64,32},{96,64},{128,96},{160,128},{192,160},{224,192},{33,... | collective-permute-start | bytes 49160 | tf_op jit(solution)/shard_map/ppermute | solution.py:354
  15.5 3.1 %collective-permute-start.2 = (f32[8,512]{1,0:T(8,128)S(1)}, f32[8,512]{1,0:T(8,128)S(1)}, u32[]{:S(2)}, u32[]{:S(2)}) collective-permute-start(f32[8,512]{1,0:T(8,128)S(1)} %get-tuple-element.29), channel_id=1, source_target_pairs={{0,1},{1,2},{2,3},{3,4},{4,5},{5,6},{6,7},{7,8},{8,9},{9,10},{10,1... | collective-permute-start | bytes 49160 | tf_op jit(solution)/shard_map/ppermute | solution.py:353
  18.6 1.3 %collective-permute-start.3 = (f32[8,512]{1,0:T(8,128)S(1)}, f32[8,512]{1,0:T(8,128)S(1)}, u32[]{:S(2)}, u32[]{:S(2)}) collective-permute-start(f32[8,512]{1,0:T(8,128)S(1)} %get-tuple-element.30), channel_id=1, source_target_pairs={{1,0},{2,1},{3,2},{4,3},{5,4},{6,5},{7,6},{8,7},{9,8},{10,9},{11,1... | collective-permute-start | bytes 49160 | tf_op jit(solution)/shard_map/ppermute | solution.py:354
  19.9 13.6 %deposit.1 = (f32[5,10240]{1,0:T(8,128)}, s32[3,10240]{1,0:T(4,128)}, f32[5,256,256]{2,1,0:T(8,128)S(1)}) custom-call(f32[8,8192]{1,0:T(8,128)S(1)} %get-tuple-element.25.stay), custom_call_target="tpu_custom_call" | custom-call | tf_op jit(solution)/shard_map/deposit/pallas_call | solution.py:359
  33.5 0.0 collective-permute-done.2.in2
  33.5 0.0 collective-permute-done.3.in3
  33.5 0.0 copy-start
  33.5 0.9 copy-done
  34.4 1.0 %arrive.1 = (f32[4,5,16,256]{3,2,1,0:T(8,128)S(1)}, f32[16,256]{1,0:T(8,128)S(1)}, f32[16,256]{1,0:T(8,128)S(1)}, f32[16,256]{1,0:T(8,128)S(1)}, f32[16,256]{1,0...) custom-call(f32[8,512]{1,0:T(8,128)S(1)} %collective-permute-done.in0, ...), custom_call_target="tpu_custom_call", output_to_operand_aliasing={{5}: (6, {}), {6}: (7, {})} | custom-call | tf_op jit(solution)/shard_map/arrive/pallas_call | solution.py:367
  35.4 3.9 %collective-permute-start.4 = (f32[16,256]{1,0:T(8,128)S(1)}, f32[16,256]{1,0:T(8,128)S(1)}, u32[]{:S(2)}, u32[]{:S(2)}) collective-permute-start(f32[16,256]{1,0:T(8,128)S(1)} %get-tuple-element.34), channel_id=1, source_target_pairs={{0,32},{32,64},{64,96},{96,128},{128,160},{160,192},{192,224},{1,3... | collective-permute-start | bytes 49160 | tf_op jit(solution)/shard_map/ppermute | solution.py:353
  39.4 1.9 %collective-permute-start.5 = (f32[16,256]{1,0:T(8,128)S(1)}, f32[16,256]{1,0:T(8,128)S(1)}, u32[]{:S(2)}, u32[]{:S(2)}) collective-permute-start(f32[16,256]{1,0:T(8,128)S(1)} %get-tuple-element.35), channel_id=1, source_target_pairs={{32,0},{64,32},{96,64},{128,96},{160,128},{192,160},{224,192},{33,... | collective-permute-start | bytes 49160 | tf_op jit(solution)/shard_map/ppermute | solution.py:354
  41.3 4.3 %collective-permute-start.6 = (f32[16,256]{1,0:T(8,128)S(1)}, f32[16,256]{1,0:T(8,128)S(1)}, u32[]{:S(2)}, u32[]{:S(2)}) collective-permute-start(f32[16,256]{1,0:T(8,128)S(1)} %get-tuple-element.36), channel_id=1, source_target_pairs={{0,1},{1,2},{2,3},{3,4},{4,5},{5,6},{6,7},{7,8},{8,9},{9,10},{10,1... | collective-permute-start | bytes 49160 | tf_op jit(solution)/shard_map/ppermute | solution.py:353
  45.6 1.3 %collective-permute-start.7 = (f32[16,256]{1,0:T(8,128)S(1)}, f32[16,256]{1,0:T(8,128)S(1)}, u32[]{:S(2)}, u32[]{:S(2)}) collective-permute-start(f32[16,256]{1,0:T(8,128)S(1)} %get-tuple-element.37), channel_id=1, source_target_pairs={{1,0},{2,1},{3,2},{4,3},{5,4},{6,5},{7,6},{8,7},{9,8},{10,9},{11,1... | collective-permute-start | bytes 49160 | tf_op jit(solution)/shard_map/ppermute | solution.py:354
  46.9 0.0 collective-permute-done.5.halo_x1
  46.9 3.2 %collective-permute-done.7.halo_y1 = f32[16,256]{1,0:T(8,128)S(1)} collective-permute-done((f32[16,256]{1,0:T(8,128)S(1)}, f32[16,256]{1,0:T(8,128)S(1)}, u32[]{:S(2)}, u32[]{:S(2)}) %collective-permute-start.7) | collective-permute-done | bytes 16416 | tf_op jit(solution)/shard_map/ppermute | solution.py:354
  50.1 1.6 %update.1 = (f32[16,16,256]{2,1,0:T(8,128)}, f32[3,16,16,256]{3,2,1,0:T(8,128)}, f32[16,16,256]{2,1,0:T(8,128)}, f32[256,128]{1,0:T(8,128)S(1)}) custom-call(f32[16,16,256]{2,1,0:T(8,128)S(1)} %copy-done.3, f32[3,16,16,256]{3,2,1,0:T(8,128)S(1)} %copy-done.2, f32[16,16,256]{2,1,0:T(8,128)S(1)} %copy-done.1, f32[5,16,16,256]{3,2,1,0:T(8,128)S(1)} %bitcast.7, ...), custom_call_target="tpu_custom_call" | custom-call | tf_op jit(solution)/shard_map/update/pallas_call | solution.py:388
  51.6 44.3 %all_to_all.9 = f32[256,1,128]{2,1,0:T(1,128)S(1)} all-to-all(f32[256,1,128]{2,1,0:T(1,128)S(1)} %bitcast.8), channel_id=1, replica_groups=mesh['gx'=8,'gy'=32] {'gx','gy'}, dimensions={0} | all-to-all | bytes 262144 | tf_op jit(solution)/shard_map/all_to_all | solution.py:399
  96.0 0.9 reduce_max.9
  (14 shorter events, 0.0 us)
Async XLA Ops:
  1.3 0.9 copy-start.4
  2.2 0.9 copy-start.5
  3.1 0.8 copy-start.6
  3.8 0.8 copy-start.7
  4.6 45.4 %copy-start.1 = (f32[16,16,256]{2,1,0:T(8,128)S(1)}, f32[16,16,256]{2,1,0:T(8,128)}, u32[]{:S(2)}) copy-start(f32[16,16,256]{2,1,0:T(8,128)} %energy.3) | copy-start | bytes 786436
  4.6 45.4 %copy-start.3 = (f32[16,16,256]{2,1,0:T(8,128)S(1)}, f32[16,16,256]{2,1,0:T(8,128)}, u32[]{:S(2)}) copy-start(f32[16,16,256]{2,1,0:T(8,128)} %density.1) | copy-start | bytes 786436
  8.6 24.9 %collective-permute-start = (f32[8,512]{1,0:T(8,128)S(1)}, f32[8,512]{1,0:T(8,128)S(1)}, u32[]{:S(2)}, u32[]{:S(2)}) collective-permute-start(f32[8,512]{1,0:T(8,128)S(1)} %get-tuple-element.27), channel_id=1, source_target_pairs={{0,32},{32,64},{64,96},{96,128},{128,160},{160,192},{192,224},{1,3... | collective-permute-start | bytes 49160 | tf_op jit(solution)/shard_map/ppermute | solution.py:353
  13.5 19.9 %collective-permute-start.1 = (f32[8,512]{1,0:T(8,128)S(1)}, f32[8,512]{1,0:T(8,128)S(1)}, u32[]{:S(2)}, u32[]{:S(2)}) collective-permute-start(f32[8,512]{1,0:T(8,128)S(1)} %get-tuple-element.28), channel_id=1, source_target_pairs={{32,0},{64,32},{96,64},{128,96},{160,128},{192,160},{224,192},{33,... | collective-permute-start | bytes 49160 | tf_op jit(solution)/shard_map/ppermute | solution.py:354
  15.5 18.0 %collective-permute-start.2 = (f32[8,512]{1,0:T(8,128)S(1)}, f32[8,512]{1,0:T(8,128)S(1)}, u32[]{:S(2)}, u32[]{:S(2)}) collective-permute-start(f32[8,512]{1,0:T(8,128)S(1)} %get-tuple-element.29), channel_id=1, source_target_pairs={{0,1},{1,2},{2,3},{3,4},{4,5},{5,6},{6,7},{7,8},{8,9},{9,10},{10,1... | collective-permute-start | bytes 49160 | tf_op jit(solution)/shard_map/ppermute | solution.py:353
  18.6 14.9 %collective-permute-start.3 = (f32[8,512]{1,0:T(8,128)S(1)}, f32[8,512]{1,0:T(8,128)S(1)}, u32[]{:S(2)}, u32[]{:S(2)}) collective-permute-start(f32[8,512]{1,0:T(8,128)S(1)} %get-tuple-element.30), channel_id=1, source_target_pairs={{1,0},{2,1},{3,2},{4,3},{5,4},{6,5},{7,6},{8,7},{9,8},{10,9},{11,1... | collective-permute-start | bytes 49160 | tf_op jit(solution)/shard_map/ppermute | solution.py:354
  33.5 1.0 copy-start
  34.4 15.6 %copy-start.2 = (f32[3,16,16,256]{3,2,1,0:T(8,128)S(1)}, f32[3,16,16,256]{3,2,1,0:T(8,128)}, u32[]{:S(2)}) copy-start(f32[3,16,16,256]{3,2,1,0:T(8,128)} %momentum.1) | copy-start | bytes 2359300
  35.4 11.4 %collective-permute-start.4 = (f32[16,256]{1,0:T(8,128)S(1)}, f32[16,256]{1,0:T(8,128)S(1)}, u32[]{:S(2)}, u32[]{:S(2)}) collective-permute-start(f32[16,256]{1,0:T(8,128)S(1)} %get-tuple-element.34), channel_id=1, source_target_pairs={{0,32},{32,64},{64,96},{96,128},{128,160},{160,192},{192,224},{1,3... | collective-permute-start | bytes 49160 | tf_op jit(solution)/shard_map/ppermute | solution.py:353
  39.4 7.5 %collective-permute-start.5 = (f32[16,256]{1,0:T(8,128)S(1)}, f32[16,256]{1,0:T(8,128)S(1)}, u32[]{:S(2)}, u32[]{:S(2)}) collective-permute-start(f32[16,256]{1,0:T(8,128)S(1)} %get-tuple-element.35), channel_id=1, source_target_pairs={{32,0},{64,32},{96,64},{128,96},{160,128},{192,160},{224,192},{33,... | collective-permute-start | bytes 49160 | tf_op jit(solution)/shard_map/ppermute | solution.py:354
  41.3 5.6 %collective-permute-start.6 = (f32[16,256]{1,0:T(8,128)S(1)}, f32[16,256]{1,0:T(8,128)S(1)}, u32[]{:S(2)}, u32[]{:S(2)}) collective-permute-start(f32[16,256]{1,0:T(8,128)S(1)} %get-tuple-element.36), channel_id=1, source_target_pairs={{0,1},{1,2},{2,3},{3,4},{4,5},{5,6},{6,7},{7,8},{8,9},{9,10},{10,1... | collective-permute-start | bytes 49160 | tf_op jit(solution)/shard_map/ppermute | solution.py:353
  45.6 4.5 %collective-permute-start.7 = (f32[16,256]{1,0:T(8,128)S(1)}, f32[16,256]{1,0:T(8,128)S(1)}, u32[]{:S(2)}, u32[]{:S(2)}) collective-permute-start(f32[16,256]{1,0:T(8,128)S(1)} %get-tuple-element.37), channel_id=1, source_target_pairs={{1,0},{2,1},{3,2},{4,3},{5,4},{6,5},{7,6},{8,7},{9,8},{10,9},{11,1... | collective-permute-start | bytes 49160 | tf_op jit(solution)/shard_map/ppermute | solution.py:354

commit v3 on v2

--- a/solution.py
+++ b/solution.py
@@ -29,9 +29,9 @@
 
 
 def prep_kernel(
-    cells_x, cells_y, count, mass, temp, vel, cell,
-    out0, out1, out2, out3, stay,
-    mass_v, temp_v, vel_v, cell_v, pay, cx, cy, pos, compact, table_v, table_s, tiles, sems,
+    cells_x, cells_y, step, count, mass, temp, vel, cell, energy,
+    even, odd, stay, own, leaving, partial,
+    mass_v, temp_v, vel_v, cell_v, pay, cx, cy, pos, compact, table_v, table_s, tiles, acc, sems,
 ):
     fetches = [
         pltpu.make_async_copy(there, here, sems.at[i])
@@ -46,6 +46,7 @@
     chunks = mass.shape[0]
     anchor_x = lax.axis_index("gx") * cells_x
     anchor_y = lax.axis_index("gy") * cells_y
+    anchor_xf, anchor_yf = anchors(cells_x, cells_y)
     for b in range(chunks):
         lanes = slice(b * LANES, (b + 1) * LANES)
         cx[b : b + 1, :] = cell[0:1, lanes]
@@ -151,9 +152,59 @@
     for h in range(4):
         word = table_s[chunks - 1, h]
         tiles[h, ((word & 1023) + (word >> 18)) >> 7] = carry[h]
-    for h, out in enumerate((out0, out1, out2, out3)):
-        for t in range(out.shape[1] // LANES):
-            out[:, t * LANES : (t + 1) * LANES] = tiles[h, t]
+    width = 4 * LANES
+    buckets = [
+        jnp.concatenate([tiles[h, t] for t in range(width // LANES)], axis=1) for h in range(4)
+    ]
+    for h in range(4):
+        along = (buckets[h][6:7] - anchor_yf) if h < 2 else (buckets[h][5:6] - anchor_xf)
+        number = cells_y if h < 2 else cells_x
+        leaving[h] = one_field(buckets[h], along, number, 4)
+    for h in range(2):
+        own[h] = buckets[h]
+    columns = cells_x * cells_y
+    deposit_fields((4,), anchor_xf, anchor_yf, cells_y, step, stay, acc)
+    for x in range(cells_x):
+        rows = slice(x * cells_y, (x + 1) * cells_y)
+        partial[x] = energy[x] + (acc[rows] + acc[columns + x * cells_y : columns + (x + 1) * cells_y])
+    up = message(buckets[3], partial[:, cells_y - 1, :], leaving[0, -1:, :], leaving[1, -1:, :])
+    down = message(buckets[2], partial[:, 0, :], leaving[0, 0:1, :], leaving[1, 0:1, :])
+    send_pair("gy", even, odd, up, down)
+
+
+def message(bucket, plane, first, second):
+    half = plane.shape[0] // 2
+    rest = jnp.zeros((6, plane.shape[1]), F32)
+    return jnp.concatenate(
+        [bucket, plane[:half], plane[half:], jnp.concatenate([first, second, rest], axis=0)], axis=1
+    )
+
+
+def unpack(got, depth):
+    width = got.shape[1] - 3 * depth
+    plane = jnp.concatenate(
+        [got[:, width : width + depth], got[:, width + depth : width + 2 * depth]], axis=0
+    )
+    corner = got[:, width + 2 * depth :]
+    return got[:, :width], plane, corner[0:1], corner[1:2]
+
+
+def send_pair(axis, even, odd, up, down):
+    is_even = (lax.axis_index(axis) & 1) == 0
+    even[...] = jnp.where(is_even, up, down)
+    odd[...] = jnp.where(is_even, down, up)
+
+
+def receive_pair(axis, even, odd):
+    is_even = (lax.axis_index(axis) & 1) == 0
+    return jnp.where(is_even, odd[...], even[...]), jnp.where(is_even, even[...], odd[...])
+
+
+def anchors(cells_x, cells_y):
+    return (
+        (lax.axis_index("gx") * cells_x).astype(F32),
+        (lax.axis_index("gy") * cells_y).astype(F32),
+    )
 
 
 def source_rows(rows):
@@ -184,107 +235,140 @@
     return jnp.where(rows[7:8] == iota((depth, n), 0).astype(F32), 1.0, 0.0).astype(BF16)
 
 
-def deposit_kernel(cells_x, cells_y, step, stay, state, where_to, dep, acc):
+def deposit_fields(fields, anchor_x, anchor_y, cells_y, step, stay, acc):
     total = stay.shape[1]
-    columns = cells_x * cells_y
-    depth = dep.shape[2]
-    anchor_x = (lax.axis_index("gx") * cells_x).astype(F32)
-    anchor_y = (lax.axis_index("gy") * cells_y).astype(F32)
+    columns = acc.shape[0] // (2 * len(fields))
+    depth = acc.shape[1]
     acc[...] = jnp.zeros(acc.shape, F32)
 
     def one(k, carry):
         rows = stay[:, pl.ds(pl.multiple_of(k * step, step), step)]
         column = (rows[5:6] - anchor_x) * cells_y + (rows[6:7] - anchor_y)
-        left = spread(column, source_rows(rows), columns)
+        sources = source_rows(rows)
+        left = spread(
+            column, [sources[f] for f in fields] + [sources[5 + f] for f in fields], columns
+        )
         acc[...] += lax.dot_general(
             left, depth_onehot(rows, depth), TRANSPOSED, preferred_element_type=F32
         )
         return carry
 
     lax.fori_loop(0, total // step, one, 0)
-    for f in range(5):
-        dep[f] = (
-            acc[f * columns : (f + 1) * columns, :] + acc[(5 + f) * columns : (6 + f) * columns, :]
-        )
-    state[:, :total] = stay[0:5, :]
-    where_to[:, :total] = stay[5:8, :].astype(I32)
-
-
-def arrive_kernel(
-    cells_x, cells_y, in0, in1, in2, in3, energy, dep4, state_in, where_in,
-    planes, face_x0, face_x1, face_y0, face_y1, state, where_to,
+
+
+def one_field(rows, along, number, f):
+    sources = source_rows(rows)
+    left = spread(along, [sources[f], sources[5 + f]], number)
+    got = lax.dot_general(left, depth_onehot(rows, 256), TRANSPOSED, preferred_element_type=F32)
+    return got[:number] + got[number:]
+
+
+def deposit_kernel(cells_x, cells_y, step, fields, with_tables, *refs):
+    columns = cells_x * cells_y
+    if with_tables:
+        stay, dep, state, where_to, acc = refs
+        total = stay.shape[1]
+        state[:, :total] = stay[0:5, :]
+        where_to[:, :total] = stay[5:8, :].astype(I32)
+    else:
+        stay, _, dep, acc = refs
+    deposit_fields(fields, *anchors(cells_x, cells_y), cells_y, step, stay, acc)
+    n = len(fields)
+    for f in range(n):
+        for x in range(cells_x):
+            high = slice((f * cells_x + x) * cells_y, (f * cells_x + x + 1) * cells_y)
+            low = slice(n * columns + high.start, n * columns + high.stop)
+            dep[f, x] = acc[high, :] + acc[low, :]
+
+
+def arrivals(rows, along, number, depth):
+    left = spread(along, source_rows(rows), number)
+    got = lax.dot_general(left, depth_onehot(rows, depth), TRANSPOSED, preferred_element_type=F32)
+    return [
+        got[f * number : (f + 1) * number] + got[(5 + f) * number : (6 + f) * number]
+        for f in range(5)
+    ]
+
+
+def relay_kernel(cells_x, cells_y, in_even, in_odd, partial, own, leaving, even, odd, planes, halo):
+    depth = partial.shape[2]
+    anchor_x, _ = anchors(cells_x, cells_y)
+    got = receive_pair("gy", in_even, in_odd)
+    parts = [unpack(g, depth) for g in got]
+    for q, (rows, plane, _, _) in enumerate(parts):
+        for f, value in enumerate(arrivals(rows, rows[5:6] - anchor_x, cells_x, depth)):
+            planes[q, f] = value
+        halo[q] = plane + leaving[2 + q]
+    row = iota((cells_y, depth), 0)
+
+    def side(x):
+        value = partial[x] + jnp.where(row == 0, planes[0, 4, x : x + 1, :], 0.0)
+        return value + jnp.where(row == cells_y - 1, planes[1, 4, x : x + 1, :], 0.0)
+
+    up = message(own[1], side(cells_x - 1), parts[0][3], parts[1][3])
+    down = message(own[0], side(0), parts[0][2], parts[1][2])
+    send_pair("gx", even, odd, up, down)
+
+
+def update_kernel(
+    cells_x, cells_y, y_even, y_odd, x_even, x_odd, density, momentum, partial, dep01, dep23,
+    planes_y, halo_y, leaving, state_in, where_in,
+    rho_out, impulse, energy_out, fastest, state, where_to, pressure, planes_x,
 ):
-    depth = planes.shape[3]
-    anchor_x = (lax.axis_index("gx") * cells_x).astype(F32)
-    anchor_y = (lax.axis_index("gy") * cells_y).astype(F32)
-    capacity = in0.shape[1]
-    for q, table in enumerate((in0, in1, in2, in3)):
-        rows = table[...]
-        along = (rows[6:7] - anchor_y) if q < 2 else (rows[5:6] - anchor_x)
-        number = cells_y if q < 2 else cells_x
-        left = spread(along, source_rows(rows), number)
-        got = lax.dot_general(left, depth_onehot(rows, depth), TRANSPOSED, preferred_element_type=F32)
-        for f in range(5):
-            planes[q, f] = (
-                got[f * number : (f + 1) * number] + got[(5 + f) * number : (6 + f) * number]
-            )
-        lanes = slice(q * capacity, (q + 1) * capacity)
-        state[:, lanes] = rows[0:5]
-        where_to[:, lanes] = rows[5:8].astype(I32)
-    scale = ADIABATIC_INDEX - 1.0
-    row = iota((cells_y, depth), 0)
-    for q, face, x in ((0, face_x0, 0), (1, face_x1, cells_x - 1)):
-        plane = energy[x] + dep4[x] + planes[q, 4]
-        plane = plane + jnp.where(row == 0, planes[2, 4, x : x + 1, :], 0.0)
-        plane = plane + jnp.where(row == cells_y - 1, planes[3, 4, x : x + 1, :], 0.0)
-        face[...] = scale * plane
-    row = iota((cells_x, depth), 0)
-    for q, face, y in ((2, face_y0, 0), (3, face_y1, cells_y - 1)):
-        plane = energy[:, y, :] + dep4[:, y, :] + planes[q, 4]
-        plane = plane + jnp.where(row == 0, planes[0, 4, y : y + 1, :], 0.0)
-        plane = plane + jnp.where(row == cells_x - 1, planes[1, 4, y : y + 1, :], 0.0)
-        face[...] = scale * plane
-
-
-def update_kernel(
-    cells_x, cells_y, density, momentum, energy, dep, planes, halo_x0, halo_x1, halo_y0, halo_y1,
-    rho_out, impulse, energy_out, fastest, pressure,
-):
-    depth = energy.shape[2]
+    depth = partial.shape[2]
+    _, anchor_y = anchors(cells_x, cells_y)
     scale = ADIABATIC_INDEX - 1.0
     shape = (cells_y, depth)
     row = iota(shape, 0)
     lane = iota(shape, 1)
+    parts = [unpack(g, depth) for g in receive_pair("gx", x_even, x_odd)]
+    for q, (rows, plane, _, _) in enumerate(parts):
+        for f, value in enumerate(arrivals(rows, rows[6:7] - anchor_y, cells_y, depth)):
+            planes_x[q, f] = value
+        pressure[q * (cells_x + 1)] = scale * (plane + leaving[q])
+    row_x = iota((cells_x, depth), 0)
+    halos = []
+    for q in range(2):
+        value = halo_y[q] + jnp.where(row_x == 0, parts[0][2 + q], 0.0)
+        halos.append(scale * (value + jnp.where(row_x == cells_x - 1, parts[1][2 + q], 0.0)))
+    tables = [parts[0][0], parts[1][0]] + [
+        unpack(g, depth)[0] for g in receive_pair("gy", y_even, y_odd)
+    ]
+    for q, rows in enumerate(tables):
+        lanes = slice(q * rows.shape[1], (q + 1) * rows.shape[1])
+        state[:, lanes] = rows[0:5]
+        where_to[:, lanes] = rows[5:8].astype(I32)
 
     def with_planes(f, x, value):
         if x == 0:
-            value = value + planes[0, f]
+            value = value + planes_x[0, f]
         if x == cells_x - 1:
-            value = value + planes[1, f]
-        value = value + jnp.where(row == 0, planes[2, f, x : x + 1, :], 0.0)
-        return value + jnp.where(row == cells_y - 1, planes[3, f, x : x + 1, :], 0.0)
-
-    pressure[0] = halo_x0[...]
-    pressure[cells_x + 1] = halo_x1[...]
+            value = value + planes_x[1, f]
+        value = value + jnp.where(row == 0, planes_y[0, f, x : x + 1, :], 0.0)
+        return value + jnp.where(row == cells_y - 1, planes_y[1, f, x : x + 1, :], 0.0)
+
     for x in range(cells_x):
-        value = with_planes(4, x, energy[x] + dep[4, x])
+        value = with_planes(4, x, partial[x])
         energy_out[x] = value
         pressure[x + 1] = scale * value
     top = jnp.zeros(shape, F32)
     for x in range(cells_x):
         here = pressure[x + 1]
         grad_x = 0.5 * (pressure[x + 2] - pressure[x])
-        after = jnp.where(row == cells_y - 1, halo_y1[x : x + 1, :], pltpu.roll(here, cells_y - 1, 0))
-        before = jnp.where(row == 0, halo_y0[x : x + 1, :], pltpu.roll(here, 1, 0))
+        after = jnp.where(
+            row == cells_y - 1, halos[1][x : x + 1, :], pltpu.roll(here, cells_y - 1, 0)
+        )
+        before = jnp.where(row == 0, halos[0][x : x + 1, :], pltpu.roll(here, 1, 0))
         grad_y = 0.5 * (after - before)
         after = jnp.where(lane == depth - 1, 0.0, pltpu.roll(here, depth - 1, 1))
         before = jnp.where(lane == 0, 0.0, pltpu.roll(here, 1, 1))
         grad_z = 0.5 * (after - before)
-        rho = with_planes(0, x, density[x] + dep[0, x])
+        rho = with_planes(0, x, density[x] + dep01[0, x])
         rho_out[x] = rho
         largest = jnp.zeros(shape, F32)
+        deposits = (dep01[1, x], dep23[0, x], dep23[1, x])
         for k, grad in enumerate((grad_x, grad_y, grad_z)):
-            value = with_planes(1 + k, x, momentum[k, x] + dep[1 + k, x]) - KICK * grad
+            value = with_planes(1 + k, x, momentum[k, x] + deposits[k]) - KICK * grad
             impulse[k, x] = value
             largest = jnp.maximum(largest, jnp.abs(value))
         wave = largest / rho + jnp.sqrt(ADIABATIC_INDEX * here / rho)
@@ -308,6 +392,14 @@
     )
 
 
+def swap(axis, even, odd):
+    size = lax.axis_size(axis)
+    pairs = lambda first: [
+        p for i in range(first, size - 1, 2) for p in ((i, i + 1), (i + 1, i))
+    ]
+    return lax.ppermute(even, axis, pairs(0)), lax.ppermute(odd, axis, pairs(1))
+
+
 def on_device(
     density, momentum, energy, parcel_mass, droplet_velocity, parcel_temp, parcel_cell, parcel_count
 ):
@@ -315,12 +407,21 @@
     rows = parcel_mass.shape[0]
     capacity = rows // 16
     chunks = rows // LANES
+    columns = cells_x * cells_y
+    step = min(1024, rows)
     sds = jax.ShapeDtypeStruct
     whole = pl.BlockSpec(memory_space=VMEM)
-    bucket = sds((8, capacity), F32)
-    *buckets, stay = call(
-        functools.partial(prep_kernel, cells_x, cells_y),
-        (bucket, bucket, bucket, bucket, sds((8, rows), F32)),
+    parcels = sds((8, capacity + 3 * depth), F32)
+    even, odd, stay, own, leaving, partial = call(
+        functools.partial(prep_kernel, cells_x, cells_y, step),
+        (
+            parcels,
+            parcels,
+            sds((8, rows), F32),
+            sds((2, 8, capacity), F32),
+            sds((4, cells_x, depth), F32),
+            sds(energy.shape, F32),
+        ),
         scratch=(
             VMEM((chunks, LANES), F32),
             VMEM((chunks, LANES), F32),
@@ -334,9 +435,12 @@
             VMEM((chunks, LANES), I32),
             pltpu.SMEM((chunks, LANES), I32),
             VMEM((4, capacity // LANES + 1, 8, LANES), F32),
+            VMEM((2 * columns, depth), F32),
             pltpu.SemaphoreType.DMA((5,)),
         ),
-        in_specs=[pl.BlockSpec(memory_space=pltpu.SMEM)] + [pl.BlockSpec(memory_space=pltpu.HBM)] * 4,
+        in_specs=[pl.BlockSpec(memory_space=pltpu.SMEM)]
+        + [pl.BlockSpec(memory_space=pltpu.HBM)] * 4
+        + [whole],
         name="prep",
     )(
         parcel_count,
@@ -344,58 +448,59 @@
         parcel_temp.reshape(chunks, LANES),
         droplet_velocity,
         parcel_cell,
-    )
-
-    def exchange(to_low_x, to_high_x, to_low_y, to_high_y):
-        got = []
-        for axis, down, up in (("gx", to_low_x, to_high_x), ("gy", to_low_y, to_high_y)):
-            ends = lax.axis_size(axis) - 1
-            got.append(lax.ppermute(up, axis, [(i, i + 1) for i in range(ends)]))
-            got.append(lax.ppermute(down, axis, [(i + 1, i) for i in range(ends)]))
-        return got
-
-    arrived = exchange(*buckets)
+        energy,
+    )
+    y_even, y_odd = swap("gy", even, odd)
     slots = rows + 4 * capacity
-    state, where_to, dep = call(
-        functools.partial(deposit_kernel, cells_x, cells_y, min(1024, rows)),
-        (sds((5, slots), F32), sds((3, slots), I32), sds((5, cells_x * cells_y, depth), F32)),
-        scratch=(VMEM((10 * cells_x * cells_y, depth), F32),),
-        name="deposit",
+    two = sds((2, cells_x, cells_y, depth), F32)
+    sums = (VMEM((4 * columns, depth), F32),)
+    dep01, state, where_to = call(
+        functools.partial(deposit_kernel, cells_x, cells_y, step, (0, 1), True),
+        (two, sds((5, slots), F32), sds((3, slots), I32)),
+        scratch=sums,
+        name="deposit01",
     )(stay)
-    dep = dep.reshape(5, cells_x, cells_y, depth)
-    face = lambda n: sds((n, depth), F32)
-    planes, *faces, state, where_to = call(
-        functools.partial(arrive_kernel, cells_x, cells_y),
-        (
-            sds((4, 5, cells_x, depth), F32),
-            face(cells_y), face(cells_y), face(cells_x), face(cells_x),
-            sds(state.shape, F32),
-            sds(where_to.shape, I32),
-        ),
-        in_specs=[whole] * 5
-        + [pl.BlockSpec((None, cells_x, cells_y, depth), lambda i: (4, 0, 0, 0))]
-        + [pl.BlockSpec(memory_space=pl.ANY)] * 2,
-        out_specs=(whole,) * 5
-        + (
-            pl.BlockSpec((5, 4 * capacity), lambda i: (0, rows // (4 * capacity))),
-            pl.BlockSpec((3, 4 * capacity), lambda i: (0, rows // (4 * capacity))),
-        ),
-        aliases={6: 5, 7: 6},
-        name="arrive",
-        grid=(1,),
-    )(*arrived, energy, dep, state, where_to)
-    halos = exchange(*faces)
-    rho, impulse, energy_out, top = call(
+    even, odd, planes_y, halo_y = call(
+        functools.partial(relay_kernel, cells_x, cells_y),
+        (parcels, parcels, sds((2, 5, cells_x, depth), F32), sds((2, cells_x, depth), F32)),
+        name="relay",
+    )(y_even, y_odd, partial, own, leaving)
+    x_even, x_odd = swap("gx", even, odd)
+    (dep23,) = call(
+        functools.partial(deposit_kernel, cells_x, cells_y, step, (2, 3), False),
+        (two,),
+        scratch=sums,
+        in_specs=[whole, pl.BlockSpec(memory_space=pl.ANY)],
+        name="deposit23",
+    )(stay, halo_y)
+    last = rows // (4 * capacity)
+    rho, impulse, energy_out, top, state, where_to = call(
         functools.partial(update_kernel, cells_x, cells_y),
         (
             sds(density.shape, F32),
             sds(momentum.shape, F32),
             sds(energy.shape, F32),
             sds((lax.axis_size(("gx", "gy")), LANES), F32),
-        ),
-        scratch=(VMEM((cells_x + 2, cells_y, depth), F32),),
+            sds(state.shape, F32),
+            sds(where_to.shape, I32),
+        ),
+        scratch=(
+            VMEM((cells_x + 2, cells_y, depth), F32),
+            VMEM((2, 5, cells_y, depth), F32),
+        ),
+        in_specs=[whole] * 12 + [pl.BlockSpec(memory_space=pl.ANY)] * 2,
+        out_specs=(whole,) * 4
+        + (
+            pl.BlockSpec((5, 4 * capacity), lambda i: (0, last)),
+            pl.BlockSpec((3, 4 * capacity), lambda i: (0, last)),
+        ),
+        aliases={12: 4, 13: 5},
+        grid=(1,),
         name="update",
-    )(density, momentum, energy, dep, planes, *halos)
+    )(
+        y_even, y_odd, x_even, x_odd, density, momentum, partial, dep01, dep23,
+        planes_y, halo_y, leaving, state, where_to,
+    )
     fastest = jnp.max(lax.all_to_all(top, ("gx", "gy"), 0, 0, tiled=True))
     return rho, impulse, energy_out, state, where_to, COURANT / fastest
 

time: 99.2 us -> 74.2 us (0.75)
  starting transfers between devices: 22.6 us -> 8.54 us
  blocking collectives: 44.3 us -> 33.3 us
  Pallas kernels: 20.1 us -> 22.9 us
  waiting for transfers between devices: 3.17 us -> 0.74 us
    ppermute x8 -> x4, starting transfers between devices: 22.6 us -> 8.54 us  [the longest x2 5.98 us: swap(): lax.ppermute(even, axis, pairs(0))]
    all_to_all x1, blocking collectives: 44.3 us -> 33.3 us  [on_device(): fastest = jnp.max(lax.all_to_all(top, ('gx', 'gy'), 0, 0, tiled=True))]
    pallas_call x3 -> x4, Pallas kernels: 18.6 us -> 21 us  [the longest x1 8.3 us: on_device(): call(functools.partial(prep_kernel, cells_x, cells_y, step), (parcels, pa...]
    ppermute x8 -> x4, waiting for transfers between devices: 3.17 us -> 0.74 us  [the longest x2 0.74 us: swap(): lax.ppermute(even, axis, pairs(0))]
    unnamed x16 -> x14, local copies, waits for them, and re-layouts: 4.27 us -> 4.28 us
  transfers between devices with their start and end apart: 8 -> 4, of which waited for: 1 -> 1; matrix products, arithmetic and copies ran while one was open for 0% -> 0% of each run, Pallas kernels for 14% -> 17%
where the time goes in v3:
time: 74.2 us; the launch traced here: 73.8 us
  blocking collectives  33.3 us (45%)
  Pallas kernels  22.9 us (31%)
  starting transfers between devices  8.54 us (12%)
  local copies, waits for them, and re-layouts  4.28 us (6%)
  between operations  3.21 us (4%)
  other arithmetic  0.87 us (1%)
    all_to_all x1, blocking collectives, on_device(): fastest = jnp.max(lax.all_to_all(top, ('gx', 'gy'), 0, 0, tiled=True))  33.3 us
    pallas_call x1, Pallas kernels, on_device(): call(functools.partial(prep_kernel, cells_x, cells_y, step), (parcels, pa...  8.3 us
    pallas_call x1, Pallas kernels, on_device(): call(functools.partial(deposit_kernel, cells_x, cells_y, step, (0, 1), Tr...  6.22 us
    pallas_call x1, Pallas kernels, on_device(): call(functools.partial(deposit_kernel, cells_x, cells_y, step, (2, 3), Fa...  6.17 us
    ppermute x2, starting transfers between devices, swap(): lax.ppermute(even, axis, pairs(0))  5.98 us
    unnamed x14, local copies, waits for them, and re-layouts  4.28 us
    ppermute x2, starting transfers between devices, swap(): lax.ppermute(odd, axis, pairs(1))  2.56 us
    pallas_call x1, Pallas kernels, on_device(): call(functools.partial(update_kernel, cells_x, cells_y), (sds(density.sha...  1.82 us
  transfers between devices with their start and end apart: 4, of which 1 were waited for; matrix products, arithmetic and copies ran while one was open for 0% of the time, Pallas kernels for 17%

profile of v3, /device:TPU:1, one launch (start us, length us, event | category | flops | bytes accessed | tf_op | source)
XLA Modules:
  0.0 73.8 jit_solution(985322511968041915)
XLA Ops:
  1.3 0.0 copy-start.2
  1.3 0.9 %copy-done.2 = f32[16,16,256]{2,1,0:T(8,128)S(1)} copy-done((f32[16,16,256]{2,1,0:T(8,128)S(1)}, f32[16,16,256]{2,1,0:T(8,128)}, u32[]{:S(2)}) %copy-start.2) | copy-done | bytes 262168
  2.2 0.9 %copy-done.3 = f32[3,8192]{1,0:T(4,128)S(1)} copy-done((f32[3,8192]{1,0:T(4,128)S(1)}, f32[3,8192]{1,0:T(4,128)}, u32[]{:S(2)}) %copy-start.3) | copy-done | bytes 98328
  3.1 0.9 %copy-done.4 = s32[3,8192]{1,0:T(4,128)S(1)} copy-done((s32[3,8192]{1,0:T(4,128)S(1)}, s32[3,8192]{1,0:T(4,128)}, u32[]{:S(2)}) %copy-start.4) | copy-done | bytes 98328
  4.0 0.8 %copy-done.5 = f32[8192]{0:T(1024)S(1)} copy-done((f32[8192]{0:T(1024)S(1)}, f32[8192]{0:T(1024)}, u32[]{:S(2)}) %copy-start.5) | copy-done | bytes 32792
  4.8 0.8 %copy-done.6 = f32[8192]{0:T(1024)S(1)} copy-done((f32[8192]{0:T(1024)S(1)}, f32[8192]{0:T(1024)}, u32[]{:S(2)}) %copy-start.6) | copy-done | bytes 32792
  5.6 8.3 %prep.1 = (f32[8,1280]{1,0:T(8,128)S(1)}, f32[8,1280]{1,0:T(8,128)S(1)}, f32[8,8192]{1,0:T(8,128)S(1)}, f32[2,8,512]{2,1,0:T(8,128)S(1)}, f32[4,16,256]{2,1,0:T(8,128)S(1)}, /*index=5*/f32[16,16,256]{2,1,0:T(8,128)S(1)}) custom-call(s32[1]{0:T(128)S(6)} %copy.19.count, f32[64,128]{1,0:T(8,128)S(1)} %bitcast.6, f32[64,128]{1,0:T(8,128)S(1)} %bitcast.7, ...), custom_call_target="tpu_custom_call" | custom-call | tf_op jit(solution)/shard_map/prep/pallas_call | solution.py:415
  13.9 0.0 copy-start
  13.9 2.1 %collective-permute-start = (f32[8,1280]{1,0:T(8,128)S(1)}, f32[8,1280]{1,0:T(8,128)S(1)}, u32[]{:S(2)}, u32[]{:S(2)}) collective-permute-start(f32[8,1280]{1,0:T(8,128)S(1)} %get-tuple-element.25), channel_id=1, source_target_pairs={{0,1},{1,0},{2,3},{3,2},{4,5},{5,4},{6,7},{7,6},{8,9},{9,8},{10,11... | collective-permute-start | bytes 122888 | tf_op jit(solution)/shard_map/ppermute | solution.py:400
  16.0 0.7 collective-permute-start.1
  16.7 0.7 collective-permute-done.in_even.y_even
  17.4 0.0 collective-permute-done.1.in_odd.y_odd
  17.4 0.4 relay.1
  17.8 3.9 %collective-permute-start.2 = (f32[8,1280]{1,0:T(8,128)S(1)}, f32[8,1280]{1,0:T(8,128)S(1)}, u32[]{:S(2)}, u32[]{:S(2)}) collective-permute-start(f32[8,1280]{1,0:T(8,128)S(1)} %get-tuple-element.30), channel_id=1, source_target_pairs={{0,32},{32,0},{64,96},{96,64},{128,160},{160,128},{192,224},{224,1... | collective-permute-start | bytes 122888 | tf_op jit(solution)/shard_map/ppermute | solution.py:400
  21.6 1.9 %collective-permute-start.3 = (f32[8,1280]{1,0:T(8,128)S(1)}, f32[8,1280]{1,0:T(8,128)S(1)}, u32[]{:S(2)}, u32[]{:S(2)}) collective-permute-start(f32[8,1280]{1,0:T(8,128)S(1)} %get-tuple-element.31), channel_id=1, source_target_pairs={{32,64},{64,32},{96,128},{128,96},{160,192},{192,160},{33,65},{65,... | collective-permute-start | bytes 122888 | tf_op jit(solution)/shard_map/ppermute | solution.py:400
  23.5 6.2 %deposit01.1 = (f32[2,16,16,256]{3,2,1,0:T(8,128)S(1)}, f32[5,10240]{1,0:T(8,128)}, s32[3,10240]{1,0:T(4,128)}) custom-call(f32[8,8192]{1,0:T(8,128)S(1)} %get-tuple-element.32.refs_0_), custom_call_target="tpu_custom_call" | custom-call | tf_op jit(solution)/shard_map/deposit01/pallas_call | solution.py:457
  29.8 0.0 copy-start.1
  29.8 6.2 %deposit23.1.dep23 = f32[2,16,16,256]{3,2,1,0:T(8,128)S(1)} custom-call(f32[8,8192]{1,0:T(8,128)S(1)} %get-tuple-element.32.refs_0_, f32[2,16,256]{2,1,0:T(8,128)S(1)} %get-tuple-element.34.refs_1_.halo_y), custom_call_target="tpu_custom_call" | custom-call | tf_op jit(solution)/shard_map/deposit23/pallas_call | solution.py:469
  36.0 0.0 collective-permute-done.2.x_even
  36.0 0.0 collective-permute-done.3.x_odd
  36.0 0.0 copy-done
  36.0 1.8 %update.1 = (f32[16,16,256]{2,1,0:T(8,128)}, f32[3,16,16,256]{3,2,1,0:T(8,128)}, f32[16,16,256]{2,1,0:T(8,128)}, f32[256,128]{1,0:T(8,128)S(1)}, f32[5,10240]{1,0:T(8,128)}, /*index=5*/s32[3,10240]{1,0:T(4,128)}) custom-call(f32[8,1280]{1,0:T(8,128)S(1)} %collective-permute-done.in_even.y_even, ...), custom_call_target="tpu_custom_call", output_to_operand_aliasing={{4}: (12, {}), {5}: (13, {})} | custom-call | tf_op jit(solution)/shard_map/update/pallas_call | solution.py:477
  37.8 33.3 %all_to_all.9 = f32[256,1,128]{2,1,0:T(1,128)S(1)} all-to-all(f32[256,1,128]{2,1,0:T(1,128)S(1)} %bitcast.5), channel_id=1, replica_groups=mesh['gx'=8,'gy'=32] {'gx','gy'}, dimensions={0} | all-to-all | bytes 262144 | tf_op jit(solution)/shard_map/all_to_all | solution.py:504
  71.1 0.9 %reduce_max.9 = f32[]{:T(128)} reduce(f32[256,1,128]{2,1,0:T(1,128)S(1)} %all_to_all.9, f32[]{:T(128)} %constant.1.clone.1), dimensions={0,1,2}, to_apply=%region_0.0 | reduce | flops 32767 | bytes 131080 | tf_op jit(solution)/shard_map/reduce_max | solution.py:504
  (5 shorter events, 0.0 us)
Async XLA Ops:
  1.3 1.0 %copy-start.2 = (f32[16,16,256]{2,1,0:T(8,128)S(1)}, f32[16,16,256]{2,1,0:T(8,128)}, u32[]{:S(2)}) copy-start(f32[16,16,256]{2,1,0:T(8,128)} %energy.1) | copy-start | bytes 786436
  2.2 0.9 %copy-start.3 = (f32[3,8192]{1,0:T(4,128)S(1)}, f32[3,8192]{1,0:T(4,128)}, u32[]{:S(2)}) copy-start(f32[3,8192]{1,0:T(4,128)} %vel.1) | copy-start | bytes 294916
  3.1 0.9 %copy-start.4 = (s32[3,8192]{1,0:T(4,128)S(1)}, s32[3,8192]{1,0:T(4,128)}, u32[]{:S(2)}) copy-start(s32[3,8192]{1,0:T(4,128)} %cell.1) | copy-start | bytes 294916
  4.0 0.8 %copy-start.5 = (f32[8192]{0:T(1024)S(1)}, f32[8192]{0:T(1024)}, u32[]{:S(2)}) copy-start(f32[8192]{0:T(1024)} %param.11) | copy-start | bytes 98308
  4.8 0.8 %copy-start.6 = (f32[8192]{0:T(1024)S(1)}, f32[8192]{0:T(1024)}, u32[]{:S(2)}) copy-start(f32[8192]{0:T(1024)} %param.13) | copy-start | bytes 98308
  13.9 22.1 %copy-start = (f32[3,16,16,256]{3,2,1,0:T(8,128)S(1)}, f32[3,16,16,256]{3,2,1,0:T(8,128)}, u32[]{:S(2)}) copy-start(f32[3,16,16,256]{3,2,1,0:T(8,128)} %momentum.1) | copy-start | bytes 2359300
  13.9 3.5 %collective-permute-start = (f32[8,1280]{1,0:T(8,128)S(1)}, f32[8,1280]{1,0:T(8,128)S(1)}, u32[]{:S(2)}, u32[]{:S(2)}) collective-permute-start(f32[8,1280]{1,0:T(8,128)S(1)} %get-tuple-element.25), channel_id=1, source_target_pairs={{0,1},{1,0},{2,3},{3,2},{4,5},{5,4},{6,7},{7,6},{8,9},{9,8},{10,11... | collective-permute-start | bytes 122888 | tf_op jit(solution)/shard_map/ppermute | solution.py:400
  16.0 1.4 %collective-permute-start.1 = (f32[8,1280]{1,0:T(8,128)S(1)}, f32[8,1280]{1,0:T(8,128)S(1)}, u32[]{:S(2)}, u32[]{:S(2)}) collective-permute-start(f32[8,1280]{1,0:T(8,128)S(1)} %get-tuple-element.26), channel_id=1, source_target_pairs={{1,2},{2,1},{3,4},{4,3},{5,6},{6,5},{7,8},{8,7},{9,10},{10,9},{11,... | collective-permute-start | bytes 122888 | tf_op jit(solution)/shard_map/ppermute | solution.py:400
  17.8 18.2 %collective-permute-start.2 = (f32[8,1280]{1,0:T(8,128)S(1)}, f32[8,1280]{1,0:T(8,128)S(1)}, u32[]{:S(2)}, u32[]{:S(2)}) collective-permute-start(f32[8,1280]{1,0:T(8,128)S(1)} %get-tuple-element.30), channel_id=1, source_target_pairs={{0,32},{32,0},{64,96},{96,64},{128,160},{160,128},{192,224},{224,1... | collective-permute-start | bytes 122888 | tf_op jit(solution)/shard_map/ppermute | solution.py:400
  21.6 14.3 %collective-permute-start.3 = (f32[8,1280]{1,0:T(8,128)S(1)}, f32[8,1280]{1,0:T(8,128)S(1)}, u32[]{:S(2)}, u32[]{:S(2)}) collective-permute-start(f32[8,1280]{1,0:T(8,128)S(1)} %get-tuple-element.31), channel_id=1, source_target_pairs={{32,64},{64,32},{96,128},{128,96},{160,192},{192,160},{33,65},{65,... | collective-permute-start | bytes 122888 | tf_op jit(solution)/shard_map/ppermute | solution.py:400
  29.8 6.2 %copy-start.1 = (f32[16,16,256]{2,1,0:T(8,128)S(1)}, f32[16,16,256]{2,1,0:T(8,128)}, u32[]{:S(2)}) copy-start(f32[16,16,256]{2,1,0:T(8,128)} %density.1) | copy-start | bytes 786436

commit v4 on v3

--- a/solution.py
+++ b/solution.py
@@ -159,7 +159,7 @@
     for h in range(4):
         along = (buckets[h][6:7] - anchor_yf) if h < 2 else (buckets[h][5:6] - anchor_xf)
         number = cells_y if h < 2 else cells_x
-        leaving[h] = one_field(buckets[h], along, number, 4)
+        leaving[h] = one_field(buckets[h], along, number, acc.shape[1], 4)
     for h in range(2):
         own[h] = buckets[h]
     columns = cells_x * cells_y
@@ -256,10 +256,10 @@
     lax.fori_loop(0, total // step, one, 0)
 
 
-def one_field(rows, along, number, f):
+def one_field(rows, along, number, depth, f):
     sources = source_rows(rows)
     left = spread(along, [sources[f], sources[5 + f]], number)
-    got = lax.dot_general(left, depth_onehot(rows, 256), TRANSPOSED, preferred_element_type=F32)
+    got = lax.dot_general(left, depth_onehot(rows, depth), TRANSPOSED, preferred_element_type=F32)
     return got[:number] + got[number:]
 
 
@@ -290,7 +290,9 @@
     ]
 
 
-def relay_kernel(cells_x, cells_y, in_even, in_odd, partial, own, leaving, even, odd, planes, halo):
+def relay_kernel(
+    cells_x, cells_y, in_even, in_odd, partial, own, leaving, _, even, odd, planes, halo
+):
     depth = partial.shape[2]
     anchor_x, _ = anchors(cells_x, cells_y)
     got = receive_pair("gy", in_even, in_odd)
@@ -376,7 +378,9 @@
     fastest[...] = jnp.broadcast_to(jnp.max(top, axis=(0, 1), keepdims=True), fastest.shape)
 
 
-def call(kernel, outs, scratch=(), out_specs=None, in_specs=None, aliases=None, name=None, **extra):
+def call(
+    kernel, outs, scratch=(), out_specs=None, in_specs=None, aliases=None, name=None, vmem=48, **extra
+):
     if in_specs is not None:
         extra["in_specs"] = in_specs
     if out_specs is not None:
@@ -386,7 +390,7 @@
         out_shape=outs,
         scratch_shapes=list(scratch),
         input_output_aliases=aliases or {},
-        compiler_params=pltpu.CompilerParams(vmem_limit_bytes=48 * 1024 * 1024),
+        compiler_params=pltpu.CompilerParams(vmem_limit_bytes=vmem * 1024 * 1024),
         name=name,
         **extra,
     )
@@ -463,8 +467,9 @@
     even, odd, planes_y, halo_y = call(
         functools.partial(relay_kernel, cells_x, cells_y),
         (parcels, parcels, sds((2, 5, cells_x, depth), F32), sds((2, cells_x, depth), F32)),
+        in_specs=[whole] * 5 + [pl.BlockSpec(memory_space=pl.ANY)],
         name="relay",
-    )(y_even, y_odd, partial, own, leaving)
+    )(y_even, y_odd, partial, own, leaving, dep01)
     x_even, x_odd = swap("gx", even, odd)
     (dep23,) = call(
         functools.partial(deposit_kernel, cells_x, cells_y, step, (2, 3), False),

time: 74.2 us -> 67.9 us (0.915)
  blocking collectives: 33.3 us -> 29 us
  starting transfers between devices: 8.54 us -> 7.25 us
    all_to_all x1, blocking collectives: 33.3 us -> 29 us  [on_device(): fastest = jnp.max(lax.all_to_all(top, ('gx', 'gy'), 0, 0, tiled=True))]
    ppermute x2, starting transfers between devices: 5.98 us -> 3.4 us  [swap(): lax.ppermute(even, axis, pairs(0))]
    ppermute x2, starting transfers between devices: 2.56 us -> 3.85 us  [swap(): lax.ppermute(odd, axis, pairs(1))]
  transfers between devices with their start and end apart: 4 -> 4, of which waited for: 1 -> 0; matrix products, arithmetic and copies ran while one was open for 0% -> 0% of each run, Pallas kernels for 17% -> 18%
where the time goes in v4:
time: 67.9 us; the launch traced here: 67.5 us
  blocking collectives  29 us (43%)
  Pallas kernels  22.9 us (34%)
  starting transfers between devices  7.25 us (11%)
  local copies, waits for them, and re-layouts  4.28 us (6%)
  between operations  3.22 us (5%)
  other arithmetic  0.87 us (1%)
    all_to_all x1, blocking collectives, on_device(): fastest = jnp.max(lax.all_to_all(top, ('gx', 'gy'), 0, 0, tiled=True))  29 us
    pallas_call x1, Pallas kernels, on_device(): call(functools.partial(prep_kernel, cells_x, cells_y, step), (parcels, pa...  8.31 us
    pallas_call x1, Pallas kernels, on_device(): call(functools.partial(deposit_kernel, cells_x, cells_y, step, (0, 1), Tr...  6.22 us
    pallas_call x1, Pallas kernels, on_device(): call(functools.partial(deposit_kernel, cells_x, cells_y, step, (2, 3), Fa...  6.16 us
    unnamed x14, local copies, waits for them, and re-layouts  4.28 us
    ppermute x2, starting transfers between devices, swap(): lax.ppermute(odd, axis, pairs(1))  3.85 us
    ppermute x2, starting transfers between devices, swap(): lax.ppermute(even, axis, pairs(0))  3.4 us
    pallas_call x1, Pallas kernels, on_device(): call(functools.partial(update_kernel, cells_x, cells_y), (sds(density.sha...  1.82 us
  transfers between devices with their start and end apart: 4, of which 0 were waited for; matrix products, arithmetic and copies ran while one was open for 0% of the time, Pallas kernels for 18%

profile of v4, /device:TPU:1, one launch (start us, length us, event | category | flops | bytes accessed | tf_op | source)
XLA Modules:
  0.0 67.5 jit_solution(454524430757918695)
XLA Ops:
  1.3 0.0 copy-start.2
  1.3 0.9 %copy-done.2 = f32[16,16,256]{2,1,0:T(8,128)S(1)} copy-done((f32[16,16,256]{2,1,0:T(8,128)S(1)}, f32[16,16,256]{2,1,0:T(8,128)}, u32[]{:S(2)}) %copy-start.2) | copy-done | bytes 262168
  2.2 0.9 %copy-done.3 = f32[3,8192]{1,0:T(4,128)S(1)} copy-done((f32[3,8192]{1,0:T(4,128)S(1)}, f32[3,8192]{1,0:T(4,128)}, u32[]{:S(2)}) %copy-start.3) | copy-done | bytes 98328
  3.1 0.9 %copy-done.4 = s32[3,8192]{1,0:T(4,128)S(1)} copy-done((s32[3,8192]{1,0:T(4,128)S(1)}, s32[3,8192]{1,0:T(4,128)}, u32[]{:S(2)}) %copy-start.4) | copy-done | bytes 98328
  4.0 0.8 %copy-done.5 = f32[8192]{0:T(1024)S(1)} copy-done((f32[8192]{0:T(1024)S(1)}, f32[8192]{0:T(1024)}, u32[]{:S(2)}) %copy-start.5) | copy-done | bytes 32792
  4.8 0.8 %copy-done.6 = f32[8192]{0:T(1024)S(1)} copy-done((f32[8192]{0:T(1024)S(1)}, f32[8192]{0:T(1024)}, u32[]{:S(2)}) %copy-start.6) | copy-done | bytes 32792
  5.6 8.3 %prep.1 = (f32[8,1280]{1,0:T(8,128)S(1)}, f32[8,1280]{1,0:T(8,128)S(1)}, f32[8,8192]{1,0:T(8,128)S(1)}, f32[2,8,512]{2,1,0:T(8,128)S(1)}, f32[4,16,256]{2,1,0:T(8,128)S(1)}, /*index=5*/f32[16,16,256]{2,1,0:T(8,128)S(1)}) custom-call(s32[1]{0:T(128)S(6)} %copy.19.count, f32[64,128]{1,0:T(8,128)S(1)} %bitcast.6, f32[64,128]{1,0:T(8,128)S(1)} %bitcast.7, ...), custom_call_target="tpu_custom_call" | custom-call | tf_op jit(solution)/shard_map/prep/pallas_call | solution.py:419
  13.9 2.1 %collective-permute-start = (f32[8,1280]{1,0:T(8,128)S(1)}, f32[8,1280]{1,0:T(8,128)S(1)}, u32[]{:S(2)}, u32[]{:S(2)}) collective-permute-start(f32[8,1280]{1,0:T(8,128)S(1)} %get-tuple-element.25), channel_id=1, source_target_pairs={{0,1},{1,0},{2,3},{3,2},{4,5},{5,4},{6,7},{7,6},{8,9},{9,8},{10,11... | collective-permute-start | bytes 122888 | tf_op jit(solution)/shard_map/ppermute | solution.py:404
  16.0 0.7 collective-permute-start.1
  16.6 6.2 %deposit01.1 = (f32[2,16,16,256]{3,2,1,0:T(8,128)S(1)}, f32[5,10240]{1,0:T(8,128)}, s32[3,10240]{1,0:T(4,128)}) custom-call(f32[8,8192]{1,0:T(8,128)S(1)} %get-tuple-element.30.refs_0_), custom_call_target="tpu_custom_call" | custom-call | tf_op jit(solution)/shard_map/deposit01/pallas_call | solution.py:461
  22.9 0.0 collective-permute-done.in_even.y_even
  22.9 0.0 collective-permute-done.1.in_odd.y_odd
  22.9 0.0 copy-start
  22.9 0.4 relay.1
  23.3 1.3 %collective-permute-start.2 = (f32[8,1280]{1,0:T(8,128)S(1)}, f32[8,1280]{1,0:T(8,128)S(1)}, u32[]{:S(2)}, u32[]{:S(2)}) collective-permute-start(f32[8,1280]{1,0:T(8,128)S(1)} %get-tuple-element.32), channel_id=1, source_target_pairs={{0,32},{32,0},{64,96},{96,64},{128,160},{160,128},{192,224},{224,1... | collective-permute-start | bytes 122888 | tf_op jit(solution)/shard_map/ppermute | solution.py:404
  24.6 3.2 %collective-permute-start.3 = (f32[8,1280]{1,0:T(8,128)S(1)}, f32[8,1280]{1,0:T(8,128)S(1)}, u32[]{:S(2)}, u32[]{:S(2)}) collective-permute-start(f32[8,1280]{1,0:T(8,128)S(1)} %get-tuple-element.33), channel_id=1, source_target_pairs={{32,64},{64,32},{96,128},{128,96},{160,192},{192,160},{33,65},{65,... | collective-permute-start | bytes 122888 | tf_op jit(solution)/shard_map/ppermute | solution.py:404
  27.8 0.0 copy-start.1
  27.8 6.2 %deposit23.1.dep23 = f32[2,16,16,256]{3,2,1,0:T(8,128)S(1)} custom-call(f32[8,8192]{1,0:T(8,128)S(1)} %get-tuple-element.30.refs_0_, f32[2,16,256]{2,1,0:T(8,128)S(1)} %get-tuple-element.34.refs_1_.halo_y), custom_call_target="tpu_custom_call" | custom-call | tf_op jit(solution)/shard_map/deposit23/pallas_call | solution.py:474
  33.9 0.0 collective-permute-done.2.x_even
  34.0 0.0 collective-permute-done.3.x_odd
  34.0 0.0 copy-done
  34.0 1.8 %update.1 = (f32[16,16,256]{2,1,0:T(8,128)}, f32[3,16,16,256]{3,2,1,0:T(8,128)}, f32[16,16,256]{2,1,0:T(8,128)}, f32[256,128]{1,0:T(8,128)S(1)}, f32[5,10240]{1,0:T(8,128)}, /*index=5*/s32[3,10240]{1,0:T(4,128)}) custom-call(f32[8,1280]{1,0:T(8,128)S(1)} %collective-permute-done.in_even.y_even, ...), custom_call_target="tpu_custom_call", output_to_operand_aliasing={{4}: (12, {}), {5}: (13, {})} | custom-call | tf_op jit(solution)/shard_map/update/pallas_call | solution.py:482
  35.8 29.0 %all_to_all.9 = f32[256,1,128]{2,1,0:T(1,128)S(1)} all-to-all(f32[256,1,128]{2,1,0:T(1,128)S(1)} %bitcast.5), channel_id=1, replica_groups=mesh['gx'=8,'gy'=32] {'gx','gy'}, dimensions={0} | all-to-all | bytes 262144 | tf_op jit(solution)/shard_map/all_to_all | solution.py:509
  64.9 0.9 %reduce_max.9 = f32[]{:T(128)} reduce(f32[256,1,128]{2,1,0:T(1,128)S(1)} %all_to_all.9, f32[]{:T(128)} %constant.1.clone.1), dimensions={0,1,2}, to_apply=%region_0.0 | reduce | flops 32767 | bytes 131080 | tf_op jit(solution)/shard_map/reduce_max | solution.py:509
  (5 shorter events, 0.0 us)
Async XLA Ops:
  1.3 1.0 %copy-start.2 = (f32[16,16,256]{2,1,0:T(8,128)S(1)}, f32[16,16,256]{2,1,0:T(8,128)}, u32[]{:S(2)}) copy-start(f32[16,16,256]{2,1,0:T(8,128)} %energy.1) | copy-start | bytes 786436
  2.2 0.9 %copy-start.3 = (f32[3,8192]{1,0:T(4,128)S(1)}, f32[3,8192]{1,0:T(4,128)}, u32[]{:S(2)}) copy-start(f32[3,8192]{1,0:T(4,128)} %vel.1) | copy-start | bytes 294916
  3.1 0.9 %copy-start.4 = (s32[3,8192]{1,0:T(4,128)S(1)}, s32[3,8192]{1,0:T(4,128)}, u32[]{:S(2)}) copy-start(s32[3,8192]{1,0:T(4,128)} %cell.1) | copy-start | bytes 294916
  4.0 0.8 %copy-start.5 = (f32[8192]{0:T(1024)S(1)}, f32[8192]{0:T(1024)}, u32[]{:S(2)}) copy-start(f32[8192]{0:T(1024)} %param.11) | copy-start | bytes 98308
  4.8 0.8 %copy-start.6 = (f32[8192]{0:T(1024)S(1)}, f32[8192]{0:T(1024)}, u32[]{:S(2)}) copy-start(f32[8192]{0:T(1024)} %param.13) | copy-start | bytes 98308
  13.9 9.0 %collective-permute-start = (f32[8,1280]{1,0:T(8,128)S(1)}, f32[8,1280]{1,0:T(8,128)S(1)}, u32[]{:S(2)}, u32[]{:S(2)}) collective-permute-start(f32[8,1280]{1,0:T(8,128)S(1)} %get-tuple-element.25), channel_id=1, source_target_pairs={{0,1},{1,0},{2,3},{3,2},{4,5},{5,4},{6,7},{7,6},{8,9},{9,8},{10,11... | collective-permute-start | bytes 122888 | tf_op jit(solution)/shard_map/ppermute | solution.py:404
  16.0 6.9 %collective-permute-start.1 = (f32[8,1280]{1,0:T(8,128)S(1)}, f32[8,1280]{1,0:T(8,128)S(1)}, u32[]{:S(2)}, u32[]{:S(2)}) collective-permute-start(f32[8,1280]{1,0:T(8,128)S(1)} %get-tuple-element.26), channel_id=1, source_target_pairs={{1,2},{2,1},{3,4},{4,3},{5,6},{6,5},{7,8},{8,7},{9,10},{10,9},{11,... | collective-permute-start | bytes 122888 | tf_op jit(solution)/shard_map/ppermute | solution.py:404
  22.9 11.1 %copy-start = (f32[3,16,16,256]{3,2,1,0:T(8,128)S(1)}, f32[3,16,16,256]{3,2,1,0:T(8,128)}, u32[]{:S(2)}) copy-start(f32[3,16,16,256]{3,2,1,0:T(8,128)} %momentum.1) | copy-start | bytes 2359300
  23.3 10.7 %collective-permute-start.2 = (f32[8,1280]{1,0:T(8,128)S(1)}, f32[8,1280]{1,0:T(8,128)S(1)}, u32[]{:S(2)}, u32[]{:S(2)}) collective-permute-start(f32[8,1280]{1,0:T(8,128)S(1)} %get-tuple-element.32), channel_id=1, source_target_pairs={{0,32},{32,0},{64,96},{96,64},{128,160},{160,128},{192,224},{224,1... | collective-permute-start | bytes 122888 | tf_op jit(solution)/shard_map/ppermute | solution.py:404
  24.6 9.4 %collective-permute-start.3 = (f32[8,1280]{1,0:T(8,128)S(1)}, f32[8,1280]{1,0:T(8,128)S(1)}, u32[]{:S(2)}, u32[]{:S(2)}) collective-permute-start(f32[8,1280]{1,0:T(8,128)S(1)} %get-tuple-element.33), channel_id=1, source_target_pairs={{32,64},{64,32},{96,128},{128,96},{160,192},{192,160},{33,65},{65,... | collective-permute-start | bytes 122888 | tf_op jit(solution)/shard_map/ppermute | solution.py:404
  27.8 6.2 %copy-start.1 = (f32[16,16,256]{2,1,0:T(8,128)S(1)}, f32[16,16,256]{2,1,0:T(8,128)}, u32[]{:S(2)}) copy-start(f32[16,16,256]{2,1,0:T(8,128)} %density.1) | copy-start | bytes 786436

commit v5 on v4

--- a/solution.py
+++ b/solution.py
@@ -28,34 +28,17 @@
     return 1.0 / (1.0 + jnp.exp(-2.0 * (temp - 2.0)))
 
 
-def prep_kernel(
-    cells_x, cells_y, step, count, mass, temp, vel, cell, energy,
-    even, odd, stay, own, leaving, partial,
-    mass_v, temp_v, vel_v, cell_v, pay, cx, cy, pos, compact, table_v, table_s, tiles, acc, sems,
-):
-    fetches = [
-        pltpu.make_async_copy(there, here, sems.at[i])
-        for i, (there, here) in enumerate(
-            ((cell, cell_v), (temp, temp_v), (mass, mass_v), (vel, vel_v))
-        )
-    ]
-    for fetch in fetches:
-        fetch.start()
-    mass, temp, vel, cell = mass_v, temp_v, vel_v, cell_v
-    fetches[0].wait()
-    chunks = mass.shape[0]
+def rank_kernel(cells_x, cells_y, count, cell, place, stays, words, masks, cx, cy):
+    chunks = place.shape[0]
     anchor_x = lax.axis_index("gx") * cells_x
     anchor_y = lax.axis_index("gy") * cells_y
-    anchor_xf, anchor_yf = anchors(cells_x, cells_y)
     for b in range(chunks):
         lanes = slice(b * LANES, (b + 1) * LANES)
         cx[b : b + 1, :] = cell[0:1, lanes]
         cy[b : b + 1, :] = cell[1:2, lanes]
     shape = (chunks, LANES)
-    live = iota(shape, 0) * LANES + iota(shape, 1) < count[0]
-    fetches[1].wait()
-    fetches[2].wait()
-    kept = mass[...] * (1.0 - SHRINK * jnp.where(live, sigmoid_of(temp[...]), 0.0))
+    lane = iota(shape, 1)
+    live = iota(shape, 0) * LANES + lane < count[0]
     local_x = cx[...] - anchor_x
     local_y = cy[...] - anchor_y
     heading = jnp.where(
@@ -66,37 +49,50 @@
         ),
     )
     heading = jnp.where(live, heading, 5)
-    masks = [jnp.where(heading == h, 1.0, 0.0) for h in range(4)]
+    hits = [jnp.where(heading == h, 1.0, 0.0) for h in range(4)]
     lane_r = iota((LANES, 2 * LANES), 0)
     lane_c = iota((LANES, 2 * LANES), 1)
     scan = jnp.where((lane_r < lane_c) | (lane_c >= LANES), 1.0, 0.0).astype(BF16)
-    both = jnp.dot(
-        jnp.concatenate(masks, axis=0).astype(BF16), scan, preferred_element_type=F32
-    )
+    both = jnp.dot(jnp.concatenate(hits, axis=0).astype(BF16), scan, preferred_element_type=F32)
     inner = [both[h * chunks : (h + 1) * chunks, :LANES] for h in range(4)]
     total = [both[h * chunks : (h + 1) * chunks, LANES:] for h in range(4)]
     below = jnp.where(iota((chunks, chunks), 1) < iota((chunks, chunks), 0), 1.0, 0.0).astype(BF16)
     base = jnp.dot(
         below, jnp.concatenate(total, axis=1).astype(BF16), preferred_element_type=F32
-    )
-    lane = iota(shape, 1)
+    ).astype(I32)
     offset = jnp.zeros(shape, F32)
-    place = jnp.full(shape, -1.0, F32)
-    words = jnp.zeros(shape, I32)
+    spot = jnp.full(shape, -1.0, F32)
+    word = jnp.zeros(shape, I32)
     for h in range(4):
-        place = jnp.where(heading == h, inner[h] + offset, place)
-        base_h = base[:, h * LANES : (h + 1) * LANES]
-        word = base_h.astype(I32) + offset.astype(I32) * 1024 + total[h].astype(I32) * (1024 * 256)
-        words = jnp.where(lane == h, word, words)
+        spot = jnp.where(heading == h, inner[h] + offset, spot)
+        start = base[:, h * LANES : (h + 1) * LANES]
+        within = start & (LANES - 1)
+        end = within + total[h].astype(I32)
+        turn = (start - offset.astype(I32)) & (LANES - 1)
+        word = jnp.where(lane == h, (start >> 7) * LANES + turn, word)
+        last = start + total[h].astype(I32)
+        word = jnp.where(lane == 4 + h, last >> 7, word)
+        masks[h, 0] = jnp.where((lane >= within) & (lane < end), 1.0, 0.0)
+        masks[h, 1] = jnp.where(lane < end - LANES, 1.0, 0.0)
+        masks[h, 2] = jnp.where(end >= LANES, 1.0, 0.0)
         offset = offset + total[h]
-    table_v[...] = words
-    load = pltpu.make_async_copy(table_v, table_s, sems.at[4])
+    words[...] = word
+    place[...] = spot
+    stays[...] = jnp.where(heading == 4, 1.0, 0.0)
+
+
+def prep_kernel(
+    cells_x, cells_y, step, mass, temp, vel, cell, energy, pos, stays, words, masks,
+    even, odd, stay, own, leaving, partial,
+    pay, compact, table, tiles, acc, sem,
+):
+    load = pltpu.make_async_copy(words, table, sem)
     load.start()
-    pos[...] = place
-    fetches[3].wait()
+    chunks = mass.shape[0]
+    anchor_xf, anchor_yf = anchors(cells_x, cells_y)
+    kept = mass[...] * (1.0 - SHRINK * sigmoid_of(temp[...]))
     pay[1:4, :] = vel[...]
     pay[5:8, :] = cell[...].astype(F32)
-    stays = jnp.where(heading == 4, 1.0, 0.0)
     for b in range(chunks):
         lanes = slice(b * LANES, (b + 1) * LANES)
         pay[0:1, lanes] = kept[b : b + 1, :]
@@ -124,7 +120,6 @@
     lax.fori_loop(0, chunks // group, pack, 0)
     tiles[...] = jnp.zeros(tiles.shape, F32)
     load.wait()
-    lane8 = iota((8, LANES), 1)
     unroll = 8
 
     def place_all(g, carry):
@@ -133,26 +128,20 @@
             b = g * unroll + u
             rows = compact[b]
             for h in range(4):
-                word = table_s[b, h]
-                start = word & 1023
-                first = (word >> 10) & 255
-                number = word >> 18
-                within = start & (LANES - 1)
-                end = within + number
-                turned = pltpu.roll(rows, (start - first) & (LANES - 1), 1)
-                merged = jnp.where((lane8 >= within) & (lane8 < end), turned, carry[h])
-                tiles[h, start >> 7] = merged
-                over = jnp.where(lane8 < end - LANES, turned, 0.0)
-                carry[h] = jnp.where(end >= LANES, over, merged)
+                word = table[b, h]
+                turned = pltpu.roll(rows, word & (LANES - 1), 1)
+                merged = jnp.where(masks[h, 0, pl.ds(b, 1), :] > 0.0, turned, carry[h])
+                tiles[h, word >> 7] = merged
+                rest = jnp.where(masks[h, 2, pl.ds(b, 1), :] > 0.0, 0.0, merged)
+                carry[h] = jnp.where(masks[h, 1, pl.ds(b, 1), :] > 0.0, turned, rest)
         return tuple(carry)
 
     carry = lax.fori_loop(
         0, chunks // unroll, place_all, tuple(jnp.zeros((8, LANES), F32) for _ in range(4))
     )
     for h in range(4):
-        word = table_s[chunks - 1, h]
-        tiles[h, ((word & 1023) + (word >> 18)) >> 7] = carry[h]
-    width = 4 * LANES
+        tiles[h, table[chunks - 1, 4 + h]] = carry[h]
+    width = own.shape[2]
     buckets = [
         jnp.concatenate([tiles[h, t] for t in range(width // LANES)], axis=1) for h in range(4)
     ]
@@ -416,6 +405,15 @@
     sds = jax.ShapeDtypeStruct
     whole = pl.BlockSpec(memory_space=VMEM)
     parcels = sds((8, capacity + 3 * depth), F32)
+    dense = sds((chunks, LANES), F32)
+    place, stays, words, masks = call(
+        functools.partial(rank_kernel, cells_x, cells_y),
+        (dense, dense, sds((chunks, LANES), I32), sds((4, 3, chunks, LANES), F32)),
+        scratch=(VMEM((chunks, LANES), I32), VMEM((chunks, LANES), I32)),
+        in_specs=[pl.BlockSpec(memory_space=pltpu.SMEM), whole],
+        name="rank",
+        cost_estimate=pl.CostEstimate(flops=10**9, bytes_accessed=10**6, transcendentals=0),
+    )(parcel_count, parcel_cell)
     even, odd, stay, own, leaving, partial = call(
         functools.partial(prep_kernel, cells_x, cells_y, step),
         (
@@ -427,32 +425,24 @@
             sds(energy.shape, F32),
         ),
         scratch=(
-            VMEM((chunks, LANES), F32),
-            VMEM((chunks, LANES), F32),
-            VMEM((3, rows), F32),
-            VMEM((3, rows), I32),
             VMEM((8, rows), F32),
-            VMEM((chunks, LANES), I32),
-            VMEM((chunks, LANES), I32),
-            VMEM((chunks, LANES), F32),
             VMEM((chunks, 8, LANES), F32),
-            VMEM((chunks, LANES), I32),
             pltpu.SMEM((chunks, LANES), I32),
             VMEM((4, capacity // LANES + 1, 8, LANES), F32),
             VMEM((2 * columns, depth), F32),
-            pltpu.SemaphoreType.DMA((5,)),
-        ),
-        in_specs=[pl.BlockSpec(memory_space=pltpu.SMEM)]
-        + [pl.BlockSpec(memory_space=pltpu.HBM)] * 4
-        + [whole],
+            pltpu.SemaphoreType.DMA,
+        ),
         name="prep",
     )(
-        parcel_count,
         parcel_mass.reshape(chunks, LANES),
         parcel_temp.reshape(chunks, LANES),
         droplet_velocity,
         parcel_cell,
         energy,
+        place,
+        stays,
+        words,
+        masks,
     )
     y_even, y_odd = swap("gy", even, odd)
     slots = rows + 4 * capacity

time: 67.9 us -> 64.2 us (0.946)
  local copies, waits for them, and re-layouts: 4.28 us -> 1.47 us
  Pallas kernels: 22.9 us -> 22.1 us
    unnamed x14, local copies, waits for them, and re-layouts: 4.28 us -> 1.47 us
    pallas_call x1, Pallas kernels: 8.31 us -> 7.11 us  [on_device(): call(functools.partial(prep_kernel, cells_x, cells_y, step), (parcels, pa...]
  transfers between devices with their start and end apart: 4 -> 4, of which waited for: 0 -> 0; matrix products, arithmetic and copies ran while one was open for 0% -> 0% of each run, Pallas kernels for 18% -> 19%
where the time goes in v5:
time: 64.2 us; the launch traced here: 64 us
  blocking collectives  29 us (45%)
  Pallas kernels  22.1 us (34%)
  starting transfers between devices  7.24 us (11%)
  between operations  3.23 us (5%)
  local copies, waits for them, and re-layouts  1.47 us (2%)
  other arithmetic  0.87 us (1%)
    all_to_all x1, blocking collectives, on_device(): fastest = jnp.max(lax.all_to_all(top, ('gx', 'gy'), 0, 0, tiled=True))  29 us
    pallas_call x1, Pallas kernels, on_device(): call(functools.partial(prep_kernel, cells_x, cells_y, step), (parcels, pa...  7.11 us
    pallas_call x1, Pallas kernels, on_device(): call(functools.partial(deposit_kernel, cells_x, cells_y, step, (0, 1), Tr...  6.22 us
    pallas_call x1, Pallas kernels, on_device(): call(functools.partial(deposit_kernel, cells_x, cells_y, step, (2, 3), Fa...  6.16 us
    ppermute x2, starting transfers between devices, swap(): lax.ppermute(odd, axis, pairs(1))  3.86 us
    ppermute x2, starting transfers between devices, swap(): lax.ppermute(even, axis, pairs(0))  3.39 us
    pallas_call x1, Pallas kernels, on_device(): call(functools.partial(update_kernel, cells_x, cells_y), (sds(density.sha...  1.82 us
    unnamed x14, local copies, waits for them, and re-layouts  1.47 us
  transfers between devices with their start and end apart: 4, of which 0 were waited for; matrix products, arithmetic and copies ran while one was open for 0% of the time, Pallas kernels for 19%

profile of v5, /device:TPU:1, one launch (start us, length us, event | category | flops | bytes accessed | tf_op | source)
XLA Modules:
  0.0 64.0 jit_solution(10257510750011675945)
XLA Ops:
  1.3 0.0 copy-start.4
  1.3 0.9 %copy-done.4 = s32[3,8192]{1,0:T(4,128)S(1)} copy-done((s32[3,8192]{1,0:T(4,128)S(1)}, s32[3,8192]{1,0:T(4,128)}, u32[]{:S(2)}) %copy-start.4) | copy-done | bytes 98328
  2.2 0.4 rank.1
  2.6 0.5 copy-done.2
  3.1 0.0 copy-done.3
  3.2 0.0 copy-done.5
  3.2 0.0 copy-done.6
  3.2 7.1 %prep.1 = (f32[8,1280]{1,0:T(8,128)S(1)}, f32[8,1280]{1,0:T(8,128)S(1)}, f32[8,8192]{1,0:T(8,128)S(1)}, f32[2,8,512]{2,1,0:T(8,128)S(1)}, f32[4,16,256]{2,1,0:T(8,128)S(1)}, /*index=5*/f32[16,16,256]{2,1,0:T(8,128)S(1)}) custom-call(f32[64,128]{1,0:T(8,128)S(1)} %bitcast.6, f32[64,128]{1,0:T(8,128)S(1)} %bitcast.7, f32[3,8192]{1,0:T(4,128)S(1)} %copy-done.3, ...), custom_call_target="tpu_custom_call" | custom-call | tf_op jit(solution)/shard_map/prep/pallas_call | solution.py:417
  10.3 2.1 %collective-permute-start = (f32[8,1280]{1,0:T(8,128)S(1)}, f32[8,1280]{1,0:T(8,128)S(1)}, u32[]{:S(2)}, u32[]{:S(2)}) collective-permute-start(f32[8,1280]{1,0:T(8,128)S(1)} %get-tuple-element.33), channel_id=1, source_target_pairs={{0,1},{1,0},{2,3},{3,2},{4,5},{5,4},{6,7},{7,6},{8,9},{9,8},{10,11... | collective-permute-start | bytes 122888 | tf_op jit(solution)/shard_map/ppermute | solution.py:393
  12.4 0.7 %collective-permute-start.1 = (f32[8,1280]{1,0:T(8,128)S(1)}, f32[8,1280]{1,0:T(8,128)S(1)}, u32[]{:S(2)}, u32[]{:S(2)}) collective-permute-start(f32[8,1280]{1,0:T(8,128)S(1)} %get-tuple-element.34), channel_id=1, source_target_pairs={{1,2},{2,1},{3,4},{4,3},{5,6},{6,5},{7,8},{8,7},{9,10},{10,9},{11,... | collective-permute-start | bytes 122888 | tf_op jit(solution)/shard_map/ppermute | solution.py:393
  13.1 6.2 %deposit01.1 = (f32[2,16,16,256]{3,2,1,0:T(8,128)S(1)}, f32[5,10240]{1,0:T(8,128)}, s32[3,10240]{1,0:T(4,128)}) custom-call(f32[8,8192]{1,0:T(8,128)S(1)} %get-tuple-element.38.refs_0_), custom_call_target="tpu_custom_call" | custom-call | tf_op jit(solution)/shard_map/deposit01/pallas_call | solution.py:451
  19.3 0.0 collective-permute-done.in_even.y_even
  19.3 0.0 collective-permute-done.1.in_odd.y_odd
  19.3 0.0 copy-start
  19.3 0.4 relay.1
  19.7 1.3 %collective-permute-start.2 = (f32[8,1280]{1,0:T(8,128)S(1)}, f32[8,1280]{1,0:T(8,128)S(1)}, u32[]{:S(2)}, u32[]{:S(2)}) collective-permute-start(f32[8,1280]{1,0:T(8,128)S(1)} %get-tuple-element.40), channel_id=1, source_target_pairs={{0,32},{32,0},{64,96},{96,64},{128,160},{160,128},{192,224},{224,1... | collective-permute-start | bytes 122888 | tf_op jit(solution)/shard_map/ppermute | solution.py:393
  21.0 3.2 %collective-permute-start.3 = (f32[8,1280]{1,0:T(8,128)S(1)}, f32[8,1280]{1,0:T(8,128)S(1)}, u32[]{:S(2)}, u32[]{:S(2)}) collective-permute-start(f32[8,1280]{1,0:T(8,128)S(1)} %get-tuple-element.41), channel_id=1, source_target_pairs={{32,64},{64,32},{96,128},{128,96},{160,192},{192,160},{33,65},{65,... | collective-permute-start | bytes 122888 | tf_op jit(solution)/shard_map/ppermute | solution.py:393
  24.2 0.0 copy-start.1
  24.2 6.2 %deposit23.1.dep23 = f32[2,16,16,256]{3,2,1,0:T(8,128)S(1)} custom-call(f32[8,8192]{1,0:T(8,128)S(1)} %get-tuple-element.38.refs_0_, f32[2,16,256]{2,1,0:T(8,128)S(1)} %get-tuple-element.42.refs_1_.halo_y), custom_call_target="tpu_custom_call" | custom-call | tf_op jit(solution)/shard_map/deposit23/pallas_call | solution.py:464
  30.4 0.0 collective-permute-done.2.x_even
  30.4 0.0 collective-permute-done.3.x_odd
  30.4 1.8 %update.1 = (f32[16,16,256]{2,1,0:T(8,128)}, f32[3,16,16,256]{3,2,1,0:T(8,128)}, f32[16,16,256]{2,1,0:T(8,128)}, f32[256,128]{1,0:T(8,128)S(1)}, f32[5,10240]{1,0:T(8,128)}, /*index=5*/s32[3,10240]{1,0:T(4,128)}) custom-call(f32[8,1280]{1,0:T(8,128)S(1)} %collective-permute-done.in_even.y_even, ...), custom_call_target="tpu_custom_call", output_to_operand_aliasing={{4}: (12, {}), {5}: (13, {})} | custom-call | tf_op jit(solution)/shard_map/update/pallas_call | solution.py:472
  32.2 29.0 %all_to_all.9 = f32[256,1,128]{2,1,0:T(1,128)S(1)} all-to-all(f32[256,1,128]{2,1,0:T(1,128)S(1)} %bitcast.5), channel_id=1, replica_groups=mesh['gx'=8,'gy'=32] {'gx','gy'}, dimensions={0} | all-to-all | bytes 262144 | tf_op jit(solution)/shard_map/all_to_all | solution.py:499
  61.3 0.9 %reduce_max.9 = f32[]{:T(128)} reduce(f32[256,1,128]{2,1,0:T(1,128)S(1)} %all_to_all.9, f32[]{:T(128)} %constant.1.clone.1), dimensions={0,1,2}, to_apply=%region_0.0 | reduce | flops 32767 | bytes 131080 | tf_op jit(solution)/shard_map/reduce_max | solution.py:499
  (6 shorter events, 0.0 us)
Async XLA Ops:
  1.3 0.9 %copy-start.4 = (s32[3,8192]{1,0:T(4,128)S(1)}, s32[3,8192]{1,0:T(4,128)}, u32[]{:S(2)}) copy-start(s32[3,8192]{1,0:T(4,128)} %cell.3) | copy-start | bytes 294916
  2.2 0.9 %copy-start.2 = (f32[16,16,256]{2,1,0:T(8,128)S(1)}, f32[16,16,256]{2,1,0:T(8,128)}, u32[]{:S(2)}) copy-start(f32[16,16,256]{2,1,0:T(8,128)} %energy.1) | copy-start | bytes 786436
  2.2 1.0 %copy-start.3 = (f32[3,8192]{1,0:T(4,128)S(1)}, f32[3,8192]{1,0:T(4,128)}, u32[]{:S(2)}) copy-start(f32[3,8192]{1,0:T(4,128)} %vel.1) | copy-start | bytes 294916
  2.2 1.0 %copy-start.5 = (f32[8192]{0:T(1024)S(1)}, f32[8192]{0:T(1024)}, u32[]{:S(2)}) copy-start(f32[8192]{0:T(1024)} %param.11) | copy-start | bytes 98308
  2.2 1.0 %copy-start.6 = (f32[8192]{0:T(1024)S(1)}, f32[8192]{0:T(1024)}, u32[]{:S(2)}) copy-start(f32[8192]{0:T(1024)} %param.13) | copy-start | bytes 98308
  10.3 9.0 %collective-permute-start = (f32[8,1280]{1,0:T(8,128)S(1)}, f32[8,1280]{1,0:T(8,128)S(1)}, u32[]{:S(2)}, u32[]{:S(2)}) collective-permute-start(f32[8,1280]{1,0:T(8,128)S(1)} %get-tuple-element.33), channel_id=1, source_target_pairs={{0,1},{1,0},{2,3},{3,2},{4,5},{5,4},{6,7},{7,6},{8,9},{9,8},{10,11... | collective-permute-start | bytes 122888 | tf_op jit(solution)/shard_map/ppermute | solution.py:393
  12.4 6.9 %collective-permute-start.1 = (f32[8,1280]{1,0:T(8,128)S(1)}, f32[8,1280]{1,0:T(8,128)S(1)}, u32[]{:S(2)}, u32[]{:S(2)}) collective-permute-start(f32[8,1280]{1,0:T(8,128)S(1)} %get-tuple-element.34), channel_id=1, source_target_pairs={{1,2},{2,1},{3,4},{4,3},{5,6},{6,5},{7,8},{8,7},{9,10},{10,9},{11,... | collective-permute-start | bytes 122888 | tf_op jit(solution)/shard_map/ppermute | solution.py:393
  19.3 11.1 %copy-start = (f32[3,16,16,256]{3,2,1,0:T(8,128)S(1)}, f32[3,16,16,256]{3,2,1,0:T(8,128)}, u32[]{:S(2)}) copy-start(f32[3,16,16,256]{3,2,1,0:T(8,128)} %momentum.1) | copy-start | bytes 2359300
  19.7 10.7 %collective-permute-start.2 = (f32[8,1280]{1,0:T(8,128)S(1)}, f32[8,1280]{1,0:T(8,128)S(1)}, u32[]{:S(2)}, u32[]{:S(2)}) collective-permute-start(f32[8,1280]{1,0:T(8,128)S(1)} %get-tuple-element.40), channel_id=1, source_target_pairs={{0,32},{32,0},{64,96},{96,64},{128,160},{160,128},{192,224},{224,1... | collective-permute-start | bytes 122888 | tf_op jit(solution)/shard_map/ppermute | solution.py:393
  21.0 9.4 %collective-permute-start.3 = (f32[8,1280]{1,0:T(8,128)S(1)}, f32[8,1280]{1,0:T(8,128)S(1)}, u32[]{:S(2)}, u32[]{:S(2)}) collective-permute-start(f32[8,1280]{1,0:T(8,128)S(1)} %get-tuple-element.41), channel_id=1, source_target_pairs={{32,64},{64,32},{96,128},{128,96},{160,192},{192,160},{33,65},{65,... | collective-permute-start | bytes 122888 | tf_op jit(solution)/shard_map/ppermute | solution.py:393
  24.2 6.2 %copy-start.1 = (f32[16,16,256]{2,1,0:T(8,128)S(1)}, f32[16,16,256]{2,1,0:T(8,128)}, u32[]{:S(2)}) copy-start(f32[16,16,256]{2,1,0:T(8,128)} %density.1) | copy-start | bytes 786436

commit v6 on v5

--- a/solution.py
+++ b/solution.py
@@ -151,13 +151,14 @@
         leaving[h] = one_field(buckets[h], along, number, acc.shape[1], 4)
     for h in range(2):
         own[h] = buckets[h]
-    columns = cells_x * cells_y
-    deposit_fields((4,), anchor_xf, anchor_yf, cells_y, step, stay, acc)
-    for x in range(cells_x):
-        rows = slice(x * cells_y, (x + 1) * cells_y)
-        partial[x] = energy[x] + (acc[rows] + acc[columns + x * cells_y : columns + (x + 1) * cells_y])
-    up = message(buckets[3], partial[:, cells_y - 1, :], leaving[0, -1:, :], leaving[1, -1:, :])
-    down = message(buckets[2], partial[:, 0, :], leaving[0, 0:1, :], leaving[1, 0:1, :])
+    outer_energy(cells_x, cells_y, anchor_xf, anchor_yf, step, stay, acc)
+    planes = [acc[q * 2 * cells_y : (q * 2 + 1) * cells_y] + acc[(q * 2 + 1) * cells_y : (q * 2 + 2) * cells_y] for q in range(4)]
+    partial[0] = energy[0] + planes[0]
+    partial[1] = energy[cells_x - 1] + planes[1]
+    up = message(
+        buckets[3], energy[:, cells_y - 1, :] + planes[3], leaving[0, -1:, :], leaving[1, -1:, :]
+    )
+    down = message(buckets[2], energy[:, 0, :] + planes[2], leaving[0, 0:1, :], leaving[1, 0:1, :])
     send_pair("gy", even, odd, up, down)
 
 
@@ -224,19 +225,20 @@
     return jnp.where(rows[7:8] == iota((depth, n), 0).astype(F32), 1.0, 0.0).astype(BF16)
 
 
-def deposit_fields(fields, anchor_x, anchor_y, cells_y, step, stay, acc):
+def outer_energy(cells_x, cells_y, anchor_x, anchor_y, step, stay, acc):
     total = stay.shape[1]
-    columns = acc.shape[0] // (2 * len(fields))
     depth = acc.shape[1]
     acc[...] = jnp.zeros(acc.shape, F32)
 
     def one(k, carry):
         rows = stay[:, pl.ds(pl.multiple_of(k * step, step), step)]
-        column = (rows[5:6] - anchor_x) * cells_y + (rows[6:7] - anchor_y)
+        x = rows[5:6] - anchor_x
+        y = rows[6:7] - anchor_y
         sources = source_rows(rows)
-        left = spread(
-            column, [sources[f] for f in fields] + [sources[5 + f] for f in fields], columns
-        )
+        pair = (sources[4], sources[9])
+        on_x = [jnp.where(x == at, v, 0.0) for at in (0.0, cells_x - 1.0) for v in pair]
+        on_y = [jnp.where(y == at, v, 0.0) for at in (0.0, cells_y - 1.0) for v in pair]
+        left = jnp.concatenate([spread(y, on_x, cells_y), spread(x, on_y, cells_x)], axis=0)
         acc[...] += lax.dot_general(
             left, depth_onehot(rows, depth), TRANSPOSED, preferred_element_type=F32
         )
@@ -252,22 +254,37 @@
     return got[:number] + got[number:]
 
 
-def deposit_kernel(cells_x, cells_y, step, fields, with_tables, *refs):
+def deposit_kernel(cells_x, cells_y, step, steps, *refs):
     columns = cells_x * cells_y
-    if with_tables:
+    if steps[0] == 0:
         stay, dep, state, where_to, acc = refs
+        before = None
         total = stay.shape[1]
         state[:, :total] = stay[0:5, :]
         where_to[:, :total] = stay[5:8, :].astype(I32)
     else:
-        stay, _, dep, acc = refs
-    deposit_fields(fields, *anchors(cells_x, cells_y), cells_y, step, stay, acc)
-    n = len(fields)
-    for f in range(n):
+        stay, before, _, dep, acc = refs
+    anchor_x, anchor_y = anchors(cells_x, cells_y)
+    acc[...] = jnp.zeros(acc.shape, F32)
+
+    def one(k, carry):
+        rows = stay[:, pl.ds(pl.multiple_of(k * step, step), step)]
+        column = (rows[5:6] - anchor_x) * cells_y + (rows[6:7] - anchor_y)
+        acc[...] += lax.dot_general(
+            spread(column, source_rows(rows), columns),
+            depth_onehot(rows, dep.shape[3]),
+            TRANSPOSED,
+            preferred_element_type=F32,
+        )
+        return carry
+
+    lax.fori_loop(*steps, one, 0)
+    for f in range(5):
         for x in range(cells_x):
             high = slice((f * cells_x + x) * cells_y, (f * cells_x + x + 1) * cells_y)
-            low = slice(n * columns + high.start, n * columns + high.stop)
-            dep[f, x] = acc[high, :] + acc[low, :]
+            low = slice(5 * columns + high.start, 5 * columns + high.stop)
+            value = acc[high, :] + acc[low, :]
+            dep[f, x] = value if before is None else before[f, x] + value
 
 
 def arrivals(rows, along, number, depth):
@@ -293,7 +310,7 @@
     row = iota((cells_y, depth), 0)
 
     def side(x):
-        value = partial[x] + jnp.where(row == 0, planes[0, 4, x : x + 1, :], 0.0)
+        value = partial[min(x, 1)] + jnp.where(row == 0, planes[0, 4, x : x + 1, :], 0.0)
         return value + jnp.where(row == cells_y - 1, planes[1, 4, x : x + 1, :], 0.0)
 
     up = message(own[1], side(cells_x - 1), parts[0][3], parts[1][3])
@@ -302,11 +319,11 @@
 
 
 def update_kernel(
-    cells_x, cells_y, y_even, y_odd, x_even, x_odd, density, momentum, partial, dep01, dep23,
+    cells_x, cells_y, y_even, y_odd, x_even, x_odd, density, momentum, energy, dep,
     planes_y, halo_y, leaving, state_in, where_in,
     rho_out, impulse, energy_out, fastest, state, where_to, pressure, planes_x,
 ):
-    depth = partial.shape[2]
+    depth = energy.shape[2]
     _, anchor_y = anchors(cells_x, cells_y)
     scale = ADIABATIC_INDEX - 1.0
     shape = (cells_y, depth)
@@ -339,7 +356,7 @@
         return value + jnp.where(row == cells_y - 1, planes_y[1, f, x : x + 1, :], 0.0)
 
     for x in range(cells_x):
-        value = with_planes(4, x, partial[x])
+        value = with_planes(4, x, energy[x] + dep[4, x])
         energy_out[x] = value
         pressure[x + 1] = scale * value
     top = jnp.zeros(shape, F32)
@@ -354,12 +371,11 @@
         after = jnp.where(lane == depth - 1, 0.0, pltpu.roll(here, depth - 1, 1))
         before = jnp.where(lane == 0, 0.0, pltpu.roll(here, 1, 1))
         grad_z = 0.5 * (after - before)
-        rho = with_planes(0, x, density[x] + dep01[0, x])
+        rho = with_planes(0, x, density[x] + dep[0, x])
         rho_out[x] = rho
         largest = jnp.zeros(shape, F32)
-        deposits = (dep01[1, x], dep23[0, x], dep23[1, x])
         for k, grad in enumerate((grad_x, grad_y, grad_z)):
-            value = with_planes(1 + k, x, momentum[k, x] + deposits[k]) - KICK * grad
+            value = with_planes(1 + k, x, momentum[k, x] + dep[1 + k, x]) - KICK * grad
             impulse[k, x] = value
             largest = jnp.maximum(largest, jnp.abs(value))
         wave = largest / rho + jnp.sqrt(ADIABATIC_INDEX * here / rho)
@@ -422,14 +438,14 @@
             sds((8, rows), F32),
             sds((2, 8, capacity), F32),
             sds((4, cells_x, depth), F32),
-            sds(energy.shape, F32),
+            sds((2, cells_y, depth), F32),
         ),
         scratch=(
             VMEM((8, rows), F32),
             VMEM((chunks, 8, LANES), F32),
             pltpu.SMEM((chunks, LANES), I32),
             VMEM((4, capacity // LANES + 1, 8, LANES), F32),
-            VMEM((2 * columns, depth), F32),
+            VMEM((4 * (cells_x + cells_y), depth), F32),
             pltpu.SemaphoreType.DMA,
         ),
         name="prep",
@@ -446,28 +462,30 @@
     )
     y_even, y_odd = swap("gy", even, odd)
     slots = rows + 4 * capacity
-    two = sds((2, cells_x, cells_y, depth), F32)
-    sums = (VMEM((4 * columns, depth), F32),)
-    dep01, state, where_to = call(
-        functools.partial(deposit_kernel, cells_x, cells_y, step, (0, 1), True),
-        (two, sds((5, slots), F32), sds((3, slots), I32)),
+    five = sds((5, cells_x, cells_y, depth), F32)
+    sums = (VMEM((10 * columns, depth), F32),)
+    steps = rows // step
+    middle = steps * 5 // 8
+    dep, state, where_to = call(
+        functools.partial(deposit_kernel, cells_x, cells_y, step, (0, middle)),
+        (five, sds((5, slots), F32), sds((3, slots), I32)),
         scratch=sums,
-        name="deposit01",
+        name="deposit1",
     )(stay)
     even, odd, planes_y, halo_y = call(
         functools.partial(relay_kernel, cells_x, cells_y),
         (parcels, parcels, sds((2, 5, cells_x, depth), F32), sds((2, cells_x, depth), F32)),
         in_specs=[whole] * 5 + [pl.BlockSpec(memory_space=pl.ANY)],
         name="relay",
-    )(y_even, y_odd, partial, own, leaving, dep01)
+    )(y_even, y_odd, partial, own, leaving, dep)
     x_even, x_odd = swap("gx", even, odd)
-    (dep23,) = call(
-        functools.partial(deposit_kernel, cells_x, cells_y, step, (2, 3), False),
-        (two,),
+    (dep,) = call(
+        functools.partial(deposit_kernel, cells_x, cells_y, step, (middle, steps)),
+        (five,),
         scratch=sums,
-        in_specs=[whole, pl.BlockSpec(memory_space=pl.ANY)],
-        name="deposit23",
-    )(stay, halo_y)
+        in_specs=[whole, whole, pl.BlockSpec(memory_space=pl.ANY)],
+        name="deposit2",
+    )(stay, dep, halo_y)
     last = rows // (4 * capacity)
     rho, impulse, energy_out, top, state, where_to = call(
         functools.partial(update_kernel, cells_x, cells_y),
@@ -483,20 +501,20 @@
             VMEM((cells_x + 2, cells_y, depth), F32),
             VMEM((2, 5, cells_y, depth), F32),
         ),
-        in_specs=[whole] * 12 + [pl.BlockSpec(memory_space=pl.ANY)] * 2,
+        in_specs=[whole] * 11 + [pl.BlockSpec(memory_space=pl.ANY)] * 2,
         out_specs=(whole,) * 4
         + (
             pl.BlockSpec((5, 4 * capacity), lambda i: (0, last)),
             pl.BlockSpec((3, 4 * capacity), lambda i: (0, last)),
         ),
-        aliases={12: 4, 13: 5},
+        aliases={11: 4, 12: 5},
         grid=(1,),
         name="update",
     )(
-        y_even, y_odd, x_even, x_odd, density, momentum, partial, dep01, dep23,
+        y_even, y_odd, x_even, x_odd, density, momentum, energy, dep,
         planes_y, halo_y, leaving, state, where_to,
     )
-    fastest = jnp.max(lax.all_to_all(top, ("gx", "gy"), 0, 0, tiled=True))
+    fastest = jnp.max(lax.all_to_all(top, ("gx", "gy"), 0, 0, tiled=True), axis=0)[0]
     return rho, impulse, energy_out, state, where_to, COURANT / fastest
 
 

time: 64.2 us -> 62.2 us (0.969)
    pallas_call x1, Pallas kernels: 7.11 us -> 5.74 us  [on_device(): call(functools.partial(prep_kernel, cells_x, cells_y, step), (parcels, pa...]
    pallas_call x2, Pallas kernels: 12.4 us -> 13.3 us  [the longest x1 8.21 us: on_device(): call(functools.partial(deposit_kernel, cells_x, cells_y, step, (0, middle...]
  transfers between devices with their start and end apart: 4 -> 4, of which waited for: 0 -> 0; matrix products, arithmetic and copies ran while one was open for 0% -> 0% of each run, Pallas kernels for 19% -> 21%
where the time goes in v6:
time: 62.2 us; the launch traced here: 62 us
  blocking collectives  28.8 us (46%)
  Pallas kernels  21.6 us (35%)
  starting transfers between devices  7.25 us (12%)
  between operations  2.63 us (4%)
  local copies, waits for them, and re-layouts  1.47 us (2%)
    all_to_all x1, blocking collectives, on_device(): lax.all_to_all(top, ('gx', 'gy'), 0, 0, tiled=True)  28.8 us
    pallas_call x1, Pallas kernels, on_device(): call(functools.partial(deposit_kernel, cells_x, cells_y, step, (0, middle...  8.21 us
    pallas_call x1, Pallas kernels, on_device(): call(functools.partial(prep_kernel, cells_x, cells_y, step), (parcels, pa...  5.74 us
    pallas_call x1, Pallas kernels, on_device(): call(functools.partial(deposit_kernel, cells_x, cells_y, step, (middle, s...  5.06 us
    ppermute x2, starting transfers between devices, swap(): lax.ppermute(odd, axis, pairs(1))  3.85 us
    ppermute x2, starting transfers between devices, swap(): lax.ppermute(even, axis, pairs(0))  3.4 us
    pallas_call x1, Pallas kernels, on_device(): call(functools.partial(update_kernel, cells_x, cells_y), (sds(density.sha...  1.82 us
    unnamed x14, local copies, waits for them, and re-layouts  1.47 us
  transfers between devices with their start and end apart: 4, of which 0 were waited for; matrix products, arithmetic and copies ran while one was open for 0% of the time, Pallas kernels for 21%

profile of v6, /device:TPU:1, one launch (start us, length us, event | category | flops | bytes accessed | tf_op | source)
XLA Modules:
  0.0 62.0 jit_solution(1262571307067569524)
XLA Ops:
  1.3 0.9 %copy-done.4 = s32[3,8192]{1,0:T(4,128)S(1)} copy-done((s32[3,8192]{1,0:T(4,128)S(1)}, s32[3,8192]{1,0:T(4,128)}, u32[]{:S(2)}) %copy-start.4) | copy-done | bytes 98328
  2.2 0.4 rank.1
  2.6 0.5 copy-done
  3.1 0.0 copy-done.3
  3.2 0.0 copy-done.5
  3.2 5.7 %prep.1 = (f32[8,1280]{1,0:T(8,128)S(1)}, f32[8,1280]{1,0:T(8,128)S(1)}, f32[8,8192]{1,0:T(8,128)S(1)}, f32[2,8,512]{2,1,0:T(8,128)S(1)}, f32[4,16,256]{2,1,0:T(8,128)S(1)}, /*index=5*/f32[2,16,256]{2,1,0:T(8,128)S(1)}) custom-call(f32[64,128]{1,0:T(8,128)S(1)} %bitcast.8, f32[64,128]{1,0:T(8,128)S(1)} %bitcast.9, f32[3,8192]{1,0:T(4,128)S(1)} %copy-done.3, ...), custom_call_target="tpu_custom_call" | custom-call | tf_op jit(solution)/shard_map/prep/pallas_call | solution.py:433
  8.9 2.1 %collective-permute-start = (f32[8,1280]{1,0:T(8,128)S(1)}, f32[8,1280]{1,0:T(8,128)S(1)}, u32[]{:S(2)}, u32[]{:S(2)}) collective-permute-start(f32[8,1280]{1,0:T(8,128)S(1)} %get-tuple-element.33), channel_id=1, source_target_pairs={{0,1},{1,0},{2,3},{3,2},{4,5},{5,4},{6,7},{7,6},{8,9},{9,8},{10,11... | collective-permute-start | bytes 122888 | tf_op jit(solution)/shard_map/ppermute | solution.py:409
  11.0 0.7 %collective-permute-start.1 = (f32[8,1280]{1,0:T(8,128)S(1)}, f32[8,1280]{1,0:T(8,128)S(1)}, u32[]{:S(2)}, u32[]{:S(2)}) collective-permute-start(f32[8,1280]{1,0:T(8,128)S(1)} %get-tuple-element.34), channel_id=1, source_target_pairs={{1,2},{2,1},{3,4},{4,3},{5,6},{6,5},{7,8},{8,7},{9,10},{10,9},{11,... | collective-permute-start | bytes 122888 | tf_op jit(solution)/shard_map/ppermute | solution.py:409
  11.7 8.2 %deposit1.1 = (f32[5,16,16,256]{3,2,1,0:T(8,128)S(1)}, f32[5,10240]{1,0:T(8,128)}, s32[3,10240]{1,0:T(4,128)}) custom-call(f32[8,8192]{1,0:T(8,128)S(1)} %get-tuple-element.38.refs_0_), custom_call_target="tpu_custom_call" | custom-call | tf_op jit(solution)/shard_map/deposit1/pallas_call | solution.py:469
  19.9 0.0 collective-permute-done.in_even.y_even
  19.9 0.0 collective-permute-done.1.in_odd.y_odd
  19.9 0.4 relay.1
  20.3 1.3 %collective-permute-start.2 = (f32[8,1280]{1,0:T(8,128)S(1)}, f32[8,1280]{1,0:T(8,128)S(1)}, u32[]{:S(2)}, u32[]{:S(2)}) collective-permute-start(f32[8,1280]{1,0:T(8,128)S(1)} %get-tuple-element.40), channel_id=1, source_target_pairs={{0,32},{32,0},{64,96},{96,64},{128,160},{160,128},{192,224},{224,1... | collective-permute-start | bytes 122888 | tf_op jit(solution)/shard_map/ppermute | solution.py:409
  21.6 3.2 %collective-permute-start.3 = (f32[8,1280]{1,0:T(8,128)S(1)}, f32[8,1280]{1,0:T(8,128)S(1)}, u32[]{:S(2)}, u32[]{:S(2)}) collective-permute-start(f32[8,1280]{1,0:T(8,128)S(1)} %get-tuple-element.41), channel_id=1, source_target_pairs={{32,64},{64,32},{96,128},{128,96},{160,192},{192,160},{33,65},{65,... | collective-permute-start | bytes 122888 | tf_op jit(solution)/shard_map/ppermute | solution.py:409
  24.8 0.0 copy-start.1
  24.8 0.0 copy-start.2
  24.8 5.1 %deposit2.1.dep = f32[5,16,16,256]{3,2,1,0:T(8,128)S(1)} custom-call(f32[8,8192]{1,0:T(8,128)S(1)} %get-tuple-element.38.refs_0_, f32[5,16,16,256]{3,2,1,0:T(8,128)S(1)} %get-tuple-element.39._.refs_1_, f32[2,16,256]{2,1,0:T(8,128)S(1)} %get-tuple-element.42.refs_2_.halo_y), custom_call_target="tpu_custom_call" | custom-call | tf_op jit(solution)/shard_map/deposit2/pallas_call | solution.py:482
  29.9 0.0 collective-permute-done.2.x_even
  29.9 0.0 collective-permute-done.3.x_odd
  29.9 0.0 copy-done.1
  29.9 0.0 copy-done.2
  29.9 1.8 %update.1 = (f32[16,16,256]{2,1,0:T(8,128)}, f32[3,16,16,256]{3,2,1,0:T(8,128)}, f32[16,16,256]{2,1,0:T(8,128)}, f32[256,128]{1,0:T(8,128)S(1)}, f32[5,10240]{1,0:T(8,128)}, /*index=5*/s32[3,10240]{1,0:T(4,128)}) custom-call(f32[8,1280]{1,0:T(8,128)S(1)} %collective-permute-done.in_even.y_even, ...), custom_call_target="tpu_custom_call", output_to_operand_aliasing={{4}: (11, {}), {5}: (12, {})} | custom-call | tf_op jit(solution)/shard_map/update/pallas_call | solution.py:490
  31.7 28.8 %all_to_all.9 = f32[256,1,128]{2,1,0:T(1,128)S(1)} all-to-all(f32[256,1,128]{2,1,0:T(1,128)S(1)} %bitcast.7), channel_id=1, replica_groups=mesh['gx'=8,'gy'=32] {'gx','gy'}, dimensions={0} | all-to-all | bytes 262144 | tf_op jit(solution)/shard_map/all_to_all | solution.py:517
  60.5 0.3 reduce_max.9
  (6 shorter events, 0.0 us)
Async XLA Ops:
  1.3 0.9 %copy-start.4 = (s32[3,8192]{1,0:T(4,128)S(1)}, s32[3,8192]{1,0:T(4,128)}, u32[]{:S(2)}) copy-start(s32[3,8192]{1,0:T(4,128)} %cell.3) | copy-start | bytes 294916
  2.2 0.9 %copy-start = (f32[16,16,256]{2,1,0:T(8,128)S(1)}, f32[16,16,256]{2,1,0:T(8,128)}, u32[]{:S(2)}) copy-start(f32[16,16,256]{2,1,0:T(8,128)} %energy.3) | copy-start | bytes 786436
  2.2 1.0 %copy-start.3 = (f32[3,8192]{1,0:T(4,128)S(1)}, f32[3,8192]{1,0:T(4,128)}, u32[]{:S(2)}) copy-start(f32[3,8192]{1,0:T(4,128)} %vel.1) | copy-start | bytes 294916
  2.2 1.0 %copy-start.5 = (f32[8192]{0:T(1024)S(1)}, f32[8192]{0:T(1024)}, u32[]{:S(2)}) copy-start(f32[8192]{0:T(1024)} %param.11) | copy-start | bytes 98308
  2.2 1.0 %copy-start.6 = (f32[8192]{0:T(1024)S(1)}, f32[8192]{0:T(1024)}, u32[]{:S(2)}) copy-start(f32[8192]{0:T(1024)} %param.13) | copy-start | bytes 98308
  8.9 11.0 %collective-permute-start = (f32[8,1280]{1,0:T(8,128)S(1)}, f32[8,1280]{1,0:T(8,128)S(1)}, u32[]{:S(2)}, u32[]{:S(2)}) collective-permute-start(f32[8,1280]{1,0:T(8,128)S(1)} %get-tuple-element.33), channel_id=1, source_target_pairs={{0,1},{1,0},{2,3},{3,2},{4,5},{5,4},{6,7},{7,6},{8,9},{9,8},{10,11... | collective-permute-start | bytes 122888 | tf_op jit(solution)/shard_map/ppermute | solution.py:409
  11.0 8.9 %collective-permute-start.1 = (f32[8,1280]{1,0:T(8,128)S(1)}, f32[8,1280]{1,0:T(8,128)S(1)}, u32[]{:S(2)}, u32[]{:S(2)}) collective-permute-start(f32[8,1280]{1,0:T(8,128)S(1)} %get-tuple-element.34), channel_id=1, source_target_pairs={{1,2},{2,1},{3,4},{4,3},{5,6},{6,5},{7,8},{8,7},{9,10},{10,9},{11,... | collective-permute-start | bytes 122888 | tf_op jit(solution)/shard_map/ppermute | solution.py:409
  20.3 9.6 %collective-permute-start.2 = (f32[8,1280]{1,0:T(8,128)S(1)}, f32[8,1280]{1,0:T(8,128)S(1)}, u32[]{:S(2)}, u32[]{:S(2)}) collective-permute-start(f32[8,1280]{1,0:T(8,128)S(1)} %get-tuple-element.40), channel_id=1, source_target_pairs={{0,32},{32,0},{64,96},{96,64},{128,160},{160,128},{192,224},{224,1... | collective-permute-start | bytes 122888 | tf_op jit(solution)/shard_map/ppermute | solution.py:409
  21.6 8.3 %collective-permute-start.3 = (f32[8,1280]{1,0:T(8,128)S(1)}, f32[8,1280]{1,0:T(8,128)S(1)}, u32[]{:S(2)}, u32[]{:S(2)}) collective-permute-start(f32[8,1280]{1,0:T(8,128)S(1)} %get-tuple-element.41), channel_id=1, source_target_pairs={{32,64},{64,32},{96,128},{128,96},{160,192},{192,160},{33,65},{65,... | collective-permute-start | bytes 122888 | tf_op jit(solution)/shard_map/ppermute | solution.py:409
  24.8 5.1 %copy-start.1 = (f32[3,16,16,256]{3,2,1,0:T(8,128)S(1)}, f32[3,16,16,256]{3,2,1,0:T(8,128)}, u32[]{:S(2)}) copy-start(f32[3,16,16,256]{3,2,1,0:T(8,128)} %momentum.1) | copy-start | bytes 2359300
  24.8 5.1 %copy-start.2 = (f32[16,16,256]{2,1,0:T(8,128)S(1)}, f32[16,16,256]{2,1,0:T(8,128)}, u32[]{:S(2)}) copy-start(f32[16,16,256]{2,1,0:T(8,128)} %density.1) | copy-start | bytes 786436

commit v7 on v6

--- a/solution.py
+++ b/solution.py
@@ -6,6 +6,7 @@
 from jax.experimental import pallas as pl
 from jax.experimental.pallas import tpu as pltpu
 from jax.sharding import PartitionSpec as P
+
 
 ADIABATIC_INDEX = 1.4
 KICK = 0.25
@@ -257,34 +258,31 @@
 def deposit_kernel(cells_x, cells_y, step, steps, *refs):
     columns = cells_x * cells_y
     if steps[0] == 0:
-        stay, dep, state, where_to, acc = refs
-        before = None
+        stay, dep, state, where_to = refs
         total = stay.shape[1]
         state[:, :total] = stay[0:5, :]
         where_to[:, :total] = stay[5:8, :].astype(I32)
+        dep[...] = jnp.zeros(dep.shape, F32)
     else:
-        stay, before, _, dep, acc = refs
+        stay, before, _, dep = refs
+        dep[...] = before[...]
     anchor_x, anchor_y = anchors(cells_x, cells_y)
-    acc[...] = jnp.zeros(acc.shape, F32)
 
     def one(k, carry):
         rows = stay[:, pl.ds(pl.multiple_of(k * step, step), step)]
         column = (rows[5:6] - anchor_x) * cells_y + (rows[6:7] - anchor_y)
-        acc[...] += lax.dot_general(
-            spread(column, source_rows(rows), columns),
-            depth_onehot(rows, dep.shape[3]),
+        sources = source_rows(rows)
+        onehot = depth_onehot(rows, dep.shape[1])
+        left = [spread(column, half, columns) for half in (sources[:5], sources[5:])]
+        dep[...] += lax.dot_general(
+            jnp.concatenate(left, axis=1),
+            jnp.concatenate([onehot, onehot], axis=1),
             TRANSPOSED,
             preferred_element_type=F32,
         )
         return carry
 
     lax.fori_loop(*steps, one, 0)
-    for f in range(5):
-        for x in range(cells_x):
-            high = slice((f * cells_x + x) * cells_y, (f * cells_x + x + 1) * cells_y)
-            low = slice(5 * columns + high.start, 5 * columns + high.stop)
-            value = acc[high, :] + acc[low, :]
-            dep[f, x] = value if before is None else before[f, x] + value
 
 
 def arrivals(rows, along, number, depth):
@@ -321,7 +319,8 @@
 def update_kernel(
     cells_x, cells_y, y_even, y_odd, x_even, x_odd, density, momentum, energy, dep,
     planes_y, halo_y, leaving, state_in, where_in,
-    rho_out, impulse, energy_out, fastest, state, where_to, pressure, planes_x,
+    rho_there, impulse_there, energy_there, fastest, state, where_to,
+    pressure, planes_x, rho_out, impulse, energy_out, sems,
 ):
     depth = energy.shape[2]
     _, anchor_y = anchors(cells_x, cells_y)
@@ -359,6 +358,9 @@
         value = with_planes(4, x, energy[x] + dep[4, x])
         energy_out[x] = value
         pressure[x + 1] = scale * value
+    leaves = [pltpu.make_async_copy(energy_out, energy_there, sems.at[0])]
+    leaves[0].start()
+    group = 4
     top = jnp.zeros(shape, F32)
     for x in range(cells_x):
         here = pressure[x + 1]
@@ -380,12 +382,20 @@
             largest = jnp.maximum(largest, jnp.abs(value))
         wave = largest / rho + jnp.sqrt(ADIABATIC_INDEX * here / rho)
         top = jnp.maximum(top, wave)
+        if (x + 1) % group == 0:
+            some = pl.ds(x + 1 - group, group)
+            for here, there in (
+                (rho_out.at[some], rho_there.at[some]),
+                (impulse.at[:, some], impulse_there.at[:, some]),
+            ):
+                leaves.append(pltpu.make_async_copy(here, there, sems.at[len(leaves)]))
+                leaves[-1].start()
     fastest[...] = jnp.broadcast_to(jnp.max(top, axis=(0, 1), keepdims=True), fastest.shape)
-
-
-def call(
-    kernel, outs, scratch=(), out_specs=None, in_specs=None, aliases=None, name=None, vmem=48, **extra
-):
+    for leave in leaves:
+        leave.wait()
+
+
+def call(kernel, outs, scratch=(), out_specs=None, in_specs=None, aliases=None, vmem=48, **extra):
     if in_specs is not None:
         extra["in_specs"] = in_specs
     if out_specs is not None:
@@ -396,7 +406,6 @@
         scratch_shapes=list(scratch),
         input_output_aliases=aliases or {},
         compiler_params=pltpu.CompilerParams(vmem_limit_bytes=vmem * 1024 * 1024),
-        name=name,
         **extra,
     )
 
@@ -406,7 +415,9 @@
     pairs = lambda first: [
         p for i in range(first, size - 1, 2) for p in ((i, i + 1), (i + 1, i))
     ]
-    return lax.ppermute(even, axis, pairs(0)), lax.ppermute(odd, axis, pairs(1))
+    odd = lax.ppermute(odd, axis, pairs(1))
+    even = lax.ppermute(even, axis, pairs(0))
+    return even, odd
 
 
 def on_device(
@@ -427,7 +438,6 @@
         (dense, dense, sds((chunks, LANES), I32), sds((4, 3, chunks, LANES), F32)),
         scratch=(VMEM((chunks, LANES), I32), VMEM((chunks, LANES), I32)),
         in_specs=[pl.BlockSpec(memory_space=pltpu.SMEM), whole],
-        name="rank",
         cost_estimate=pl.CostEstimate(flops=10**9, bytes_accessed=10**6, transcendentals=0),
     )(parcel_count, parcel_cell)
     even, odd, stay, own, leaving, partial = call(
@@ -448,7 +458,6 @@
             VMEM((4 * (cells_x + cells_y), depth), F32),
             pltpu.SemaphoreType.DMA,
         ),
-        name="prep",
     )(
         parcel_mass.reshape(chunks, LANES),
         parcel_temp.reshape(chunks, LANES),
@@ -462,30 +471,26 @@
     )
     y_even, y_odd = swap("gy", even, odd)
     slots = rows + 4 * capacity
-    five = sds((5, cells_x, cells_y, depth), F32)
-    sums = (VMEM((10 * columns, depth), F32),)
+    five = sds((5 * columns, depth), F32)
     steps = rows // step
     middle = steps * 5 // 8
     dep, state, where_to = call(
         functools.partial(deposit_kernel, cells_x, cells_y, step, (0, middle)),
         (five, sds((5, slots), F32), sds((3, slots), I32)),
-        scratch=sums,
-        name="deposit1",
     )(stay)
     even, odd, planes_y, halo_y = call(
         functools.partial(relay_kernel, cells_x, cells_y),
         (parcels, parcels, sds((2, 5, cells_x, depth), F32), sds((2, cells_x, depth), F32)),
         in_specs=[whole] * 5 + [pl.BlockSpec(memory_space=pl.ANY)],
-        name="relay",
     )(y_even, y_odd, partial, own, leaving, dep)
     x_even, x_odd = swap("gx", even, odd)
     (dep,) = call(
         functools.partial(deposit_kernel, cells_x, cells_y, step, (middle, steps)),
         (five,),
-        scratch=sums,
         in_specs=[whole, whole, pl.BlockSpec(memory_space=pl.ANY)],
-        name="deposit2",
+        aliases={1: 0},
     )(stay, dep, halo_y)
+    dep = dep.reshape(5, cells_x, cells_y, depth)
     last = rows // (4 * capacity)
     rho, impulse, energy_out, top, state, where_to = call(
         functools.partial(update_kernel, cells_x, cells_y),
@@ -500,16 +505,20 @@
         scratch=(
             VMEM((cells_x + 2, cells_y, depth), F32),
             VMEM((2, 5, cells_y, depth), F32),
+            VMEM(density.shape, F32),
+            VMEM(momentum.shape, F32),
+            VMEM(energy.shape, F32),
+            pltpu.SemaphoreType.DMA((1 + 2 * (cells_x // 4),)),
         ),
         in_specs=[whole] * 11 + [pl.BlockSpec(memory_space=pl.ANY)] * 2,
-        out_specs=(whole,) * 4
+        out_specs=(pl.BlockSpec(memory_space=pl.ANY),) * 3
+        + (whole,)
         + (
             pl.BlockSpec((5, 4 * capacity), lambda i: (0, last)),
             pl.BlockSpec((3, 4 * capacity), lambda i: (0, last)),
         ),
         aliases={11: 4, 12: 5},
         grid=(1,),
-        name="update",
     )(
         y_even, y_odd, x_even, x_odd, density, momentum, energy, dep,
         planes_y, halo_y, leaving, state, where_to,

time: 62.2 us -> 62.3 us (level)
  no operation moved by 1% of the time
where the time goes in v7:
time: 62.3 us; the launch traced here: 62.1 us
  blocking collectives  28.7 us (46%)
  Pallas kernels  21.7 us (35%)
  starting transfers between devices  7.26 us (12%)
  between operations  2.63 us (4%)
  local copies, waits for them, and re-layouts  1.47 us (2%)
    all_to_all x1, blocking collectives, on_device(): lax.all_to_all(top, ('gx', 'gy'), 0, 0, tiled=True)  28.7 us
    pallas_call x1, Pallas kernels, on_device(): call(functools.partial(deposit_kernel, cells_x, cells_y, step, (0, middle...  7.98 us
    pallas_call x1, Pallas kernels, on_device(): call(functools.partial(prep_kernel, cells_x, cells_y, step), (parcels, pa...  5.74 us
    pallas_call x1, Pallas kernels, on_device(): call(functools.partial(deposit_kernel, cells_x, cells_y, step, (middle, s...  4.87 us
    ppermute x2, starting transfers between devices, swap(): odd = lax.ppermute(odd, axis, pairs(1))  3.87 us
    ppermute x2, starting transfers between devices, swap(): even = lax.ppermute(even, axis, pairs(0))  3.39 us
    pallas_call x1, Pallas kernels, on_device(): call(functools.partial(update_kernel, cells_x, cells_y), (sds(density.sha...  2.38 us
    unnamed x14, local copies, waits for them, and re-layouts  1.47 us
  transfers between devices with their start and end apart: 4, of which 0 were waited for; matrix products, arithmetic and copies ran while one was open for 0% of the time, Pallas kernels for 21%

profile of v7, /device:TPU:1, one launch (start us, length us, event | category | flops | bytes accessed | tf_op | source)
XLA Modules:
  0.0 62.1 jit_solution(6297707663604083993)
XLA Ops:
  1.3 0.0 copy-start.4
  1.3 0.9 %copy-done.4 = s32[3,8192]{1,0:T(4,128)S(1)} copy-done((s32[3,8192]{1,0:T(4,128)S(1)}, s32[3,8192]{1,0:T(4,128)}, u32[]{:S(2)}) %copy-start.4) | copy-done | bytes 98328
  2.2 0.4 shard_map.127
  2.6 0.5 copy-done
  3.1 0.0 copy-done.3
  3.2 0.0 copy-done.5
  3.2 0.0 copy-done.6
  3.2 5.7 %shard_map.128 = (f32[8,1280]{1,0:T(8,128)S(1)}, f32[8,1280]{1,0:T(8,128)S(1)}, f32[8,8192]{1,0:T(8,128)S(1)}, f32[2,8,512]{2,1,0:T(8,128)S(1)}, f32[4,16,256]{2,1,0:T(8,128)S(1)}, /*index=5*/f32[2,16,256]{2,1,0:T(8,128)S(1)}) custom-call(f32[64,128]{1,0:T(8,128)S(1)} %bitcast.10, f32[64,128]{1,0:T(8,128)S(1)} %bitcast.11, f32[3,8192]{1,0:T(4,128)S(1)} %copy-done.3, ...), custom_call_target="tpu_custom_call" | custom-call | tf_op jit(solution)/shard_map/pallas_call | solution.py:443
  8.9 2.1 %collective-permute-start = (f32[8,1280]{1,0:T(8,128)S(1)}, f32[8,1280]{1,0:T(8,128)S(1)}, u32[]{:S(2)}, u32[]{:S(2)}) collective-permute-start(f32[8,1280]{1,0:T(8,128)S(1)} %get-tuple-element.33), channel_id=1, source_target_pairs={{0,1},{1,0},{2,3},{3,2},{4,5},{5,4},{6,7},{7,6},{8,9},{9,8},{10,11... | collective-permute-start | bytes 122888 | tf_op jit(solution)/shard_map/ppermute | solution.py:419
  11.0 0.7 %collective-permute-start.1 = (f32[8,1280]{1,0:T(8,128)S(1)}, f32[8,1280]{1,0:T(8,128)S(1)}, u32[]{:S(2)}, u32[]{:S(2)}) collective-permute-start(f32[8,1280]{1,0:T(8,128)S(1)} %get-tuple-element.34), channel_id=1, source_target_pairs={{1,2},{2,1},{3,4},{4,3},{5,6},{6,5},{7,8},{8,7},{9,10},{10,9},{11,... | collective-permute-start | bytes 122888 | tf_op jit(solution)/shard_map/ppermute | solution.py:418
  11.7 8.0 %shard_map.129 = (f32[1280,256]{1,0:T(8,128)S(1)}, f32[5,10240]{1,0:T(8,128)}, s32[3,10240]{1,0:T(4,128)}) custom-call(f32[8,8192]{1,0:T(8,128)S(1)} %get-tuple-element.38.refs_0_), custom_call_target="tpu_custom_call" | custom-call | tf_op jit(solution)/shard_map/pallas_call | solution.py:477
  19.7 0.0 collective-permute-done.in_even.y_even
  19.7 0.0 collective-permute-done.1.in_odd.y_odd
  19.7 0.4 shard_map.130
  20.1 1.3 %collective-permute-start.2 = (f32[8,1280]{1,0:T(8,128)S(1)}, f32[8,1280]{1,0:T(8,128)S(1)}, u32[]{:S(2)}, u32[]{:S(2)}) collective-permute-start(f32[8,1280]{1,0:T(8,128)S(1)} %get-tuple-element.40), channel_id=1, source_target_pairs={{0,32},{32,0},{64,96},{96,64},{128,160},{160,128},{192,224},{224,1... | collective-permute-start | bytes 122888 | tf_op jit(solution)/shard_map/ppermute | solution.py:419
  21.3 3.2 %collective-permute-start.3 = (f32[8,1280]{1,0:T(8,128)S(1)}, f32[8,1280]{1,0:T(8,128)S(1)}, u32[]{:S(2)}, u32[]{:S(2)}) collective-permute-start(f32[8,1280]{1,0:T(8,128)S(1)} %get-tuple-element.41), channel_id=1, source_target_pairs={{32,64},{64,32},{96,128},{128,96},{160,192},{192,160},{33,65},{65,... | collective-permute-start | bytes 122888 | tf_op jit(solution)/shard_map/ppermute | solution.py:418
  24.6 0.0 copy-start.1
  24.6 0.0 copy-start.2
  24.6 4.9 %shard_map.131 = f32[1280,256]{1,0:T(8,128)S(1)} custom-call(f32[8,8192]{1,0:T(8,128)S(1)} %get-tuple-element.38.refs_0_, f32[1280,256]{1,0:T(8,128)S(1)} %get-tuple-element.39._.refs_1_, f32[2,16,256]{2,1,0:T(8,128)S(1)} %get-tuple-element.42.refs_2_.halo_y), custom_call_target="tpu_custom_call", output_to_operand_aliasing={{}: (1, {})} | custom-call | tf_op jit(solution)/shard_map/pallas_call | solution.py:487
  29.5 0.0 collective-permute-done.2.x_even
  29.5 0.0 collective-permute-done.3.x_odd
  29.5 2.4 %shard_map.132 = (f32[16,16,256]{2,1,0:T(8,128)}, f32[3,16,16,256]{3,2,1,0:T(8,128)}, f32[16,16,256]{2,1,0:T(8,128)}, f32[256,128]{1,0:T(8,128)S(1)}, f32[5,10240]{1,0:T(8,128)}, /*index=5*/s32[3,10240]{1,0:T(4,128)}) custom-call(f32[8,1280]{1,0:T(8,128)S(1)} %collective-permute-done.in_even.y_even, ...), custom_call_target="tpu_custom_call", output_to_operand_aliasing={{4}: (11, {}), {5}: (12, {})} | custom-call | tf_op jit(solution)/shard_map/pallas_call | solution.py:495
  31.9 28.7 %all_to_all.9 = f32[256,1,128]{2,1,0:T(1,128)S(1)} all-to-all(f32[256,1,128]{2,1,0:T(1,128)S(1)} %bitcast.9), channel_id=1, replica_groups=mesh['gx'=8,'gy'=32] {'gx','gy'}, dimensions={0} | all-to-all | bytes 262144 | tf_op jit(solution)/shard_map/all_to_all | solution.py:526
  60.6 0.3 reduce_max.9
  (6 shorter events, 0.0 us)
Async XLA Ops:
  1.3 0.9 %copy-start.4 = (s32[3,8192]{1,0:T(4,128)S(1)}, s32[3,8192]{1,0:T(4,128)}, u32[]{:S(2)}) copy-start(s32[3,8192]{1,0:T(4,128)} %cell.3) | copy-start | bytes 294916
  2.2 0.9 %copy-start = (f32[16,16,256]{2,1,0:T(8,128)S(1)}, f32[16,16,256]{2,1,0:T(8,128)}, u32[]{:S(2)}) copy-start(f32[16,16,256]{2,1,0:T(8,128)} %energy.3) | copy-start | bytes 786436
  2.2 1.0 %copy-start.3 = (f32[3,8192]{1,0:T(4,128)S(1)}, f32[3,8192]{1,0:T(4,128)}, u32[]{:S(2)}) copy-start(f32[3,8192]{1,0:T(4,128)} %vel.1) | copy-start | bytes 294916
  2.2 1.0 %copy-start.5 = (f32[8192]{0:T(1024)S(1)}, f32[8192]{0:T(1024)}, u32[]{:S(2)}) copy-start(f32[8192]{0:T(1024)} %param.11) | copy-start | bytes 98308
  2.2 1.0 %copy-start.6 = (f32[8192]{0:T(1024)S(1)}, f32[8192]{0:T(1024)}, u32[]{:S(2)}) copy-start(f32[8192]{0:T(1024)} %param.13) | copy-start | bytes 98308
  8.9 10.8 %collective-permute-start = (f32[8,1280]{1,0:T(8,128)S(1)}, f32[8,1280]{1,0:T(8,128)S(1)}, u32[]{:S(2)}, u32[]{:S(2)}) collective-permute-start(f32[8,1280]{1,0:T(8,128)S(1)} %get-tuple-element.33), channel_id=1, source_target_pairs={{0,1},{1,0},{2,3},{3,2},{4,5},{5,4},{6,7},{7,6},{8,9},{9,8},{10,11... | collective-permute-start | bytes 122888 | tf_op jit(solution)/shard_map/ppermute | solution.py:419
  11.0 8.7 %collective-permute-start.1 = (f32[8,1280]{1,0:T(8,128)S(1)}, f32[8,1280]{1,0:T(8,128)S(1)}, u32[]{:S(2)}, u32[]{:S(2)}) collective-permute-start(f32[8,1280]{1,0:T(8,128)S(1)} %get-tuple-element.34), channel_id=1, source_target_pairs={{1,2},{2,1},{3,4},{4,3},{5,6},{6,5},{7,8},{8,7},{9,10},{10,9},{11,... | collective-permute-start | bytes 122888 | tf_op jit(solution)/shard_map/ppermute | solution.py:418
  20.1 9.4 %collective-permute-start.2 = (f32[8,1280]{1,0:T(8,128)S(1)}, f32[8,1280]{1,0:T(8,128)S(1)}, u32[]{:S(2)}, u32[]{:S(2)}) collective-permute-start(f32[8,1280]{1,0:T(8,128)S(1)} %get-tuple-element.40), channel_id=1, source_target_pairs={{0,32},{32,0},{64,96},{96,64},{128,160},{160,128},{192,224},{224,1... | collective-permute-start | bytes 122888 | tf_op jit(solution)/shard_map/ppermute | solution.py:419
  21.3 8.1 %collective-permute-start.3 = (f32[8,1280]{1,0:T(8,128)S(1)}, f32[8,1280]{1,0:T(8,128)S(1)}, u32[]{:S(2)}, u32[]{:S(2)}) collective-permute-start(f32[8,1280]{1,0:T(8,128)S(1)} %get-tuple-element.41), channel_id=1, source_target_pairs={{32,64},{64,32},{96,128},{128,96},{160,192},{192,160},{33,65},{65,... | collective-permute-start | bytes 122888 | tf_op jit(solution)/shard_map/ppermute | solution.py:418
  24.6 4.9 %copy-start.1 = (f32[3,16,16,256]{3,2,1,0:T(8,128)S(1)}, f32[3,16,16,256]{3,2,1,0:T(8,128)}, u32[]{:S(2)}) copy-start(f32[3,16,16,256]{3,2,1,0:T(8,128)} %momentum.1) | copy-start | bytes 2359300
  24.6 4.9 %copy-start.2 = (f32[16,16,256]{2,1,0:T(8,128)S(1)}, f32[16,16,256]{2,1,0:T(8,128)}, u32[]{:S(2)}) copy-start(f32[16,16,256]{2,1,0:T(8,128)} %density.1) | copy-start | bytes 786436

commit v8 on v7

--- a/solution.py
+++ b/solution.py
@@ -17,6 +17,7 @@
 BF16 = jnp.bfloat16
 I32 = jnp.int32
 LANES = 128
+KINDS = 6
 VMEM = pltpu.VMEM
 TRANSPOSED = (((1,), (1,)), ((), ()))
 
@@ -29,7 +30,7 @@
     return 1.0 / (1.0 + jnp.exp(-2.0 * (temp - 2.0)))
 
 
-def rank_kernel(cells_x, cells_y, count, cell, place, stays, words, masks, cx, cy):
+def rank_kernel(cells_x, cells_y, count, cell, place, stays, words, masks, numbers, cx, cy):
     chunks = place.shape[0]
     anchor_x = lax.axis_index("gx") * cells_x
     anchor_y = lax.axis_index("gy") * cells_y
@@ -49,14 +50,15 @@
             local_x >= cells_x, 1, jnp.where(local_y < 0, 2, jnp.where(local_y >= cells_y, 3, 4))
         ),
     )
-    heading = jnp.where(live, heading, 5)
-    hits = [jnp.where(heading == h, 1.0, 0.0) for h in range(4)]
+    heading = jnp.where((heading == 4) & (local_x >= cells_x // 2), 5, heading)
+    heading = jnp.where(live, heading, KINDS)
+    hits = [jnp.where(heading == h, 1.0, 0.0) for h in range(KINDS)]
     lane_r = iota((LANES, 2 * LANES), 0)
     lane_c = iota((LANES, 2 * LANES), 1)
     scan = jnp.where((lane_r < lane_c) | (lane_c >= LANES), 1.0, 0.0).astype(BF16)
     both = jnp.dot(jnp.concatenate(hits, axis=0).astype(BF16), scan, preferred_element_type=F32)
-    inner = [both[h * chunks : (h + 1) * chunks, :LANES] for h in range(4)]
-    total = [both[h * chunks : (h + 1) * chunks, LANES:] for h in range(4)]
+    inner = [both[h * chunks : (h + 1) * chunks, :LANES] for h in range(KINDS)]
+    total = [both[h * chunks : (h + 1) * chunks, LANES:] for h in range(KINDS)]
     below = jnp.where(iota((chunks, chunks), 1) < iota((chunks, chunks), 0), 1.0, 0.0).astype(BF16)
     base = jnp.dot(
         below, jnp.concatenate(total, axis=1).astype(BF16), preferred_element_type=F32
@@ -64,7 +66,8 @@
     offset = jnp.zeros(shape, F32)
     spot = jnp.full(shape, -1.0, F32)
     word = jnp.zeros(shape, I32)
-    for h in range(4):
+    number = jnp.zeros((1, LANES), I32)
+    for h in range(KINDS):
         spot = jnp.where(heading == h, inner[h] + offset, spot)
         start = base[:, h * LANES : (h + 1) * LANES]
         within = start & (LANES - 1)
@@ -72,19 +75,21 @@
         turn = (start - offset.astype(I32)) & (LANES - 1)
         word = jnp.where(lane == h, (start >> 7) * LANES + turn, word)
         last = start + total[h].astype(I32)
-        word = jnp.where(lane == 4 + h, last >> 7, word)
+        word = jnp.where(lane == KINDS + h, last >> 7, word)
+        number = jnp.where(lane[0:1] == h, last[chunks - 1 :], number)
         masks[h, 0] = jnp.where((lane >= within) & (lane < end), 1.0, 0.0)
         masks[h, 1] = jnp.where(lane < end - LANES, 1.0, 0.0)
         masks[h, 2] = jnp.where(end >= LANES, 1.0, 0.0)
         offset = offset + total[h]
     words[...] = word
+    numbers[...] = number
     place[...] = spot
-    stays[...] = jnp.where(heading == 4, 1.0, 0.0)
+    stays[...] = jnp.where((heading == 4) | (heading == 5), 1.0, 0.0)
 
 
 def prep_kernel(
     cells_x, cells_y, step, mass, temp, vel, cell, energy, pos, stays, words, masks,
-    even, odd, stay, own, leaving, partial,
+    even, odd, stay, own, leaving, partial, low, high,
     pay, compact, table, tiles, acc, sem,
 ):
     load = pltpu.make_async_copy(words, table, sem)
@@ -109,17 +114,19 @@
             slots = pos[pl.ds(b, 1), :]
             onehot = jnp.where(slots == iota((LANES, LANES), 0).astype(F32), 1.0, 0.0).astype(BF16)
             rows = pay[:, pl.ds(pl.multiple_of(b * LANES, LANES), LANES)]
-            high = rows.astype(BF16).astype(F32)
-            rest = rows - high
+            first = rows.astype(BF16).astype(F32)
+            rest = rows - first
             middle = rest.astype(BF16).astype(F32)
-            low = rest - middle
-            parts = jnp.concatenate([high, middle, low, jnp.zeros_like(low)], axis=0).astype(BF16)
+            last = rest - middle
+            parts = jnp.concatenate([first, middle, last, jnp.zeros_like(last)], axis=0).astype(BF16)
             got = lax.dot_general(parts, onehot, TRANSPOSED, preferred_element_type=F32)
             compact[b] = got[0:8] + got[8:16] + got[16:24]
         return carry
 
     lax.fori_loop(0, chunks // group, pack, 0)
-    tiles[...] = jnp.zeros(tiles.shape, F32)
+    for ref in (tiles, low, high):
+        ref[...] = jnp.zeros(ref.shape, F32)
+    lists = [tiles.at[h] for h in range(4)] + [low, high]
     load.wait()
     unroll = 8
 
@@ -128,20 +135,20 @@
         for u in range(unroll):
             b = g * unroll + u
             rows = compact[b]
-            for h in range(4):
+            for h in range(KINDS):
                 word = table[b, h]
                 turned = pltpu.roll(rows, word & (LANES - 1), 1)
                 merged = jnp.where(masks[h, 0, pl.ds(b, 1), :] > 0.0, turned, carry[h])
-                tiles[h, word >> 7] = merged
+                lists[h][word >> 7] = merged
                 rest = jnp.where(masks[h, 2, pl.ds(b, 1), :] > 0.0, 0.0, merged)
                 carry[h] = jnp.where(masks[h, 1, pl.ds(b, 1), :] > 0.0, turned, rest)
         return tuple(carry)
 
     carry = lax.fori_loop(
-        0, chunks // unroll, place_all, tuple(jnp.zeros((8, LANES), F32) for _ in range(4))
-    )
-    for h in range(4):
-        tiles[h, table[chunks - 1, 4 + h]] = carry[h]
+        0, chunks // unroll, place_all, tuple(jnp.zeros((8, LANES), F32) for _ in range(KINDS))
+    )
+    for h in range(KINDS):
+        lists[h][table[chunks - 1, KINDS + h]] = carry[h]
     width = own.shape[2]
     buckets = [
         jnp.concatenate([tiles[h, t] for t in range(width // LANES)], axis=1) for h in range(4)
@@ -255,25 +262,26 @@
     return got[:number] + got[number:]
 
 
-def deposit_kernel(cells_x, cells_y, step, steps, *refs):
-    columns = cells_x * cells_y
-    if steps[0] == 0:
+def deposit_kernel(cells_x, cells_y, half, numbers, table, *refs):
+    step = 4 * LANES
+    if half == 0:
         stay, dep, state, where_to = refs
         total = stay.shape[1]
         state[:, :total] = stay[0:5, :]
         where_to[:, :total] = stay[5:8, :].astype(I32)
-        dep[...] = jnp.zeros(dep.shape, F32)
     else:
-        stay, before, _, dep = refs
-        dep[...] = before[...]
+        _, dep = refs
+    dep[...] = jnp.zeros(dep.shape, F32)
+    columns = cells_x // 2 * cells_y
     anchor_x, anchor_y = anchors(cells_x, cells_y)
+    anchor_x = anchor_x + half * (cells_x // 2)
 
     def one(k, carry):
-        rows = stay[:, pl.ds(pl.multiple_of(k * step, step), step)]
+        rows = jnp.concatenate([table[4 * k + t] for t in range(4)], axis=1)
         column = (rows[5:6] - anchor_x) * cells_y + (rows[6:7] - anchor_y)
         sources = source_rows(rows)
         onehot = depth_onehot(rows, dep.shape[1])
-        left = [spread(column, half, columns) for half in (sources[:5], sources[5:])]
+        left = [spread(column, part, columns) for part in (sources[:5], sources[5:])]
         dep[...] += lax.dot_general(
             jnp.concatenate(left, axis=1),
             jnp.concatenate([onehot, onehot], axis=1),
@@ -282,7 +290,7 @@
         )
         return carry
 
-    lax.fori_loop(*steps, one, 0)
+    lax.fori_loop(0, (numbers[0, 4 + half] + step - 1) // step, one, 0)
 
 
 def arrivals(rows, along, number, depth):
@@ -317,10 +325,9 @@
 
 
 def update_kernel(
-    cells_x, cells_y, y_even, y_odd, x_even, x_odd, density, momentum, energy, dep,
+    cells_x, cells_y, y_even, y_odd, x_even, x_odd, density, momentum, energy, dep_low, dep_high,
     planes_y, halo_y, leaving, state_in, where_in,
-    rho_there, impulse_there, energy_there, fastest, state, where_to,
-    pressure, planes_x, rho_out, impulse, energy_out, sems,
+    rho_out, impulse, energy_out, fastest, state, where_to, pressure, planes_x,
 ):
     depth = energy.shape[2]
     _, anchor_y = anchors(cells_x, cells_y)
@@ -347,6 +354,8 @@
         where_to[:, lanes] = rows[5:8].astype(I32)
 
     def with_planes(f, x, value):
+        half = cells_x // 2
+        value = value + (dep_low if x < half else dep_high)[f, x % half]
         if x == 0:
             value = value + planes_x[0, f]
         if x == cells_x - 1:
@@ -355,12 +364,9 @@
         return value + jnp.where(row == cells_y - 1, planes_y[1, f, x : x + 1, :], 0.0)
 
     for x in range(cells_x):
-        value = with_planes(4, x, energy[x] + dep[4, x])
+        value = with_planes(4, x, energy[x])
         energy_out[x] = value
         pressure[x + 1] = scale * value
-    leaves = [pltpu.make_async_copy(energy_out, energy_there, sems.at[0])]
-    leaves[0].start()
-    group = 4
     top = jnp.zeros(shape, F32)
     for x in range(cells_x):
         here = pressure[x + 1]
@@ -373,26 +379,16 @@
         after = jnp.where(lane == depth - 1, 0.0, pltpu.roll(here, depth - 1, 1))
         before = jnp.where(lane == 0, 0.0, pltpu.roll(here, 1, 1))
         grad_z = 0.5 * (after - before)
-        rho = with_planes(0, x, density[x] + dep[0, x])
+        rho = with_planes(0, x, density[x])
         rho_out[x] = rho
         largest = jnp.zeros(shape, F32)
         for k, grad in enumerate((grad_x, grad_y, grad_z)):
-            value = with_planes(1 + k, x, momentum[k, x] + dep[1 + k, x]) - KICK * grad
+            value = with_planes(1 + k, x, momentum[k, x]) - KICK * grad
             impulse[k, x] = value
             largest = jnp.maximum(largest, jnp.abs(value))
         wave = largest / rho + jnp.sqrt(ADIABATIC_INDEX * here / rho)
         top = jnp.maximum(top, wave)
-        if (x + 1) % group == 0:
-            some = pl.ds(x + 1 - group, group)
-            for here, there in (
-                (rho_out.at[some], rho_there.at[some]),
-                (impulse.at[:, some], impulse_there.at[:, some]),
-            ):
-                leaves.append(pltpu.make_async_copy(here, there, sems.at[len(leaves)]))
-                leaves[-1].start()
     fastest[...] = jnp.broadcast_to(jnp.max(top, axis=(0, 1), keepdims=True), fastest.shape)
-    for leave in leaves:
-        leave.wait()
 
 
 def call(kernel, outs, scratch=(), out_specs=None, in_specs=None, aliases=None, vmem=48, **extra):
@@ -433,14 +429,20 @@
     whole = pl.BlockSpec(memory_space=VMEM)
     parcels = sds((8, capacity + 3 * depth), F32)
     dense = sds((chunks, LANES), F32)
-    place, stays, words, masks = call(
+    place, stays, words, masks, numbers = call(
         functools.partial(rank_kernel, cells_x, cells_y),
-        (dense, dense, sds((chunks, LANES), I32), sds((4, 3, chunks, LANES), F32)),
+        (
+            dense,
+            dense,
+            sds((chunks, LANES), I32),
+            sds((KINDS, 3, chunks, LANES), F32),
+            sds((1, LANES), I32),
+        ),
         scratch=(VMEM((chunks, LANES), I32), VMEM((chunks, LANES), I32)),
         in_specs=[pl.BlockSpec(memory_space=pltpu.SMEM), whole],
         cost_estimate=pl.CostEstimate(flops=10**9, bytes_accessed=10**6, transcendentals=0),
     )(parcel_count, parcel_cell)
-    even, odd, stay, own, leaving, partial = call(
+    even, odd, stay, own, leaving, partial, low, high = call(
         functools.partial(prep_kernel, cells_x, cells_y, step),
         (
             parcels,
@@ -449,6 +451,8 @@
             sds((2, 8, capacity), F32),
             sds((4, cells_x, depth), F32),
             sds((2, cells_y, depth), F32),
+            sds((chunks + 1, 8, LANES), F32),
+            sds((chunks + 1, 8, LANES), F32),
         ),
         scratch=(
             VMEM((8, rows), F32),
@@ -471,26 +475,25 @@
     )
     y_even, y_odd = swap("gy", even, odd)
     slots = rows + 4 * capacity
-    five = sds((5 * columns, depth), F32)
-    steps = rows // step
-    middle = steps * 5 // 8
-    dep, state, where_to = call(
-        functools.partial(deposit_kernel, cells_x, cells_y, step, (0, middle)),
-        (five, sds((5, slots), F32), sds((3, slots), I32)),
-    )(stay)
+    half = sds((5 * columns // 2, depth), F32)
+    smem = pl.BlockSpec(memory_space=pltpu.SMEM)
+    dep_low, state, where_to = call(
+        functools.partial(deposit_kernel, cells_x, cells_y, 0),
+        (half, sds((5, slots), F32), sds((3, slots), I32)),
+        in_specs=[smem, whole, whole],
+    )(numbers, low, stay)
     even, odd, planes_y, halo_y = call(
         functools.partial(relay_kernel, cells_x, cells_y),
         (parcels, parcels, sds((2, 5, cells_x, depth), F32), sds((2, cells_x, depth), F32)),
         in_specs=[whole] * 5 + [pl.BlockSpec(memory_space=pl.ANY)],
-    )(y_even, y_odd, partial, own, leaving, dep)
+    )(y_even, y_odd, partial, own, leaving, dep_low)
     x_even, x_odd = swap("gx", even, odd)
-    (dep,) = call(
-        functools.partial(deposit_kernel, cells_x, cells_y, step, (middle, steps)),
-        (five,),
-        in_specs=[whole, whole, pl.BlockSpec(memory_space=pl.ANY)],
-        aliases={1: 0},
-    )(stay, dep, halo_y)
-    dep = dep.reshape(5, cells_x, cells_y, depth)
+    (dep_high,) = call(
+        functools.partial(deposit_kernel, cells_x, cells_y, 1),
+        (half,),
+        in_specs=[smem, whole, pl.BlockSpec(memory_space=pl.ANY)],
+    )(numbers, high, halo_y)
+    dep_low, dep_high = (d.reshape(5, cells_x // 2, cells_y, depth) for d in (dep_low, dep_high))
     last = rows // (4 * capacity)
     rho, impulse, energy_out, top, state, where_to = call(
         functools.partial(update_kernel, cells_x, cells_y),
@@ -505,22 +508,17 @@
         scratch=(
             VMEM((cells_x + 2, cells_y, depth), F32),
             VMEM((2, 5, cells_y, depth), F32),
-            VMEM(density.shape, F32),
-            VMEM(momentum.shape, F32),
-            VMEM(energy.shape, F32),
-            pltpu.SemaphoreType.DMA((1 + 2 * (cells_x // 4),)),
-        ),
-        in_specs=[whole] * 11 + [pl.BlockSpec(memory_space=pl.ANY)] * 2,
-        out_specs=(pl.BlockSpec(memory_space=pl.ANY),) * 3
-        + (whole,)
+        ),
+        in_specs=[whole] * 12 + [pl.BlockSpec(memory_space=pl.ANY)] * 2,
+        out_specs=(whole,) * 4
         + (
             pl.BlockSpec((5, 4 * capacity), lambda i: (0, last)),
             pl.BlockSpec((3, 4 * capacity), lambda i: (0, last)),
         ),
-        aliases={11: 4, 12: 5},
+        aliases={12: 4, 13: 5},
         grid=(1,),
     )(
-        y_even, y_odd, x_even, x_odd, density, momentum, energy, dep,
+        y_even, y_odd, x_even, x_odd, density, momentum, energy, dep_low, dep_high,
         planes_y, halo_y, leaving, state, where_to,
     )
     fastest = jnp.max(lax.all_to_all(top, ("gx", "gy"), 0, 0, tiled=True), axis=0)[0]

time: 62.3 us -> 58.8 us (0.944)
  Pallas kernels: 21.7 us -> 12.8 us
  blocking collectives: 28.7 us -> 31.1 us
  waiting for transfers between devices: 0.01 us -> 1.71 us
  starting transfers between devices: 7.26 us -> 8.66 us
    pallas_call x2, Pallas kernels: 12.9 us -> 4.15 us  [the longest x1 2.49 us: on_device(): call(functools.partial(deposit_kernel, cells_x, cells_y, 0), (half, sds((...]
    ppermute x2, starting transfers between devices: 3.39 us -> 6.1 us  [swap(): even = lax.ppermute(even, axis, pairs(0))]
    all_to_all x1, blocking collectives: 28.7 us -> 31.1 us  [on_device(): lax.all_to_all(top, ('gx', 'gy'), 0, 0, tiled=True)]
    ppermute x2, waiting for transfers between devices: 0.01 us -> 1.7 us  [swap(): odd = lax.ppermute(odd, axis, pairs(1))]
    ppermute x2, starting transfers between devices: 3.87 us -> 2.56 us  [swap(): odd = lax.ppermute(odd, axis, pairs(1))]
  transfers between devices with their start and end apart: 4 -> 4, of which waited for: 0 -> 1; matrix products, arithmetic and copies ran while one was open for 0% -> 0% of each run, Pallas kernels for 21% -> 7%
where the time goes in v8:
time: 58.8 us; the launch traced here: 58.6 us
  blocking collectives  31.1 us (53%)
  Pallas kernels  12.8 us (22%)
  starting transfers between devices  8.66 us (15%)
  between operations  2.58 us (4%)
  waiting for transfers between devices  1.71 us (3%)
  local copies, waits for them, and re-layouts  1.4 us (2%)
    all_to_all x1, blocking collectives, on_device(): lax.all_to_all(top, ('gx', 'gy'), 0, 0, tiled=True)  31.1 us
    ppermute x2, starting transfers between devices, swap(): even = lax.ppermute(even, axis, pairs(0))  6.1 us
    pallas_call x1, Pallas kernels, on_device(): call(functools.partial(prep_kernel, cells_x, cells_y, step), (parcels, pa...  6.03 us
    ppermute x2, starting transfers between devices, swap(): odd = lax.ppermute(odd, axis, pairs(1))  2.56 us
    pallas_call x1, Pallas kernels, on_device(): call(functools.partial(deposit_kernel, cells_x, cells_y, 0), (half, sds((...  2.49 us
    pallas_call x1, Pallas kernels, on_device(): call(functools.partial(update_kernel, cells_x, cells_y), (sds(density.sha...  1.81 us
    ppermute x2, waiting for transfers between devices, swap(): odd = lax.ppermute(odd, axis, pairs(1))  1.7 us
    pallas_call x1, Pallas kernels, on_device(): call(functools.partial(deposit_kernel, cells_x, cells_y, 1), (half,), in_...  1.66 us
  transfers between devices with their start and end apart: 4, of which 1 were waited for; matrix products, arithmetic and copies ran while one was open for 0% of the time, Pallas kernels for 7%

profile of v8, /device:TPU:1, one launch (start us, length us, event | category | flops | bytes accessed | tf_op | source)
XLA Modules:
  0.0 58.6 jit_solution(14739092574331675007)
XLA Ops:
  1.3 0.0 copy-start.4
  1.3 0.9 %copy-done.4 = s32[3,8192]{1,0:T(4,128)S(1)} copy-done((s32[3,8192]{1,0:T(4,128)S(1)}, s32[3,8192]{1,0:T(4,128)}, u32[]{:S(2)}) %copy-start.4) | copy-done | bytes 98328
  2.2 0.5 shard_map.127
  2.7 0.5 copy-done
  3.1 0.0 copy-done.3
  3.2 0.0 copy-done.5
  3.2 0.0 copy-done.6
  3.2 6.0 %shard_map.128 = (f32[8,1280]{1,0:T(8,128)S(1)}, f32[8,1280]{1,0:T(8,128)S(1)}, f32[8,8192]{1,0:T(8,128)S(1)}, f32[2,8,512]{2,1,0:T(8,128)S(1)}, f32[4,16,256]{2...) custom-call(f32[64,128]{1,0:T(8,128)S(1)} %bitcast.12, ...), custom_call_target="tpu_custom_call" | custom-call | tf_op jit(solution)/shard_map/pallas_call | solution.py:445
  9.2 2.1 %collective-permute-start = (f32[8,1280]{1,0:T(8,128)S(1)}, f32[8,1280]{1,0:T(8,128)S(1)}, u32[]{:S(2)}, u32[]{:S(2)}) collective-permute-start(f32[8,1280]{1,0:T(8,128)S(1)} %get-tuple-element.36), channel_id=1, source_target_pairs={{0,1},{1,0},{2,3},{3,2},{4,5},{5,4},{6,7},{7,6},{8,9},{9,8},{10,11... | collective-permute-start | bytes 122888 | tf_op jit(solution)/shard_map/ppermute | solution.py:415
  11.3 0.7 %collective-permute-start.1 = (f32[8,1280]{1,0:T(8,128)S(1)}, f32[8,1280]{1,0:T(8,128)S(1)}, u32[]{:S(2)}, u32[]{:S(2)}) collective-permute-start(f32[8,1280]{1,0:T(8,128)S(1)} %get-tuple-element.37), channel_id=1, source_target_pairs={{1,2},{2,1},{3,4},{4,3},{5,6},{6,5},{7,8},{8,7},{9,10},{10,9},{11,... | collective-permute-start | bytes 122888 | tf_op jit(solution)/shard_map/ppermute | solution.py:414
  12.0 2.5 %shard_map.129 = (f32[640,256]{1,0:T(8,128)S(1)}, f32[5,10240]{1,0:T(8,128)}, s32[3,10240]{1,0:T(4,128)}) custom-call(s32[1,128]{1,0:T(1,128)S(1)} %get-tuple-element.41.numbers, f32[65,8,128]{2,1,0:T(8,128)S(1)} %get-tuple-element.42.table, f32[8,8192]{1,0:T(8,128)S(1)} %get-tuple-element.43.refs_0_), custom_call_target="tpu_custom_call" | custom-call | tf_op jit(solution)/shard_map/pallas_call | solution.py:480
  14.5 0.0 collective-permute-done.in_even.y_even
  14.5 0.0 collective-permute-done.1.in_odd.y_odd
  14.5 0.4 shard_map.130
  14.9 4.0 %collective-permute-start.2 = (f32[8,1280]{1,0:T(8,128)S(1)}, f32[8,1280]{1,0:T(8,128)S(1)}, u32[]{:S(2)}, u32[]{:S(2)}) collective-permute-start(f32[8,1280]{1,0:T(8,128)S(1)} %get-tuple-element.45), channel_id=1, source_target_pairs={{0,32},{32,0},{64,96},{96,64},{128,160},{160,128},{192,224},{224,1... | collective-permute-start | bytes 122888 | tf_op jit(solution)/shard_map/ppermute | solution.py:415
  18.8 1.9 %collective-permute-start.3 = (f32[8,1280]{1,0:T(8,128)S(1)}, f32[8,1280]{1,0:T(8,128)S(1)}, u32[]{:S(2)}, u32[]{:S(2)}) collective-permute-start(f32[8,1280]{1,0:T(8,128)S(1)} %get-tuple-element.46), channel_id=1, source_target_pairs={{32,64},{64,32},{96,128},{128,96},{160,192},{192,160},{33,65},{65,... | collective-permute-start | bytes 122888 | tf_op jit(solution)/shard_map/ppermute | solution.py:414
  20.8 0.0 copy-start.2
  20.8 1.7 %shard_map.131 = f32[640,256]{1,0:T(8,128)S(1)} custom-call(s32[1,128]{1,0:T(1,128)S(1)} %get-tuple-element.41.numbers, f32[65,8,128]{2,1,0:T(8,128)S(1)} %get-tuple-element.47.table, f32[2,16,256]{2,1,0:T(8,128)S(1)} %get-tuple-element.48.refs_0_.halo_y), custom_call_target="tpu_custom_call" | custom-call | tf_op jit(solution)/shard_map/pallas_call | solution.py:491
  22.4 0.0 collective-permute-done.2.x_even
  22.5 1.7 %collective-permute-done.3.x_odd = f32[8,1280]{1,0:T(8,128)S(1)} collective-permute-done((f32[8,1280]{1,0:T(8,128)S(1)}, f32[8,1280]{1,0:T(8,128)S(1)}, u32[]{:S(2)}, u32[]{:S(2)}) %collective-permute-start.3) | collective-permute-done | bytes 40992 | tf_op jit(solution)/shard_map/ppermute | solution.py:414
  24.2 0.0 copy-done.2
  24.2 1.8 %shard_map.132 = (f32[16,16,256]{2,1,0:T(8,128)}, f32[3,16,16,256]{3,2,1,0:T(8,128)}, f32[16,16,256]{2,1,0:T(8,128)}, f32[256,128]{1,0:T(8,128)S(1)}, f32[5,10240]{1,0:T(8,128)}, /*index=5*/s32[3,10240]{1,0:T(4,128)}) custom-call(f32[8,1280]{1,0:T(8,128)S(1)} %collective-permute-done.in_even.y_even, ...), custom_call_target="tpu_custom_call", output_to_operand_aliasing={{4}: (12, {}), {5}: (13, {})} | custom-call | tf_op jit(solution)/shard_map/pallas_call | solution.py:498
  26.0 31.1 %all_to_all.9 = f32[256,1,128]{2,1,0:T(1,128)S(1)} all-to-all(f32[256,1,128]{2,1,0:T(1,128)S(1)} %bitcast.11), channel_id=1, replica_groups=mesh['gx'=8,'gy'=32] {'gx','gy'}, dimensions={0} | all-to-all | bytes 262144 | tf_op jit(solution)/shard_map/all_to_all | solution.py:524
  57.1 0.3 reduce_max.9
  (6 shorter events, 0.0 us)
Async XLA Ops:
  1.3 0.9 %copy-start.4 = (s32[3,8192]{1,0:T(4,128)S(1)}, s32[3,8192]{1,0:T(4,128)}, u32[]{:S(2)}) copy-start(s32[3,8192]{1,0:T(4,128)} %cell.3) | copy-start | bytes 294916
  2.2 0.9 %copy-start = (f32[16,16,256]{2,1,0:T(8,128)S(1)}, f32[16,16,256]{2,1,0:T(8,128)}, u32[]{:S(2)}) copy-start(f32[16,16,256]{2,1,0:T(8,128)} %energy.3) | copy-start | bytes 786436
  2.2 1.0 %copy-start.3 = (f32[3,8192]{1,0:T(4,128)S(1)}, f32[3,8192]{1,0:T(4,128)}, u32[]{:S(2)}) copy-start(f32[3,8192]{1,0:T(4,128)} %vel.1) | copy-start | bytes 294916
  2.2 1.0 %copy-start.5 = (f32[8192]{0:T(1024)S(1)}, f32[8192]{0:T(1024)}, u32[]{:S(2)}) copy-start(f32[8192]{0:T(1024)} %param.11) | copy-start | bytes 98308
  2.2 1.0 %copy-start.6 = (f32[8192]{0:T(1024)S(1)}, f32[8192]{0:T(1024)}, u32[]{:S(2)}) copy-start(f32[8192]{0:T(1024)} %param.13) | copy-start | bytes 98308
  9.2 5.3 %collective-permute-start = (f32[8,1280]{1,0:T(8,128)S(1)}, f32[8,1280]{1,0:T(8,128)S(1)}, u32[]{:S(2)}, u32[]{:S(2)}) collective-permute-start(f32[8,1280]{1,0:T(8,128)S(1)} %get-tuple-element.36), channel_id=1, source_target_pairs={{0,1},{1,0},{2,3},{3,2},{4,5},{5,4},{6,7},{7,6},{8,9},{9,8},{10,11... | collective-permute-start | bytes 122888 | tf_op jit(solution)/shard_map/ppermute | solution.py:415
  11.3 3.2 %collective-permute-start.1 = (f32[8,1280]{1,0:T(8,128)S(1)}, f32[8,1280]{1,0:T(8,128)S(1)}, u32[]{:S(2)}, u32[]{:S(2)}) collective-permute-start(f32[8,1280]{1,0:T(8,128)S(1)} %get-tuple-element.37), channel_id=1, source_target_pairs={{1,2},{2,1},{3,4},{4,3},{5,6},{6,5},{7,8},{8,7},{9,10},{10,9},{11,... | collective-permute-start | bytes 122888 | tf_op jit(solution)/shard_map/ppermute | solution.py:414
  14.5 9.7 %copy-start.1 = (f32[3,16,16,256]{3,2,1,0:T(8,128)S(1)}, f32[3,16,16,256]{3,2,1,0:T(8,128)}, u32[]{:S(2)}) copy-start(f32[3,16,16,256]{3,2,1,0:T(8,128)} %momentum.1) | copy-start | bytes 2359300
  14.9 7.6 %collective-permute-start.2 = (f32[8,1280]{1,0:T(8,128)S(1)}, f32[8,1280]{1,0:T(8,128)S(1)}, u32[]{:S(2)}, u32[]{:S(2)}) collective-permute-start(f32[8,1280]{1,0:T(8,128)S(1)} %get-tuple-element.45), channel_id=1, source_target_pairs={{0,32},{32,0},{64,96},{96,64},{128,160},{160,128},{192,224},{224,1... | collective-permute-start | bytes 122888 | tf_op jit(solution)/shard_map/ppermute | solution.py:415
  18.8 5.3 %collective-permute-start.3 = (f32[8,1280]{1,0:T(8,128)S(1)}, f32[8,1280]{1,0:T(8,128)S(1)}, u32[]{:S(2)}, u32[]{:S(2)}) collective-permute-start(f32[8,1280]{1,0:T(8,128)S(1)} %get-tuple-element.46), channel_id=1, source_target_pairs={{32,64},{64,32},{96,128},{128,96},{160,192},{192,160},{33,65},{65,... | collective-permute-start | bytes 122888 | tf_op jit(solution)/shard_map/ppermute | solution.py:414
  20.8 3.4 %copy-start.2 = (f32[16,16,256]{2,1,0:T(8,128)S(1)}, f32[16,16,256]{2,1,0:T(8,128)}, u32[]{:S(2)}) copy-start(f32[16,16,256]{2,1,0:T(8,128)} %density.1) | copy-start | bytes 786436

commit v9 on v8

--- a/solution.py
+++ b/solution.py
@@ -106,7 +106,7 @@
     for b in range(chunks):
         lanes = slice(b * LANES, (b + 1) * LANES)
         stay[:, lanes] = jnp.where(stays[b : b + 1, :] > 0.0, pay[:, lanes], 0.0)
-    group = 16
+    group = min(32, chunks)
 
     def pack(g, carry):
         for u in range(group):
@@ -159,7 +159,7 @@
         leaving[h] = one_field(buckets[h], along, number, acc.shape[1], 4)
     for h in range(2):
         own[h] = buckets[h]
-    outer_energy(cells_x, cells_y, anchor_xf, anchor_yf, step, stay, acc)
+    outer_energy(cells_x, cells_y, anchor_xf, anchor_yf, 2 * step, stay, acc)
     planes = [acc[q * 2 * cells_y : (q * 2 + 1) * cells_y] + acc[(q * 2 + 1) * cells_y : (q * 2 + 2) * cells_y] for q in range(4)]
     partial[0] = energy[0] + planes[0]
     partial[1] = energy[cells_x - 1] + planes[1]
@@ -263,7 +263,7 @@
 
 
 def deposit_kernel(cells_x, cells_y, half, numbers, table, *refs):
-    step = 4 * LANES
+    step = 8 * LANES
     if half == 0:
         stay, dep, state, where_to = refs
         total = stay.shape[1]
@@ -277,17 +277,15 @@
     anchor_x = anchor_x + half * (cells_x // 2)
 
     def one(k, carry):
-        rows = jnp.concatenate([table[4 * k + t] for t in range(4)], axis=1)
+        rows = jnp.concatenate([table[8 * k + t] for t in range(8)], axis=1)
         column = (rows[5:6] - anchor_x) * cells_y + (rows[6:7] - anchor_y)
-        sources = source_rows(rows)
-        onehot = depth_onehot(rows, dep.shape[1])
-        left = [spread(column, part, columns) for part in (sources[:5], sources[5:])]
-        dep[...] += lax.dot_general(
-            jnp.concatenate(left, axis=1),
-            jnp.concatenate([onehot, onehot], axis=1),
+        got = lax.dot_general(
+            spread(column, source_rows(rows), columns),
+            depth_onehot(rows, dep.shape[1]),
             TRANSPOSED,
             preferred_element_type=F32,
         )
+        dep[...] += got[: 5 * columns] + got[5 * columns :]
         return carry
 
     lax.fori_loop(0, (numbers[0, 4 + half] + step - 1) // step, one, 0)

time: 58.8 us -> 58 us (0.986)
  Pallas kernels: 12.8 us -> 11.6 us
    pallas_call x1, Pallas kernels: 6.03 us -> 5.23 us  [on_device(): call(functools.partial(prep_kernel, cells_x, cells_y, step), (parcels, pa...]
  transfers between devices with their start and end apart: 4 -> 4, of which waited for: 1 -> 1; matrix products, arithmetic and copies ran while one was open for 0% -> 0% of each run, Pallas kernels for 7% -> 6%
where the time goes in v9:
time: 58 us; the launch traced here: 57.8 us
  blocking collectives  31.4 us (54%)
  Pallas kernels  11.6 us (20%)
  starting transfers between devices  8.61 us (15%)
  between operations  2.58 us (4%)
  waiting for transfers between devices  1.91 us (3%)
  local copies, waits for them, and re-layouts  1.4 us (2%)
    all_to_all x1, blocking collectives, on_device(): lax.all_to_all(top, ('gx', 'gy'), 0, 0, tiled=True)  31.4 us
    ppermute x2, starting transfers between devices, swap(): even = lax.ppermute(even, axis, pairs(0))  6.05 us
    pallas_call x1, Pallas kernels, on_device(): call(functools.partial(prep_kernel, cells_x, cells_y, step), (parcels, pa...  5.23 us
    ppermute x2, starting transfers between devices, swap(): odd = lax.ppermute(odd, axis, pairs(1))  2.56 us
    pallas_call x1, Pallas kernels, on_device(): call(functools.partial(deposit_kernel, cells_x, cells_y, 0), (half, sds((...  2.29 us
    ppermute x2, waiting for transfers between devices, swap(): odd = lax.ppermute(odd, axis, pairs(1))  1.9 us
    pallas_call x1, Pallas kernels, on_device(): call(functools.partial(update_kernel, cells_x, cells_y), (sds(density.sha...  1.82 us
    pallas_call x1, Pallas kernels, on_device(): call(functools.partial(deposit_kernel, cells_x, cells_y, 1), (half,), in_...  1.46 us
  transfers between devices with their start and end apart: 4, of which 1 were waited for; matrix products, arithmetic and copies ran while one was open for 0% of the time, Pallas kernels for 6%

profile of v9, /device:TPU:1, one launch (start us, length us, event | category | flops | bytes accessed | tf_op | source)
XLA Modules:
  0.0 57.8 jit_solution(1857747908580060181)
XLA Ops:
  1.3 0.0 copy-start.4
  1.3 0.9 %copy-done.4 = s32[3,8192]{1,0:T(4,128)S(1)} copy-done((s32[3,8192]{1,0:T(4,128)S(1)}, s32[3,8192]{1,0:T(4,128)}, u32[]{:S(2)}) %copy-start.4) | copy-done | bytes 98328
  2.2 0.5 shard_map.127
  2.7 0.5 copy-done
  3.1 0.0 copy-done.3
  3.2 0.0 copy-done.5
  3.2 0.0 copy-done.6
  3.2 5.2 %shard_map.128 = (f32[8,1280]{1,0:T(8,128)S(1)}, f32[8,1280]{1,0:T(8,128)S(1)}, f32[8,8192]{1,0:T(8,128)S(1)}, f32[2,8,512]{2,1,0:T(8,128)S(1)}, f32[4,16,256]{2...) custom-call(f32[64,128]{1,0:T(8,128)S(1)} %bitcast.12, ...), custom_call_target="tpu_custom_call" | custom-call | tf_op jit(solution)/shard_map/pallas_call | solution.py:443
  8.4 2.1 %collective-permute-start = (f32[8,1280]{1,0:T(8,128)S(1)}, f32[8,1280]{1,0:T(8,128)S(1)}, u32[]{:S(2)}, u32[]{:S(2)}) collective-permute-start(f32[8,1280]{1,0:T(8,128)S(1)} %get-tuple-element.36), channel_id=1, source_target_pairs={{0,1},{1,0},{2,3},{3,2},{4,5},{5,4},{6,7},{7,6},{8,9},{9,8},{10,11... | collective-permute-start | bytes 122888 | tf_op jit(solution)/shard_map/ppermute | solution.py:413
  10.5 0.7 %collective-permute-start.1 = (f32[8,1280]{1,0:T(8,128)S(1)}, f32[8,1280]{1,0:T(8,128)S(1)}, u32[]{:S(2)}, u32[]{:S(2)}) collective-permute-start(f32[8,1280]{1,0:T(8,128)S(1)} %get-tuple-element.37), channel_id=1, source_target_pairs={{1,2},{2,1},{3,4},{4,3},{5,6},{6,5},{7,8},{8,7},{9,10},{10,9},{11,... | collective-permute-start | bytes 122888 | tf_op jit(solution)/shard_map/ppermute | solution.py:412
  11.2 2.3 %shard_map.129 = (f32[640,256]{1,0:T(8,128)S(1)}, f32[5,10240]{1,0:T(8,128)}, s32[3,10240]{1,0:T(4,128)}) custom-call(s32[1,128]{1,0:T(1,128)S(1)} %get-tuple-element.41.numbers, f32[65,8,128]{2,1,0:T(8,128)S(1)} %get-tuple-element.42.table, f32[8,8192]{1,0:T(8,128)S(1)} %get-tuple-element.43.refs_0_), custom_call_target="tpu_custom_call" | custom-call | tf_op jit(solution)/shard_map/pallas_call | solution.py:478
  13.5 0.0 collective-permute-done.in_even.y_even
  13.5 0.0 collective-permute-done.1.in_odd.y_odd
  13.5 0.4 shard_map.130
  13.9 3.9 %collective-permute-start.2 = (f32[8,1280]{1,0:T(8,128)S(1)}, f32[8,1280]{1,0:T(8,128)S(1)}, u32[]{:S(2)}, u32[]{:S(2)}) collective-permute-start(f32[8,1280]{1,0:T(8,128)S(1)} %get-tuple-element.45), channel_id=1, source_target_pairs={{0,32},{32,0},{64,96},{96,64},{128,160},{160,128},{192,224},{224,1... | collective-permute-start | bytes 122888 | tf_op jit(solution)/shard_map/ppermute | solution.py:413
  17.8 1.9 %collective-permute-start.3 = (f32[8,1280]{1,0:T(8,128)S(1)}, f32[8,1280]{1,0:T(8,128)S(1)}, u32[]{:S(2)}, u32[]{:S(2)}) collective-permute-start(f32[8,1280]{1,0:T(8,128)S(1)} %get-tuple-element.46), channel_id=1, source_target_pairs={{32,64},{64,32},{96,128},{128,96},{160,192},{192,160},{33,65},{65,... | collective-permute-start | bytes 122888 | tf_op jit(solution)/shard_map/ppermute | solution.py:412
  19.7 0.0 copy-start.2
  19.7 1.5 %shard_map.131 = f32[640,256]{1,0:T(8,128)S(1)} custom-call(s32[1,128]{1,0:T(1,128)S(1)} %get-tuple-element.41.numbers, f32[65,8,128]{2,1,0:T(8,128)S(1)} %get-tuple-element.47.table, f32[2,16,256]{2,1,0:T(8,128)S(1)} %get-tuple-element.48.refs_0_.halo_y), custom_call_target="tpu_custom_call" | custom-call | tf_op jit(solution)/shard_map/pallas_call | solution.py:489
  21.2 0.0 collective-permute-done.2.x_even
  21.2 1.9 %collective-permute-done.3.x_odd = f32[8,1280]{1,0:T(8,128)S(1)} collective-permute-done((f32[8,1280]{1,0:T(8,128)S(1)}, f32[8,1280]{1,0:T(8,128)S(1)}, u32[]{:S(2)}, u32[]{:S(2)}) %collective-permute-start.3) | collective-permute-done | bytes 40992 | tf_op jit(solution)/shard_map/ppermute | solution.py:412
  23.1 0.0 copy-done.2
  23.1 1.8 %shard_map.132 = (f32[16,16,256]{2,1,0:T(8,128)}, f32[3,16,16,256]{3,2,1,0:T(8,128)}, f32[16,16,256]{2,1,0:T(8,128)}, f32[256,128]{1,0:T(8,128)S(1)}, f32[5,10240]{1,0:T(8,128)}, /*index=5*/s32[3,10240]{1,0:T(4,128)}) custom-call(f32[8,1280]{1,0:T(8,128)S(1)} %collective-permute-done.in_even.y_even, ...), custom_call_target="tpu_custom_call", output_to_operand_aliasing={{4}: (12, {}), {5}: (13, {})} | custom-call | tf_op jit(solution)/shard_map/pallas_call | solution.py:496
  24.9 31.4 %all_to_all.9 = f32[256,1,128]{2,1,0:T(1,128)S(1)} all-to-all(f32[256,1,128]{2,1,0:T(1,128)S(1)} %bitcast.11), channel_id=1, replica_groups=mesh['gx'=8,'gy'=32] {'gx','gy'}, dimensions={0} | all-to-all | bytes 262144 | tf_op jit(solution)/shard_map/all_to_all | solution.py:522
  56.3 0.3 reduce_max.9
  (6 shorter events, 0.0 us)
Async XLA Ops:
  1.3 0.9 %copy-start.4 = (s32[3,8192]{1,0:T(4,128)S(1)}, s32[3,8192]{1,0:T(4,128)}, u32[]{:S(2)}) copy-start(s32[3,8192]{1,0:T(4,128)} %cell.3) | copy-start | bytes 294916
  2.2 0.9 %copy-start = (f32[16,16,256]{2,1,0:T(8,128)S(1)}, f32[16,16,256]{2,1,0:T(8,128)}, u32[]{:S(2)}) copy-start(f32[16,16,256]{2,1,0:T(8,128)} %energy.3) | copy-start | bytes 786436
  2.2 1.0 %copy-start.3 = (f32[3,8192]{1,0:T(4,128)S(1)}, f32[3,8192]{1,0:T(4,128)}, u32[]{:S(2)}) copy-start(f32[3,8192]{1,0:T(4,128)} %vel.1) | copy-start | bytes 294916
  2.2 1.0 %copy-start.5 = (f32[8192]{0:T(1024)S(1)}, f32[8192]{0:T(1024)}, u32[]{:S(2)}) copy-start(f32[8192]{0:T(1024)} %param.11) | copy-start | bytes 98308
  2.2 1.0 %copy-start.6 = (f32[8192]{0:T(1024)S(1)}, f32[8192]{0:T(1024)}, u32[]{:S(2)}) copy-start(f32[8192]{0:T(1024)} %param.13) | copy-start | bytes 98308
  8.4 5.1 %collective-permute-start = (f32[8,1280]{1,0:T(8,128)S(1)}, f32[8,1280]{1,0:T(8,128)S(1)}, u32[]{:S(2)}, u32[]{:S(2)}) collective-permute-start(f32[8,1280]{1,0:T(8,128)S(1)} %get-tuple-element.36), channel_id=1, source_target_pairs={{0,1},{1,0},{2,3},{3,2},{4,5},{5,4},{6,7},{7,6},{8,9},{9,8},{10,11... | collective-permute-start | bytes 122888 | tf_op jit(solution)/shard_map/ppermute | solution.py:413
  10.5 3.0 %collective-permute-start.1 = (f32[8,1280]{1,0:T(8,128)S(1)}, f32[8,1280]{1,0:T(8,128)S(1)}, u32[]{:S(2)}, u32[]{:S(2)}) collective-permute-start(f32[8,1280]{1,0:T(8,128)S(1)} %get-tuple-element.37), channel_id=1, source_target_pairs={{1,2},{2,1},{3,4},{4,3},{5,6},{6,5},{7,8},{8,7},{9,10},{10,9},{11,... | collective-permute-start | bytes 122888 | tf_op jit(solution)/shard_map/ppermute | solution.py:412
  13.5 9.6 %copy-start.1 = (f32[3,16,16,256]{3,2,1,0:T(8,128)S(1)}, f32[3,16,16,256]{3,2,1,0:T(8,128)}, u32[]{:S(2)}) copy-start(f32[3,16,16,256]{3,2,1,0:T(8,128)} %momentum.1) | copy-start | bytes 2359300
  13.9 7.3 %collective-permute-start.2 = (f32[8,1280]{1,0:T(8,128)S(1)}, f32[8,1280]{1,0:T(8,128)S(1)}, u32[]{:S(2)}, u32[]{:S(2)}) collective-permute-start(f32[8,1280]{1,0:T(8,128)S(1)} %get-tuple-element.45), channel_id=1, source_target_pairs={{0,32},{32,0},{64,96},{96,64},{128,160},{160,128},{192,224},{224,1... | collective-permute-start | bytes 122888 | tf_op jit(solution)/shard_map/ppermute | solution.py:413
  17.8 5.3 %collective-permute-start.3 = (f32[8,1280]{1,0:T(8,128)S(1)}, f32[8,1280]{1,0:T(8,128)S(1)}, u32[]{:S(2)}, u32[]{:S(2)}) collective-permute-start(f32[8,1280]{1,0:T(8,128)S(1)} %get-tuple-element.46), channel_id=1, source_target_pairs={{32,64},{64,32},{96,128},{128,96},{160,192},{192,160},{33,65},{65,... | collective-permute-start | bytes 122888 | tf_op jit(solution)/shard_map/ppermute | solution.py:412
  19.7 3.4 %copy-start.2 = (f32[16,16,256]{2,1,0:T(8,128)S(1)}, f32[16,16,256]{2,1,0:T(8,128)}, u32[]{:S(2)}) copy-start(f32[16,16,256]{2,1,0:T(8,128)} %density.1) | copy-start | bytes 786436
